TPU v7x, 256 devices: a whole 4x4x8 slice. The times are simulated.
256 devices in a mesh: row: 16 (over z, core), col: 16 (over x, y).
Axes of the slice: x: 4, y: 4, z: 8, core: 2. Of those that a mesh axis runs over, the one named last changes fastest.
Arguments:
- images: bfloat16 [4096, 12, 12, 272], P(('row', 'col')), may hold values from -20 to 20
- expand_weight: bfloat16 [2, 272, 1632], replicated, may hold values from -0.375 to 0.375
- depth_kernel: float32 [2, 25, 1632], replicated, may hold values from -1.25 to 1.25
- squeeze_weight: float32 [2, 1632, 68], replicated, may hold values from -0.15625 to 0.15625
- squeeze_bias: float32 [2, 68], replicated, may hold values from -3 to 3
- excite_weight: float32 [2, 68, 1632], replicated, may hold values from -0.75 to 0.75
- excite_bias: float32 [2, 1632], replicated, may hold values from -4 to 4
- project_weight: bfloat16 [2, 1632, 272], replicated, may hold values from -0.15625 to 0.15625
- mid_gain: float32 [2, 2, 1632], replicated, may hold values from 0.5 to 1.5
- mid_bias: float32 [2, 2, 1632], replicated, may hold values from -3 to 3
- out_gain: float32 [2, 272], replicated, may hold values from 0.5 to 1.5
- out_bias: float32 [2, 272], replicated, may hold values from -3 to 3
- mid_mean: float32 [2, 2, 1632], replicated, may hold values from -4 to 4
- mid_var: float32 [2, 2, 1632], replicated, may hold values from 0.05 to 20
- out_mean: float32 [2, 272], replicated, may hold values from -4 to 4
- out_var: float32 [2, 272], replicated, may hold values from 0.05 to 20
Outputs:
- block_output: bfloat16 [4096, 12, 12, 272], P(('row', 'col'))
- mid_mean_new: float32 [2, 2, 1632], replicated
- mid_var_new: float32 [2, 2, 1632], replicated
- out_mean_new: float32 [2, 272], replicated
- out_var_new: float32 [2, 272], replicated
All inputs are finite; a program needn't handle non-finite values.
Results may differ from a plain program's by a relative error of at most 0.0049.
The roundings to bfloat16 on the way count: a program that leaves them out, or rounds other values in their place, can miss the bound.
Values sent between devices are 32-bit elements; how exact they have to be, the bound alone decides.
No kernel may reach another device: no remote copies, remote signals or barrier semaphores. Data moves between devices by JAX's collectives and lax.ppermute only.
A program may use at most 128 MiB of HBM per device.

v0:
```python
import jax
import jax.numpy as jnp
from jax import lax
from jax.sharding import PartitionSpec as P

KERN = 5
LAYERS = 2


EPSILON = 0.001
RATIO_MAX = 3.0
SHIFT_MAX = 5.0
MOMENTUM = 0.01


def from_everyone(shard, axis):
    copies = jnp.broadcast_to(shard, (lax.axis_size(axis), *shard.shape))
    return lax.all_to_all(copies, axis, split_axis=0, concat_axis=0, tiled=True)


def over_copies(shard, axis):
    everything = from_everyone(shard, axis)
    return jnp.sum(everything, axis=0)


def packed_total(arrays, axis):
    ravelled, at, finished = (jnp.concatenate([a.reshape(-1) for a in arrays]), 0, [])
    subtotal = over_copies(ravelled, axis)
    for a in arrays:
        finished.append(subtotal[at : at + a.size].reshape(a.shape))
        at += a.size
    return tuple(finished)


def coefficients(first_sum, second_sum, row_count, run_mean, run_var, gain, bias):
    offset = first_sum / row_count
    batch_var = second_sum / row_count - offset * offset
    batch_mean = run_mean + offset
    batch_sigma = jnp.sqrt(batch_var + EPSILON)
    run_sigma = jnp.sqrt(run_var + EPSILON)
    scale_ratio = jnp.clip(batch_sigma / run_sigma, 1.0 / RATIO_MAX, RATIO_MAX)
    shift_clip = jnp.clip(offset / run_sigma, -SHIFT_MAX, SHIFT_MAX)
    gain_scale = gain * scale_ratio / batch_sigma
    gain_shift = bias + gain * shift_clip - batch_mean * gain_scale
    new_mean = run_mean + MOMENTUM * offset
    new_var = run_var + MOMENTUM * (batch_var - run_var)
    return (gain_scale, gain_shift, new_mean, new_var)


def renorm(values, run_mean, run_var, gain, bias):
    centered = values - run_mean
    first_sum = jnp.sum(centered, axis=(0, 1, 2))
    second_sum = jnp.sum(centered * centered, axis=(0, 1, 2))
    row_count = float(
        values.shape[0]
        * values.shape[1]
        * values.shape[2]
        * lax.axis_size("row")
        * lax.axis_size("col")
    )
    first_sum, second_sum = packed_total((first_sum, second_sum), "row")
    first_sum, second_sum = packed_total((first_sum, second_sum), "col")
    return coefficients(first_sum, second_sum, row_count, run_mean, run_var, gain, bias)


def project_rows(images, matrix):
    leading = images.shape[:3]
    flat_rows = images.reshape(-1, images.shape[3])
    product = jnp.dot(flat_rows, matrix, preferred_element_type=jnp.float32)
    return product.reshape(leading + (matrix.shape[1],))


def depthwise(active, kernel):
    reach = KERN // 2
    side_len = active.shape[1]
    padded = jnp.pad(active, ((0, 0), (reach, reach), (reach, reach), (0, 0)))
    running_total = jnp.zeros(active.shape, jnp.float32)
    for row_step in range(KERN):
        for col_step in range(KERN):
            window = padded[:, row_step : row_step + side_len, col_step : col_step + side_len, :]
            running_total = running_total + window * kernel[row_step * KERN + col_step]
    return running_total


def excite(lifted, reduce_w, reduce_b, grow_w, grow_b):
    pooled = jnp.mean(lifted, axis=(1, 2))
    squeezed = jax.nn.silu(jnp.dot(pooled, reduce_w, precision=lax.Precision.HIGHEST) + reduce_b)
    se_gate = jax.nn.sigmoid(jnp.dot(squeezed, grow_w, precision=lax.Precision.HIGHEST) + grow_b)
    return (lifted * se_gate[:, None, None, :]).astype(jnp.bfloat16)


def per_device(
    images,
    expand_weight,
    depth_kernel,
    squeeze_weight,
    squeeze_bias,
    excite_weight,
    excite_bias,
    project_weight,
    mid_gain,
    mid_bias,
    out_gain,
    out_bias,
    mid_mean,
    mid_var,
    out_mean,
    out_var,
):
    current = images
    mean_layers, var_layers, out_means, out_vars = ([], [], [], [])
    for layer_index in range(LAYERS):
        expanded = project_rows(current, expand_weight[layer_index])
        first_coef = renorm(
            expanded,
            mid_mean[layer_index, 0],
            mid_var[layer_index, 0],
            mid_gain[layer_index, 0],
            mid_bias[layer_index, 0],
        )
        active = jax.nn.silu(expanded * first_coef[0] + first_coef[1]).astype(jnp.bfloat16)
        spread = depthwise(active, depth_kernel[layer_index])
        second_coef = renorm(
            spread,
            mid_mean[layer_index, 1],
            mid_var[layer_index, 1],
            mid_gain[layer_index, 1],
            mid_bias[layer_index, 1],
        )
        lifted = jax.nn.silu(spread * second_coef[0] + second_coef[1])
        scaled = excite(
            lifted,
            squeeze_weight[layer_index],
            squeeze_bias[layer_index],
            excite_weight[layer_index],
            excite_bias[layer_index],
        )
        projected = project_rows(scaled, project_weight[layer_index])
        third_coef = renorm(
            projected,
            out_mean[layer_index],
            out_var[layer_index],
            out_gain[layer_index],
            out_bias[layer_index],
        )
        current = (current.astype(jnp.float32) + projected * third_coef[0] + third_coef[1]).astype(
            jnp.bfloat16
        )
        mean_layers.append(jnp.stack([first_coef[2], second_coef[2]]))
        var_layers.append(jnp.stack([first_coef[3], second_coef[3]]))
        out_means.append(third_coef[2])
        out_vars.append(third_coef[3])
    return (
        current,
        jnp.stack(mean_layers),
        jnp.stack(var_layers),
        jnp.stack(out_means),
        jnp.stack(out_vars),
    )


def solution(mesh):
    in_specs = (
        P(("row", "col"), None, None, None),
        P(),
        P(),
        P(),
        P(),
        P(),
        P(),
        P(),
        P(),
        P(),
        P(),
        P(),
        P(),
        P(),
        P(),
        P(),
    )
    out_specs = (P(("row", "col"), None, None, None), P(), P(), P(), P())
    return jax.shard_map(
        per_device, mesh=mesh, in_specs=in_specs, out_specs=out_specs, check_vma=False
    )
```

profile of v0, /device:TPU:1, one launch (start us, length us, event | category | flops | bytes accessed | tf_op | source)
XLA Modules:
  0.0 348.9 jit_solution(1646781650467022592)
XLA Ops:
  1.6 11.5 %subtract_reduce_fusion.3 = (f32[1632]{0:T(1024)S(1)}, f32[1632]{0:T(1024)S(1)}, f32[16,12,12,1632]{3,0,2,1:T(8,128)}) fusion(f32[1632]{0:T(1024)S(1)} %get-tuple-element.73, bf16[16,12,12,272]{3,0,2,1:T(8,128)(2,1)} %param.16, bf16[2,272,1632]{2,1,0:T(8,128)(2,1)} %param.17), kind=kOutput, calls=%fused_computation.63 | convolution fusion | flops 2060546816 | bytes 17734784 | tf_op jit(solution)/shard_map/dot_general | solution.py:69
  14.1 10.0 %all-to-all-start = ((f32[16,1,3264]{2,1,0:T(1,128)}), f32[16,1,3264]{2,1,0:T(1,128)S(1)}, u32[]{:S(2)}, u32[]{:S(2)}) async-start(f32[16,1,3264]{2,1,0:T(1,128)} %broadcast_in_dim.24), calls=%async_computation | async-start | bytes 425984 | tf_op jit(solution)/shard_map/all_to_all | solution.py:18
  25.3 9.3 %all-to-all-done = f32[16,1,3264]{2,1,0:T(1,128)S(1)} async-done(((f32[16,1,3264]{2,1,0:T(1,128)}), f32[16,1,3264]{2,1,0:T(1,128)S(1)}, u32[]{:S(2)}, u32[]{:S(2)}) %all-to-all-start) | async-done | bytes 208928 | tf_op jit(solution)/shard_map/all_to_all | solution.py:18
  35.5 6.8 %all-to-all-start.1 = ((f32[16,1,3264]{2,1,0:T(1,128)}), f32[16,1,3264]{2,1,0:T(1,128)S(1)}, u32[]{:S(2)}, u32[]{:S(2)}) async-start(f32[16,1,3264]{2,1,0:T(1,128)} %broadcast_in_dim.25), calls=%async_computation.1 | async-start | bytes 425984 | tf_op jit(solution)/shard_map/all_to_all | solution.py:18
  42.7 7.3 %all-to-all-done.1 = f32[16,1,3264]{2,1,0:T(1,128)S(1)} async-done(((f32[16,1,3264]{2,1,0:T(1,128)}), f32[16,1,3264]{2,1,0:T(1,128)S(1)}, u32[]{:S(2)}, u32[]{:S(2)}) %all-to-all-start.1) | async-done | bytes 208928 | tf_op jit(solution)/shard_map/all_to_all | solution.py:18
  50.2 7.8 %multiply_convert_fusion.3 = bf16[16,12,12,1632]{3,0,2,1:T(8,128)(2,1)S(1)} fusion(f32[16,12,12,1632]{3,0,2,1:T(8,128)} %get-tuple-element.125, f32[1632]{0:T(1024)S(1)} %get-tuple-element.105, f32[1632]{0:T(1024)S(1)} %get-tuple-element.106), kind=kLoop, calls=%fused_computation.58 | loop fusion | flops 26320896 | bytes 22573824 | tf_op jit(solution)/shard_map/convert_element_type | solution.py:121
  58.0 50.2 %subtract_reduce_fusion.2 = (f32[1632]{0:T(1024)S(1)}, f32[1632]{0:T(1024)S(1)}, f32[16,12,12,1632]{3,0,2,1:T(8,128)}) fusion(f32[1632]{0:T(1024)S(1)} %get-tuple-element.72, f32[1632]{0:T(1024)S(1)} %get-tuple-element.40, f32[1632]{0:T(1024)S(1)} %get-tuple-element.41, f32[1632]{0:T(1024)S(1)} %get-tuple-element.42, f32[1632]{0:T(1024)S(1)} %get-tuple-element.43, ...), kind=kLoop, calls=%fused_computation.62 | loop fusion | flops 293286720 | bytes 22743552 | tf_op jit(solution)/shard_map/reduce_sum | solution.py:52
  114.4 10.0 %all-to-all-done.2 = f32[16,1,3264]{2,1,0:T(1,128)S(1)} async-done(((f32[16,1,3264]{2,1,0:T(1,128)}), f32[16,1,3264]{2,1,0:T(1,128)S(1)}, u32[]{:S(2)}, u32[]{:S(2)}) %all-to-all-start.2) | async-done | bytes 208928 | tf_op jit(solution)/shard_map/all_to_all | solution.py:18
  128.9 7.6 %all-to-all-done.3 = f32[16,1,3264]{2,1,0:T(1,128)S(1)} async-done(((f32[16,1,3264]{2,1,0:T(1,128)}), f32[16,1,3264]{2,1,0:T(1,128)S(1)}, u32[]{:S(2)}, u32[]{:S(2)}) %all-to-all-start.3) | async-done | bytes 208928 | tf_op jit(solution)/shard_map/all_to_all | solution.py:18
  136.8 8.0 %fusion.22 = f32[16,1632]{1,0:T(8,128)S(1)} fusion(f32[1632]{0:T(1024)S(1)} %get-tuple-element.102, f32[16,12,12,1632]{3,0,2,1:T(8,128)} %get-tuple-element.104, f32[1632]{0:T(1024)S(1)} %get-tuple-element.103), kind=kLoop, calls=%fused_computation.96 | loop fusion | flops 26294784 | bytes 15158016 | tf_op jit(solution)/shard_map/reduce_sum | solution.py:86
  146.4 7.5 %subtract_reduce_fusion.5 = (f32[272]{0:T(512)S(1)}, f32[272]{0:T(512)S(1)}, f32[16,12,12,272]{3,0,2,1:T(8,128)}) fusion(f32[272]{0:T(512)S(1)} %get-tuple-element.88, bf16[2,1632,272]{1,2,0:T(8,128)(2,1)} %param.23, f32[16,1632]{1,0:T(8,128)S(1)} %fusion.7, f32[1632]{0:T(1024)S(1)} %get-tuple-element.102, f32[16,12,12,1632]{3,0,2,1:T(8,128)S(1)} %copy-done.1, ...), kind=kOutput, calls=%fused_computation.73 | convolution fusion | flops 2078096896 | bytes 18573248 | tf_op jit(solution)/shard_map/dot_general | solution.py:69
  159.2 7.5 %all-to-all-done.4 = f32[16,1,544]{2,1,0:T(1,128)S(1)} async-done(((f32[16,1,544]{2,1,0:T(1,128)}), f32[16,1,544]{2,1,0:T(1,128)S(1)}, u32[]{:S(2)}, u32[]{:S(2)}) %all-to-all-start.4) | async-done | bytes 34848 | tf_op jit(solution)/shard_map/all_to_all | solution.py:18
  170.9 6.4 %all-to-all-done.5 = f32[16,1,544]{2,1,0:T(1,128)S(1)} async-done(((f32[16,1,544]{2,1,0:T(1,128)}), f32[16,1,544]{2,1,0:T(1,128)S(1)}, u32[]{:S(2)}, u32[]{:S(2)}) %all-to-all-start.5) | async-done | bytes 34848 | tf_op jit(solution)/shard_map/all_to_all | solution.py:18
  180.5 8.9 %subtract_reduce_fusion.1 = (f32[1632]{0:T(1024)S(1)}, f32[1632]{0:T(1024)S(1)}, f32[16,12,12,1632]{3,0,2,1:T(8,128)}) fusion(f32[1632]{0:T(1024)S(1)} %get-tuple-element.74, bf16[16,12,12,272]{3,0,2,1:T(8,128)(2,1)S(1)} %add_convert_fusion.1, bf16[2,272,1632]{2,1,0:T(8,128)(2,1)} %param.17), kind=kOutput, calls=%fused_computation.61 | convolution fusion | flops 2060546816 | bytes 17218688 | tf_op jit(solution)/shard_map/dot_general | solution.py:69
  189.6 14.8 %all_to_all.72 = f32[16,1,3264]{2,1,0:T(1,128)S(1)} all-to-all(f32[16,1,3264]{2,1,0:T(1,128)S(1)} %broadcast_in_dim.56), channel_id=1, replica_groups=mesh['row'=16,'col'=16] {'row'}, dimensions={0} | all-to-all | bytes 417792 | tf_op jit(solution)/shard_map/all_to_all | solution.py:18
  210.4 6.5 %all-to-all-done.7 = f32[16,1,3264]{2,1,0:T(1,128)S(1)} async-done(((f32[16,1,3264]{2,1,0:T(1,128)}), f32[16,1,3264]{2,1,0:T(1,128)S(1)}, u32[]{:S(2)}, u32[]{:S(2)}) %all-to-all-start.7) | async-done | bytes 208928 | tf_op jit(solution)/shard_map/all_to_all | solution.py:18
  217.1 7.8 %multiply_convert_fusion.1 = bf16[16,12,12,1632]{3,0,2,1:T(8,128)(2,1)S(1)} fusion(f32[16,12,12,1632]{3,0,2,1:T(8,128)} %get-tuple-element.127, f32[1632]{0:T(1024)S(1)} %get-tuple-element.98, f32[1632]{0:T(1024)S(1)} %get-tuple-element.99), kind=kLoop, calls=%fused_computation.52 | loop fusion | flops 26320896 | bytes 22573824 | tf_op jit(solution)/shard_map/convert_element_type | solution.py:121
  224.9 50.2 %subtract_reduce_fusion = (f32[1632]{0:T(1024)S(1)}, f32[1632]{0:T(1024)S(1)}, f32[16,12,12,1632]{3,0,2,1:T(8,128)}) fusion(f32[1632]{0:T(1024)S(1)} %get-tuple-element.71, f32[1632]{0:T(1024)S(1)} %get-tuple-element.66, f32[1632]{0:T(1024)S(1)} %get-tuple-element.55, f32[1632]{0:T(1024)S(1)} %get-tuple-element.18, f32[1632]{0:T(1024)S(1)} %get-tuple-element.19, ...), kind=kLoop, calls=%fused_computation.60 | loop fusion | flops 293286720 | bytes 22743552 | tf_op jit(solution)/shard_map/reduce_sum | solution.py:52
  280.4 10.6 %all-to-all-done.8 = f32[16,1,3264]{2,1,0:T(1,128)S(1)} async-done(((f32[16,1,3264]{2,1,0:T(1,128)}), f32[16,1,3264]{2,1,0:T(1,128)S(1)}, u32[]{:S(2)}, u32[]{:S(2)}) %all-to-all-start.8) | async-done | bytes 208928 | tf_op jit(solution)/shard_map/all_to_all | solution.py:18
  295.5 7.6 %all-to-all-done.9 = f32[16,1,3264]{2,1,0:T(1,128)S(1)} async-done(((f32[16,1,3264]{2,1,0:T(1,128)}), f32[16,1,3264]{2,1,0:T(1,128)S(1)}, u32[]{:S(2)}, u32[]{:S(2)}) %all-to-all-start.9) | async-done | bytes 208928 | tf_op jit(solution)/shard_map/all_to_all | solution.py:18
  303.3 8.0 %fusion.23 = f32[16,1632]{1,0:T(8,128)S(1)} fusion(f32[1632]{0:T(1024)S(1)} %get-tuple-element.95, f32[16,12,12,1632]{3,0,2,1:T(8,128)} %get-tuple-element.97, f32[1632]{0:T(1024)S(1)} %get-tuple-element.96), kind=kLoop, calls=%fused_computation.97 | loop fusion | flops 26294784 | bytes 15158016 | tf_op jit(solution)/shard_map/reduce_sum | solution.py:86
  313.0 7.5 %subtract_reduce_fusion.4 = (f32[272]{0:T(512)S(1)}, f32[272]{0:T(512)S(1)}, f32[16,12,12,272]{3,0,2,1:T(8,128)}) fusion(f32[272]{0:T(512)S(1)} %get-tuple-element.87, bf16[2,1632,272]{1,2,0:T(8,128)(2,1)} %param.23, f32[16,1632]{1,0:T(8,128)S(1)} %fusion.11, f32[1632]{0:T(1024)S(1)} %get-tuple-element.95, f32[16,12,12,1632]{3,0,2,1:T(8,128)S(1)} %copy-done, ...), kind=kOutput, calls=%fused_computation.72 | convolution fusion | flops 2078096896 | bytes 18573248 | tf_op jit(solution)/shard_map/dot_general | solution.py:69
  326.3 6.9 %all-to-all-done.10 = f32[16,1,544]{2,1,0:T(1,128)S(1)} async-done(((f32[16,1,544]{2,1,0:T(1,128)}), f32[16,1,544]{2,1,0:T(1,128)S(1)}, u32[]{:S(2)}, u32[]{:S(2)}) %all-to-all-start.10) | async-done | bytes 34848 | tf_op jit(solution)/shard_map/all_to_all | solution.py:18
  338.0 5.8 %all-to-all-done.11 = f32[16,1,544]{2,1,0:T(1,128)S(1)} async-done(((f32[16,1,544]{2,1,0:T(1,128)}), f32[16,1,544]{2,1,0:T(1,128)S(1)}, u32[]{:S(2)}, u32[]{:S(2)}) %all-to-all-start.11) | async-done | bytes 34848 | tf_op jit(solution)/shard_map/all_to_all | solution.py:18
  (112 shorter events, 63.5 us)
Async XLA Ops:
  0.6 23.4 %copy-start.8 = (f32[2,1632]{1,0:T(2,128)S(1)}, f32[2,1632]{1,0:T(2,128)}, u32[]{:S(2)}) copy-start(f32[2,1632]{1,0:T(2,128)} %param.22) | copy-start | bytes 39172
  0.6 23.4 %copy-start.5 = (f32[2,2,1632]{2,1,0:T(2,128)S(1)}, f32[2,2,1632]{2,1,0:T(2,128)}, u32[]{:S(2)}) copy-start(f32[2,2,1632]{2,1,0:T(2,128)} %param.24) | copy-start | bytes 78340
  0.7 23.5 %copy-start.4 = (f32[2,25,1632]{2,0,1:T(2,128)S(1)}, f32[2,25,1632]{2,0,1:T(2,128)}, u32[]{:S(2)}) copy-start(f32[2,25,1632]{2,0,1:T(2,128)} %param.18) | copy-start | bytes 979204
  0.7 23.7 %copy-start.7 = (f32[2,2,1632]{2,1,0:T(2,128)S(1)}, f32[2,2,1632]{2,1,0:T(2,128)}, u32[]{:S(2)}) copy-start(f32[2,2,1632]{2,1,0:T(2,128)} %param.29) | copy-start | bytes 78340
  0.7 23.7 %copy-start.6 = (f32[2,2,1632]{2,1,0:T(2,128)S(1)}, f32[2,2,1632]{2,1,0:T(2,128)}, u32[]{:S(2)}) copy-start(f32[2,2,1632]{2,1,0:T(2,128)} %param.25) | copy-start | bytes 78340
  0.7 23.9 %copy-start.2 = (f32[2,1632,68]{1,0,2:T(2,128)S(1)}, f32[2,1632,68]{1,0,2:T(2,128)}, u32[]{:S(2)}) copy-start(f32[2,1632,68]{1,0,2:T(2,128)} %param.19) | copy-start | bytes 2663428
  1.6 40.7 %copy-start.9 = (f32[2,272]{1,0:T(2,128)S(1)}, f32[2,272]{1,0:T(2,128)}, u32[]{:S(2)}) copy-start(f32[2,272]{1,0:T(2,128)} %param.30) | copy-start | bytes 6532
  14.1 20.5 %all-to-all-start = ((f32[16,1,3264]{2,1,0:T(1,128)}), f32[16,1,3264]{2,1,0:T(1,128)S(1)}, u32[]{:S(2)}, u32[]{:S(2)}) async-start(f32[16,1,3264]{2,1,0:T(1,128)} %broadcast_in_dim.24), calls=%async_computation | async-start | bytes 425984 | tf_op jit(solution)/shard_map/all_to_all | solution.py:18
  35.5 14.4 %all-to-all-start.1 = ((f32[16,1,3264]{2,1,0:T(1,128)}), f32[16,1,3264]{2,1,0:T(1,128)S(1)}, u32[]{:S(2)}, u32[]{:S(2)}) async-start(f32[16,1,3264]{2,1,0:T(1,128)} %broadcast_in_dim.25), calls=%async_computation.1 | async-start | bytes 425984 | tf_op jit(solution)/shard_map/all_to_all | solution.py:18
  58.0 55.7 %copy-start.3 = (f32[2,68,1632]{2,0,1:T(2,128)S(1)}, f32[2,68,1632]{2,0,1:T(2,128)}, u32[]{:S(2)}) copy-start(f32[2,68,1632]{2,0,1:T(2,128)} %param.21) | copy-start | bytes 2663428
  58.0 70.8 %copy-start.13 = (f32[2,68]{1,0:T(2,128)S(1)}, f32[2,68]{1,0:T(2,128)}, u32[]{:S(2)}) copy-start(f32[2,68]{1,0:T(2,128)} %param.20) | copy-start | bytes 1636
  109.1 15.3 %all-to-all-start.2 = ((f32[16,1,3264]{2,1,0:T(1,128)}), f32[16,1,3264]{2,1,0:T(1,128)S(1)}, u32[]{:S(2)}, u32[]{:S(2)}) async-start(f32[16,1,3264]{2,1,0:T(1,128)} %broadcast_in_dim.52), calls=%async_computation.2 | async-start | bytes 425984 | tf_op jit(solution)/shard_map/all_to_all | solution.py:18
  125.3 11.2 %all-to-all-start.3 = ((f32[16,1,3264]{2,1,0:T(1,128)}), f32[16,1,3264]{2,1,0:T(1,128)S(1)}, u32[]{:S(2)}, u32[]{:S(2)}) async-start(f32[16,1,3264]{2,1,0:T(1,128)} %broadcast_in_dim.53), calls=%async_computation.3 | async-start | bytes 425984 | tf_op jit(solution)/shard_map/all_to_all | solution.py:18
  136.6 9.8 %copy-start.1 = (f32[16,12,12,1632]{3,0,2,1:T(8,128)S(1)}, f32[16,12,12,1632]{3,0,2,1:T(8,128)}, u32[]{:S(2)}) copy-start(f32[16,12,12,1632]{3,0,2,1:T(8,128)} %get-tuple-element.104) | copy-start | bytes 45121540
  146.4 12.7 %copy-start.10 = (f32[2,272]{1,0:T(2,128)S(1)}, f32[2,272]{1,0:T(2,128)}, u32[]{:S(2)}) copy-start(f32[2,272]{1,0:T(2,128)} %param.27) | copy-start | bytes 6532
  146.4 12.7 %copy-start.11 = (f32[2,272]{1,0:T(2,128)S(1)}, f32[2,272]{1,0:T(2,128)}, u32[]{:S(2)}) copy-start(f32[2,272]{1,0:T(2,128)} %param.31) | copy-start | bytes 6532
  146.4 24.4 %copy-start.12 = (f32[2,272]{1,0:T(2,128)S(1)}, f32[2,272]{1,0:T(2,128)}, u32[]{:S(2)}) copy-start(f32[2,272]{1,0:T(2,128)} %param.26) | copy-start | bytes 6532
  154.7 12.0 %all-to-all-start.4 = ((f32[16,1,544]{2,1,0:T(1,128)}), f32[16,1,544]{2,1,0:T(1,128)S(1)}, u32[]{:S(2)}, u32[]{:S(2)}) async-start(f32[16,1,544]{2,1,0:T(1,128)} %broadcast_in_dim.54), calls=%async_computation.4 | async-start | bytes 81920 | tf_op jit(solution)/shard_map/all_to_all | solution.py:18
  167.4 9.9 %all-to-all-start.5 = ((f32[16,1,544]{2,1,0:T(1,128)}), f32[16,1,544]{2,1,0:T(1,128)S(1)}, u32[]{:S(2)}, u32[]{:S(2)}) async-start(f32[16,1,544]{2,1,0:T(1,128)} %broadcast_in_dim.55), calls=%async_computation.5 | async-start | bytes 81920 | tf_op jit(solution)/shard_map/all_to_all | solution.py:18
  205.4 11.5 %all-to-all-start.7 = ((f32[16,1,3264]{2,1,0:T(1,128)}), f32[16,1,3264]{2,1,0:T(1,128)S(1)}, u32[]{:S(2)}, u32[]{:S(2)}) async-start(f32[16,1,3264]{2,1,0:T(1,128)} %broadcast_in_dim.57), calls=%async_computation.7 | async-start | bytes 425984 | tf_op jit(solution)/shard_map/all_to_all | solution.py:18
  276.0 14.9 %all-to-all-start.8 = ((f32[16,1,3264]{2,1,0:T(1,128)}), f32[16,1,3264]{2,1,0:T(1,128)S(1)}, u32[]{:S(2)}, u32[]{:S(2)}) async-start(f32[16,1,3264]{2,1,0:T(1,128)} %broadcast_in_dim.58), calls=%async_computation.8 | async-start | bytes 425984 | tf_op jit(solution)/shard_map/all_to_all | solution.py:18
  291.9 11.2 %all-to-all-start.9 = ((f32[16,1,3264]{2,1,0:T(1,128)}), f32[16,1,3264]{2,1,0:T(1,128)S(1)}, u32[]{:S(2)}, u32[]{:S(2)}) async-start(f32[16,1,3264]{2,1,0:T(1,128)} %broadcast_in_dim.59), calls=%async_computation.9 | async-start | bytes 425984 | tf_op jit(solution)/shard_map/all_to_all | solution.py:18
  321.2 12.0 %all-to-all-start.10 = ((f32[16,1,544]{2,1,0:T(1,128)}), f32[16,1,544]{2,1,0:T(1,128)S(1)}, u32[]{:S(2)}, u32[]{:S(2)}) async-start(f32[16,1,544]{2,1,0:T(1,128)} %broadcast_in_dim.60), calls=%async_computation.10 | async-start | bytes 81920 | tf_op jit(solution)/shard_map/all_to_all | solution.py:18
  333.9 9.9 %all-to-all-start.11 = ((f32[16,1,544]{2,1,0:T(1,128)}), f32[16,1,544]{2,1,0:T(1,128)S(1)}, u32[]{:S(2)}, u32[]{:S(2)}) async-start(f32[16,1,544]{2,1,0:T(1,128)} %broadcast_in_dim.61), calls=%async_computation.11 | async-start | bytes 81920 | tf_op jit(solution)/shard_map/all_to_all | solution.py:18
  (1 other events, 9.8 us)
where the time goes:
time: 350 us; the launch traced here: 349 us
  other arithmetic  144 us (41%)
  waiting for transfers between devices  85.3 us (24%)
  starting transfers between devices  52.4 us (15%)
  matrix products  37.2 us (11%)
  blocking collectives  14.8 us (4%)
  local copies, waits for them, and re-layouts  14.4 us (4%)
    reduce_sum x2, other arithmetic, renorm(): first_sum = jnp.sum(centered, axis=(0, 1, 2))  100 us
    all_to_all x11, waiting for transfers between devices, from_everyone(): return lax.all_to_all(copies, axis, split_axis=0, concat_axis=0, tiled=True)  85.3 us
    all_to_all x11, starting transfers between devices, from_everyone(): return lax.all_to_all(copies, axis, split_axis=0, concat_axis=0, tiled=True)  52.4 us
    dot_general x4, matrix products, project_rows(): product = jnp.dot(flat_rows, matrix, preferred_element_type=jnp.float32)  35.4 us
    reduce_sum x2, other arithmetic, excite(): pooled = jnp.mean(lifted, axis=(1, 2))  15.9 us
    convert_element_type x2, other arithmetic, per_device(): jax.nn.silu(expanded * first_coef[0] + first_coef[1]).astype(jnp.bfloat16)  15.6 us
    all_to_all x1, blocking collectives, from_everyone(): return lax.all_to_all(copies, axis, split_axis=0, concat_axis=0, tiled=True)  14.8 us
    broadcast_in_dim x12, local copies, waits for them, and re-layouts, from_everyone(): copies = jnp.broadcast_to(shard, (lax.axis_size(axis), *shard.shape))  8.22 us
  transfers between devices with their start and end apart: 11, of which 11 were waited for; matrix products, arithmetic and copies ran while one was open for 1% of the time, Pallas kernels for 0%

commit v1 on v0

v1 whole, which is shorter than its diff:
```python
import functools
import jax
import jax.numpy as jnp
from jax import lax
from jax.experimental import pallas as pl
from jax.experimental.pallas import tpu as pltpu
from jax.sharding import PartitionSpec as P

KERN = 5
LAYERS = 2
EPSILON = 0.001
RATIO_MAX = 3.0
SHIFT_MAX = 5.0
MOMENTUM = 0.01
LANE = 128
WIDE = 256


def coefficients(received, row_count, run_mean, run_var, gain, bias):
    sums = jnp.sum(received, axis=0)
    offset = sums[0:1] / row_count
    batch_var = sums[1:2] / row_count - offset * offset
    batch_mean = run_mean + offset
    batch_sigma = jnp.sqrt(batch_var + EPSILON)
    run_sigma = jnp.sqrt(run_var + EPSILON)
    scale_ratio = jnp.clip(batch_sigma / run_sigma, 1.0 / RATIO_MAX, RATIO_MAX)
    shift_clip = jnp.clip(offset / run_sigma, -SHIFT_MAX, SHIFT_MAX)
    gain_scale = gain * scale_ratio / batch_sigma
    gain_shift = bias + gain * shift_clip - batch_mean * gain_scale
    new_mean = run_mean + MOMENTUM * offset
    new_var = run_var + MOMENTUM * (batch_var - run_var)
    return gain_scale, gain_shift, new_mean, new_var


def half_silu(half):
    return half + half * jnp.tanh(half)


def fold_rows(block):
    return jnp.sum(block.reshape(block.shape[0] // 8, 8, block.shape[1]), axis=0)


def store_stats(stat_ref, first, second):
    members = stat_ref.shape[0]
    pair = jnp.concatenate(
        [jnp.sum(first, axis=0, keepdims=True), jnp.sum(second, axis=0, keepdims=True)], axis=0
    )
    stat_ref[...] = jnp.broadcast_to(pair[None], (members,) + pair.shape)


def expand_moments(x_ref, w_ref, mean, stat_ref, chunk):
    rows = x_ref.shape[0]
    weight = w_ref[0]

    def step(i, carry):
        first, second = carry
        start = pl.multiple_of(i * chunk, chunk)
        values = jnp.dot(x_ref[pl.ds(start, chunk), :], weight, preferred_element_type=jnp.float32)
        centered = values - mean
        return first + fold_rows(centered), second + fold_rows(centered * centered)

    zero = jnp.zeros((8, weight.shape[1]), jnp.float32)
    first, second = lax.fori_loop(0, rows // chunk, step, (zero, zero))
    store_stats(stat_ref, first, second)


def moments_kernel(x_ref, w_ref, mean_ref, stat_ref, *, chunk):
    expand_moments(x_ref, w_ref, mean_ref[0, 0:1], stat_ref, chunk)


def moments_call(x, expand_weight, mid_mean, layer, members):
    rows, out = x.shape
    mid = expand_weight.shape[2]
    steps = pl.cdiv(mid, WIDE)
    return pl.pallas_call(
        functools.partial(moments_kernel, chunk=rows // 6),
        grid=(steps,),
        in_specs=[
            pl.BlockSpec((rows, out), lambda j: (0, 0)),
            pl.BlockSpec((1, out, WIDE), lambda j: (layer, 0, j)),
            pl.BlockSpec((1, 2, WIDE), lambda j: (layer, 0, j)),
        ],
        out_specs=pl.BlockSpec((members, 2, WIDE), lambda j: (0, 0, j)),
        out_shape=jax.ShapeDtypeStruct((members, 2, mid), jnp.float32),
        name="expand_moments",
    )(x, expand_weight, mid_mean)


def depth_kernel_body(
    x_ref, w_ref, dk_ref, recv_ref, mean_ref, var_ref, gain_ref, bias_ref, mean2_ref,
    spread_ref, stat_ref, new_ref, act_ref, *, row_count, side, chunk,
):
    j = pl.program_id(0)
    rows = x_ref.shape[0]
    reach = KERN // 2

    @pl.when(j % 2 == 0)
    def _():
        scale, shift, new_mean, new_var = coefficients(
            recv_ref[...], row_count, mean_ref[0, 0:1], var_ref[0, 0:1], gain_ref[0, 0:1], bias_ref[0, 0:1]
        )
        new_ref[...] = jnp.concatenate([new_mean, new_var], axis=0)
        scale = 0.5 * scale
        shift = 0.5 * shift
        weight = w_ref[0]
        cells = chunk // 16

        def step(i, carry):
            start = pl.multiple_of(i * chunk, chunk)
            values = jnp.dot(x_ref[pl.ds(start, chunk), :], weight, preferred_element_type=jnp.float32)
            active = half_silu(values * scale + shift).astype(jnp.bfloat16).astype(jnp.float32)
            active = active.reshape(cells, 2, 8, WIDE)
            at = pl.multiple_of(i * cells, cells)
            for s in range(2):
                for b in range(2):
                    act_ref[s, b, pl.ds(at, cells)] = active[:, b, :, s * LANE : (s + 1) * LANE]
            return carry

        lax.fori_loop(0, rows // chunk, step, 0)

    mean2 = mean2_ref[0, 1:2]
    s = j % 2

    def half(b, carry):
        first, second = carry
        for h in range(side):
            acc = [None] * side
            for i in range(KERN):
                r = h + i - reach
                if r < 0 or r >= side:
                    continue
                line = [act_ref[s, b, r * side + w] for w in range(side)]
                for k in range(KERN):
                    tap = dk_ref[0, i * KERN + k : i * KERN + k + 1, :]
                    tap = jnp.broadcast_to(tap, (8, LANE))
                    for w in range(side):
                        p = w + k - reach
                        if p < 0 or p >= side:
                            continue
                        term = line[p] * tap
                        acc[w] = term if acc[w] is None else acc[w] + term
            for w in range(side):
                spread_ref[h * side + w, b] = acc[w]
                centered = acc[w] - mean2
                first = first + centered
                second = second + centered * centered
        return first, second

    zero = jnp.zeros((8, LANE), jnp.float32)
    first, second = lax.fori_loop(0, 2, half, (zero, zero))
    store_stats(stat_ref, first, second)


def depth_call(x, expand_weight, depth_kernel, received, mid_mean, mid_var, mid_gain, mid_bias, layer, side, row_count):
    rows, out = x.shape
    mid = expand_weight.shape[2]
    members = received.shape[0]
    cells = side * side
    steps = pl.cdiv(mid, LANE)
    pair = pl.BlockSpec((1, 2, WIDE), lambda j: (layer, 0, j // 2))
    return pl.pallas_call(
        functools.partial(depth_kernel_body, row_count=row_count, side=side, chunk=rows // 12),
        grid=(steps,),
        in_specs=[
            pl.BlockSpec((rows, out), lambda j: (0, 0)),
            pl.BlockSpec((1, out, WIDE), lambda j: (layer, 0, j // 2)),
            pl.BlockSpec((1, KERN * KERN, LANE), lambda j: (layer, 0, j)),
            pl.BlockSpec((members, 2, WIDE), lambda j: (0, 0, j // 2)),
            pair, pair, pair, pair,
            pl.BlockSpec((1, 2, LANE), lambda j: (layer, 0, j)),
        ],
        out_specs=[
            pl.BlockSpec((cells, 2, 8, LANE), lambda j: (0, 0, 0, j)),
            pl.BlockSpec((members, 2, LANE), lambda j: (0, 0, j)),
            pl.BlockSpec((2, WIDE), lambda j: (0, j // 2)),
        ],
        out_shape=[
            jax.ShapeDtypeStruct((cells, 2, 8, mid), jnp.float32),
            jax.ShapeDtypeStruct((members, 2, mid), jnp.float32),
            jax.ShapeDtypeStruct((2, mid), jnp.float32),
        ],
        scratch_shapes=[pltpu.VMEM((2, 2, cells, 8, LANE), jnp.float32)],
        name="depthwise",
    )(x, expand_weight, depth_kernel, received, mid_mean, mid_var, mid_gain, mid_bias, mid_mean)


def lift_kernel(
    spread_ref, recv_ref, mean_ref, var_ref, gain_ref, bias_ref,
    w1_ref, b1_ref, w2_ref, b2_ref, wp_ref, mean3_ref,
    proj_ref, stat_ref, new_ref,
    lift_ref, pool_ref, gate_ref, scaled_ref, sum_ref, *, row_count, blocks, mid, layer, parts,
):
    j = pl.program_id(0)
    cells = lift_ref.shape[1]
    group = cells // parts

    @pl.when(j < blocks)
    def _():
        scale, shift, new_mean, new_var = coefficients(
            recv_ref[...], row_count, mean_ref[0, 1:2], var_ref[0, 1:2], gain_ref[0, 1:2], bias_ref[0, 1:2]
        )
        new_ref[...] = jnp.concatenate([new_mean, new_var], axis=0)
        scale = 0.5 * scale
        shift = 0.5 * shift

        def step(i, pooled):
            at = pl.multiple_of(i * 4, 4)
            values = spread_ref[pl.ds(at, 4)]
            lifted = half_silu(values * scale + shift)
            lift_ref[j, pl.ds(at, 4)] = lifted
            return pooled + jnp.sum(lifted, axis=0)

        pooled = lax.fori_loop(0, cells // 4, step, jnp.zeros((2, 8, WIDE), jnp.float32))
        pool_ref[j] = (pooled * (1.0 / cells)).reshape(16, WIDE)

    @pl.when(j == blocks)
    def _():
        last = mid - (blocks - 1) * WIDE
        squeezed = b1_ref[layer : layer + 1, :] + jnp.zeros((16, b1_ref.shape[1]), jnp.float32)
        for k in range(blocks):
            size = WIDE if k < blocks - 1 else last
            squeezed = squeezed + jnp.dot(
                pool_ref[k, :, :size], w1_ref[0, k * WIDE : k * WIDE + size, :],
                precision=lax.Precision.HIGHEST, preferred_element_type=jnp.float32,
            )
        squeezed = half_silu(0.5 * squeezed)
        for k in range(blocks):
            size = WIDE if k < blocks - 1 else last
            grown = jnp.dot(
                squeezed, w2_ref[0, :, k * WIDE : k * WIDE + size],
                precision=lax.Precision.HIGHEST, preferred_element_type=jnp.float32,
            ) + b2_ref[layer : layer + 1, k * WIDE : k * WIDE + size]
            gate_ref[k, :, :, :size] = jax.nn.sigmoid(grown).reshape(2, 8, size)

    @pl.when(j >= blocks)
    def _():
        part = j - blocks
        base = pl.multiple_of(part * group, group)
        last = mid - (blocks - 1) * WIDE
        for k in range(blocks):
            size = WIDE if k < blocks - 1 else last
            gate = gate_ref[k, :, :, :size]

            def step(i, carry):
                at = pl.multiple_of(i * 4, 4)
                lifted = lift_ref[k, pl.ds(base + at, 4), :, :, :size]
                scaled = (lifted * gate).reshape(64, size).astype(jnp.bfloat16)
                scaled_ref[pl.ds(pl.multiple_of(i * 64, 64), 64), k * WIDE : k * WIDE + size] = scaled
                return carry

            lax.fori_loop(0, group // 4, step, 0)
        projected = jnp.dot(scaled_ref[...], wp_ref[0], preferred_element_type=jnp.float32)
        proj_ref[...] = projected
        centered = projected - mean3_ref[layer : layer + 1, :]
        first = fold_rows(centered)
        second = fold_rows(centered * centered)

        @pl.when(part == 0)
        def _():
            sum_ref[0] = first
            sum_ref[1] = second

        @pl.when(part > 0)
        def _():
            sum_ref[0] += first
            sum_ref[1] += second

        @pl.when(part == parts - 1)
        def _():
            store_stats(stat_ref, sum_ref[0], sum_ref[1])


def lift_call(
    spread, received, mid_mean, mid_var, mid_gain, mid_bias,
    squeeze_weight, squeeze_bias, excite_weight, excite_bias, project_weight, out_mean, layer, row_count,
):
    cells, _, _, mid = spread.shape
    members = received.shape[0]
    out = project_weight.shape[2]
    squeeze = squeeze_weight.shape[2]
    blocks = pl.cdiv(mid, WIDE)
    parts = 3
    rows = cells * 16
    here = lambda j: jnp.minimum(j, blocks - 1)
    pair = pl.BlockSpec((1, 2, WIDE), lambda j: (layer, 0, here(j)))
    return pl.pallas_call(
        functools.partial(
            lift_kernel, row_count=row_count, blocks=blocks, mid=mid, layer=layer, parts=parts
        ),
        grid=(blocks + parts,),
        in_specs=[
            pl.BlockSpec((cells, 2, 8, WIDE), lambda j: (0, 0, 0, here(j))),
            pl.BlockSpec((members, 2, WIDE), lambda j: (0, 0, here(j))),
            pair, pair, pair, pair,
            pl.BlockSpec((1, mid, squeeze), lambda j: (layer, 0, 0)),
            pl.BlockSpec((LAYERS, squeeze), lambda j: (0, 0)),
            pl.BlockSpec((1, squeeze, mid), lambda j: (layer, 0, 0)),
            pl.BlockSpec((LAYERS, mid), lambda j: (0, 0)),
            pl.BlockSpec((1, mid, out), lambda j: (layer, 0, 0)),
            pl.BlockSpec((LAYERS, out), lambda j: (0, 0)),
        ],
        out_specs=[
            pl.BlockSpec((rows // parts, out), lambda j: (jnp.maximum(j - blocks, 0), 0)),
            pl.BlockSpec((members, 2, out), lambda j: (0, 0, 0)),
            pl.BlockSpec((2, WIDE), lambda j: (0, here(j))),
        ],
        out_shape=[
            jax.ShapeDtypeStruct((rows, out), jnp.float32),
            jax.ShapeDtypeStruct((members, 2, out), jnp.float32),
            jax.ShapeDtypeStruct((2, mid), jnp.float32),
        ],
        scratch_shapes=[
            pltpu.VMEM((blocks, cells, 2, 8, WIDE), jnp.float32),
            pltpu.VMEM((blocks, 16, WIDE), jnp.float32),
            pltpu.VMEM((blocks, 2, 8, WIDE), jnp.float32),
            pltpu.VMEM((rows // parts, mid), jnp.bfloat16),
            pltpu.VMEM((2, 8, out), jnp.float32),
        ],
        name="lift_project",
    )(
        spread, received, mid_mean, mid_var, mid_gain, mid_bias,
        squeeze_weight, squeeze_bias, excite_weight, excite_bias, project_weight, out_mean,
    )


def output_kernel(
    x_ref, proj_ref, recv_ref, mean_ref, var_ref, gain_ref, bias_ref, *rest, row_count, layer, chunk, follow
):
    if follow:
        w_ref, mid_mean_ref, next_ref, new_ref, stat_ref = rest
    else:
        next_ref, new_ref = rest

    def produce():
        at = slice(layer, layer + 1)
        scale, shift, new_mean, new_var = coefficients(
            recv_ref[...], row_count, mean_ref[at], var_ref[at], gain_ref[at], bias_ref[at]
        )
        new_ref[...] = jnp.concatenate([new_mean, new_var], axis=0)

        def step(i, carry):
            here = pl.ds(pl.multiple_of(i * 64, 64), 64)
            total = x_ref[here, :].astype(jnp.float32) + proj_ref[here, :] * scale + shift
            next_ref[here, :] = total.astype(jnp.bfloat16)
            return carry

        lax.fori_loop(0, x_ref.shape[0] // 64, step, 0)

    if follow:
        pl.when(pl.program_id(0) == 0)(produce)
        expand_moments(next_ref, w_ref, mid_mean_ref[0, 0:1], stat_ref, chunk)
    else:
        produce()


def output_call(x, projected, received, out_mean, out_var, out_gain, out_bias, layer, row_count, follow=None):
    rows, out = x.shape
    members = received.shape[0]
    whole = pl.BlockSpec((LAYERS, out), lambda j: (0, 0))
    flat = pl.BlockSpec((rows, out), lambda j: (0, 0))
    in_specs = [flat, flat, pl.BlockSpec((members, 2, out), lambda j: (0, 0, 0)), whole, whole, whole, whole]
    out_specs = [flat, pl.BlockSpec((2, out), lambda j: (0, 0))]
    out_shape = [jax.ShapeDtypeStruct((rows, out), jnp.bfloat16), jax.ShapeDtypeStruct((2, out), jnp.float32)]
    operands = [x, projected, received, out_mean, out_var, out_gain, out_bias]
    steps = 1
    if follow is not None:
        expand_weight, mid_mean, sharers = follow
        mid = expand_weight.shape[2]
        steps = pl.cdiv(mid, WIDE)
        in_specs += [
            pl.BlockSpec((1, out, WIDE), lambda j: (layer + 1, 0, j)),
            pl.BlockSpec((1, 2, WIDE), lambda j: (layer + 1, 0, j)),
        ]
        out_specs.append(pl.BlockSpec((sharers, 2, WIDE), lambda j: (0, 0, j)))
        out_shape.append(jax.ShapeDtypeStruct((sharers, 2, mid), jnp.float32))
        operands += [expand_weight, mid_mean]
    return pl.pallas_call(
        functools.partial(
            output_kernel, row_count=row_count, layer=layer, chunk=rows // 6, follow=follow is not None
        ),
        grid=(steps,),
        in_specs=in_specs,
        out_specs=out_specs,
        out_shape=out_shape,
        name="block_output",
    )(*operands)


def exchange(stats):
    sums = lax.all_to_all(stats, "row", split_axis=0, concat_axis=0, tiled=True)
    total = jnp.sum(sums, axis=0)
    copies = jnp.broadcast_to(total[None], (lax.axis_size("col"),) + total.shape)
    return lax.all_to_all(copies, "col", split_axis=0, concat_axis=0, tiled=True)


def per_device(
    images, expand_weight, depth_kernel, squeeze_weight, squeeze_bias, excite_weight, excite_bias,
    project_weight, mid_gain, mid_bias, out_gain, out_bias, mid_mean, mid_var, out_mean, out_var,
):
    batch, side, _, out = images.shape
    members = lax.axis_size("row")
    row_count = float(batch * side * side * members * lax.axis_size("col"))
    current = jnp.transpose(images, (1, 2, 0, 3)).reshape(side * side * batch, out)
    mid_new, out_new = [], []
    stats = moments_call(current, expand_weight, mid_mean, 0, members)
    for layer in range(LAYERS):
        received = exchange(stats)
        spread, stats, first_new = depth_call(
            current, expand_weight, depth_kernel, received, mid_mean, mid_var, mid_gain, mid_bias,
            layer, side, row_count,
        )
        received = exchange(stats)
        projected, stats, second_new = lift_call(
            spread, received, mid_mean, mid_var, mid_gain, mid_bias, squeeze_weight, squeeze_bias,
            excite_weight, excite_bias, project_weight, out_mean, layer, row_count,
        )
        received = exchange(stats)
        follow = (expand_weight, mid_mean, members) if layer + 1 < LAYERS else None
        results = output_call(
            current, projected, received, out_mean, out_var, out_gain, out_bias, layer, row_count, follow
        )
        current, third_new = results[0], results[1]
        if follow is not None:
            stats = results[2]
        mid_new.append(jnp.stack([first_new, second_new]))
        out_new.append(third_new)
    mid_new = jnp.stack(mid_new)
    out_new = jnp.stack(out_new)
    block_output = jnp.transpose(current.reshape(side, side, batch, out), (2, 0, 1, 3))
    return block_output, mid_new[:, :, 0], mid_new[:, :, 1], out_new[:, 0], out_new[:, 1]


def solution(mesh):
    split = P(("row", "col"), None, None, None)
    return jax.shard_map(
        per_device, mesh=mesh, in_specs=(split,) + (P(),) * 15, out_specs=(split, P(), P(), P(), P()), check_vma=False
    )
```

time: 350 us -> 335 us (0.957)
  Pallas kernels: 0 us -> 167 us
  other arithmetic: 144 us -> 1.93 us
  blocking collectives: 14.8 us -> 100 us
  waiting for transfers between devices: 85.3 us -> 28.3 us
  matrix products: 37.2 us -> 0 us
  starting transfers between devices: 52.4 us -> 21.8 us
    pallas_call x0 -> x7, Pallas kernels: none -> 167 us  [the longest x2 92.2 us: depth_call(): pl.pallas_call(functools.partial(depth_kernel_body, row_count=row_count,...]
    reduce_sum x16 -> x6, other arithmetic: 118 us -> 0.37 us  [exchange(): total = jnp.sum(sums, axis=0)]
    all_to_all x1 -> x7, blocking collectives: 14.8 us -> 100 us  [the longest x5 78.4 us: exchange(): sums = lax.all_to_all(stats, 'row', split_axis=0, concat_axis=0, tiled=True)]
    all_to_all x11 -> x5, waiting for transfers between devices: 85.3 us -> 28.3 us  [the longest x4 21.5 us: exchange(): lax.all_to_all(copies, 'col', split_axis=0, concat_axis=0, tiled=True)]
    dot_general x8 -> x0, matrix products: 37.2 us -> none  [the longest x4 35.4 us: project_rows(): product = jnp.dot(flat_rows, matrix, preferred_element_type=jnp.float32)]
    all_to_all x11 -> x5, starting transfers between devices: 52.4 us -> 21.8 us  [the longest x4 17.3 us: exchange(): lax.all_to_all(copies, 'col', split_axis=0, concat_axis=0, tiled=True)]
    convert_element_type x4 -> x0, other arithmetic: 22.5 us -> none  [the longest x2 15.6 us: per_device(): jax.nn.silu(expanded * first_coef[0] + first_coef[1]).astype(jnp.bfloat16)]
    unnamed x28, local copies, waits for them, and re-layouts: 1.63 us -> 10.9 us
  transfers between devices with their start and end apart: 11 -> 5, of which waited for: 11 -> 5; matrix products, arithmetic and copies ran while one was open for 1% -> 3% of each run, Pallas kernels for 0% -> 0%
where the time goes in v1:
time: 335 us; the launch traced here: 334 us
  Pallas kernels  167 us (50%)
  blocking collectives  100 us (30%)
  waiting for transfers between devices  28.3 us (8%)
  starting transfers between devices  21.8 us (7%)
  local copies, waits for them, and re-layouts  13.9 us (4%)
    pallas_call x2, Pallas kernels, depth_call(): pl.pallas_call(functools.partial(depth_kernel_body, row_count=row_count,...  92.2 us
    all_to_all x5, blocking collectives, exchange(): sums = lax.all_to_all(stats, 'row', split_axis=0, concat_axis=0, tiled=True)  78.4 us
    pallas_call x2, Pallas kernels, lift_call(): pl.pallas_call(functools.partial(lift_kernel, row_count=row_count, blocks...  40.3 us
    all_to_all x2, blocking collectives, exchange(): lax.all_to_all(copies, 'col', split_axis=0, concat_axis=0, tiled=True)  21.8 us
    all_to_all x4, waiting for transfers between devices, exchange(): lax.all_to_all(copies, 'col', split_axis=0, concat_axis=0, tiled=True)  21.5 us
    pallas_call x2, Pallas kernels, output_call(): pl.pallas_call(functools.partial(output_kernel, row_count=row_count, laye...  20.9 us
    all_to_all x4, starting transfers between devices, exchange(): lax.all_to_all(copies, 'col', split_axis=0, concat_axis=0, tiled=True)  17.3 us
    pallas_call x1, Pallas kernels, moments_call(): pl.pallas_call(functools.partial(moments_kernel, chunk=rows // 6), grid=(...  13.8 us
  transfers between devices with their start and end apart: 5, of which 5 were waited for; matrix products, arithmetic and copies ran while one was open for 3% of the time, Pallas kernels for 0%

profile of v1, /device:TPU:1, one launch (start us, length us, event | category | flops | bytes accessed | tf_op | source)
XLA Modules:
  0.0 334.1 jit_solution(9203886658436906325)
XLA Ops:
  0.6 13.8 %expand_moments.1 = f32[16,2,1632]{2,1,0:T(2,128)} custom-call(bf16[2304,272]{1,0:T(8,128)(2,1)} %bitcast.24, bf16[2,272,1632]{2,1,0:T(8,128)(2,1)} %w_ref.5, f32[2,2,1632]{2,1,0:T(2,128)} %mean_ref.12), custom_call_target="tpu_custom_call" | custom-call | tf_op jit(solution)/shard_map/expand_moments/pallas_call | solution.py:75
  14.4 20.5 %all_to_all.60 = f32[16,2,1632]{2,1,0:T(2,128)S(1)} all-to-all(f32[16,2,1632]{2,1,0:T(2,128)} %expand_moments.1), channel_id=1, replica_groups=mesh['row'=16,'col'=16] {'row'}, dimensions={0} | all-to-all | bytes 417792 | tf_op jit(solution)/shard_map/all_to_all | solution.py:390
  35.8 6.8 %all-to-all-start.1 = ((f32[16,2,1632]{2,1,0:T(2,128)}), f32[16,2,1632]{2,1,0:T(2,128)S(1)}, u32[]{:S(2)}, u32[]{:S(2)}) async-start(f32[16,2,1632]{2,1,0:T(2,128)} %broadcast_in_dim.12), calls=%async_computation.1 | async-start | bytes 425984 | tf_op jit(solution)/shard_map/all_to_all | solution.py:393
  43.3 6.9 %all-to-all-done.1.recv_ref = f32[16,2,1632]{2,1,0:T(2,128)S(1)} async-done(((f32[16,2,1632]{2,1,0:T(2,128)}), f32[16,2,1632]{2,1,0:T(2,128)S(1)}, u32[]{:S(2)}, u32[]{:S(2)}) %all-to-all-start.1) | async-done | bytes 208928 | tf_op jit(solution)/shard_map/all_to_all | solution.py:393
  50.9 46.1 %depthwise.2 = (f32[144,2,8,1632]{3,2,1,0:T(8,128)}, f32[16,2,1632]{2,1,0:T(2,128)}, f32[2,1632]{1,0:T(2,128)}) custom-call(bf16[2304,272]{1,0:T(8,128)(2,1)} %bitcast.25, bf16[2,272,1632]{2,1,0:T(8,128)(2,1)} %w_ref.5, f32[2,25,1632]{2,1,0:T(8,128)} %copy.21.dk_ref, f32[16,2,1632]{2,1,0:T(2,128)} %copy-done.2, f32[2,2,1632]{2,1,0:T(2,128)} %mean_ref.12, ...), custom_call_target="tpu_custom_call" | custom-call | tf_op jit(solution)/shard_map/depthwise/pallas_call | solution.py:161
  97.0 15.3 %all_to_all.61 = f32[16,2,1632]{2,1,0:T(2,128)S(1)} all-to-all(f32[16,2,1632]{2,1,0:T(2,128)} %get-tuple-element.23), channel_id=1, replica_groups=mesh['row'=16,'col'=16] {'row'}, dimensions={0} | all-to-all | bytes 417792 | tf_op jit(solution)/shard_map/all_to_all | solution.py:390
  113.1 3.5 %all-to-all-start.3 = ((f32[16,2,1632]{2,1,0:T(2,128)}), f32[16,2,1632]{2,1,0:T(2,128)S(1)}, u32[]{:S(2)}, u32[]{:S(2)}) async-start(f32[16,2,1632]{2,1,0:T(2,128)} %broadcast_in_dim.13), calls=%async_computation.3 | async-start | bytes 425984 | tf_op jit(solution)/shard_map/all_to_all | solution.py:393
  120.2 2.6 copy.24.wp_ref
  124.9 20.1 %lift_project.2 = (f32[2304,272]{1,0:T(8,128)}, f32[16,2,272]{2,1,0:T(2,128)}, f32[2,1632]{1,0:T(2,128)}) custom-call(f32[144,2,8,1632]{3,2,1,0:T(8,128)} %get-tuple-element.22.spread_ref, f32[16,2,1632]{2,1,0:T(2,128)} %copy-done.4, f32[2,2,1632]{2,1,0:T(2,128)} %mean_ref.12, f32[2,2,1632]{2,1,0:T(2,128)} %var_ref.10, f32[2,2,1632]{2,1,0:T(2,128)} %gain_ref.10, ...), custom_call_target="tpu_custom_call" | custom-call | tf_op jit(solution)/shard_map/lift_project/pallas_call | solution.py:286
  145.1 12.0 %all_to_all.62 = f32[16,2,272]{2,1,0:T(2,128)S(1)} all-to-all(f32[16,2,272]{2,1,0:T(2,128)} %get-tuple-element.25), channel_id=1, replica_groups=mesh['row'=16,'col'=16] {'row'}, dimensions={0} | all-to-all | bytes 69632 | tf_op jit(solution)/shard_map/all_to_all | solution.py:390
  157.1 10.5 %all_to_all.63.recv_ref = f32[16,2,272]{2,1,0:T(2,128)} all-to-all(f32[16,2,272]{2,1,0:T(2,128)S(1)} %broadcast_in_dim.14), channel_id=1, replica_groups=mesh['row'=16,'col'=16] {'col'}, dimensions={0} | all-to-all | bytes 69632 | tf_op jit(solution)/shard_map/all_to_all | solution.py:393
  167.7 16.3 %block_output.2 = (bf16[2304,272]{1,0:T(8,128)(2,1)}, f32[2,272]{1,0:T(2,128)}, f32[16,2,1632]{2,1,0:T(2,128)}) custom-call(bf16[2304,272]{1,0:T(8,128)(2,1)} %bitcast.26, f32[2304,272]{1,0:T(8,128)} %get-tuple-element.24.proj_ref, f32[16,2,272]{2,1,0:T(2,128)} %all_to_all.63.recv_ref, f32[2,272]{1,0:T(2,128)} %mean_ref.13, f32[2,272]{1,0:T(2,128)} %var_ref.11, ...), custom_call_target="tpu_custom_call" | custom-call | tf_op jit(solution)/shard_map/block_output/pallas_call | solution.py:377
  183.9 15.7 %all_to_all.64 = f32[16,2,1632]{2,1,0:T(2,128)S(1)} all-to-all(f32[16,2,1632]{2,1,0:T(2,128)} %get-tuple-element.27), channel_id=1, replica_groups=mesh['row'=16,'col'=16] {'row'}, dimensions={0} | all-to-all | bytes 417792 | tf_op jit(solution)/shard_map/all_to_all | solution.py:390
  199.8 11.3 %all_to_all.65.recv_ref = f32[16,2,1632]{2,1,0:T(2,128)} all-to-all(f32[16,2,1632]{2,1,0:T(2,128)S(1)} %broadcast_in_dim.15), channel_id=1, replica_groups=mesh['row'=16,'col'=16] {'col'}, dimensions={0} | all-to-all | bytes 417792 | tf_op jit(solution)/shard_map/all_to_all | solution.py:393
  211.1 46.1 %depthwise.3 = (f32[144,2,8,1632]{3,2,1,0:T(8,128)}, f32[16,2,1632]{2,1,0:T(2,128)}, f32[2,1632]{1,0:T(2,128)}) custom-call(bf16[2304,272]{1,0:T(8,128)(2,1)} %get-tuple-element.26.x_ref, bf16[2,272,1632]{2,1,0:T(8,128)(2,1)} %w_ref.5, f32[2,25,1632]{2,1,0:T(8,128)} %copy.21.dk_ref, f32[16,2,1632]{2,1,0:T(2,128)} %all_to_all.65.recv_ref, ...), custom_call_target="tpu_custom_call" | custom-call | tf_op jit(solution)/shard_map/depthwise/pallas_call | solution.py:161
  257.2 14.9 %all_to_all.66 = f32[16,2,1632]{2,1,0:T(2,128)S(1)} all-to-all(f32[16,2,1632]{2,1,0:T(2,128)} %get-tuple-element.29), channel_id=1, replica_groups=mesh['row'=16,'col'=16] {'row'}, dimensions={0} | all-to-all | bytes 417792 | tf_op jit(solution)/shard_map/all_to_all | solution.py:390
  272.9 3.5 %all-to-all-start.9 = ((f32[16,2,1632]{2,1,0:T(2,128)}), f32[16,2,1632]{2,1,0:T(2,128)S(1)}, u32[]{:S(2)}, u32[]{:S(2)}) async-start(f32[16,2,1632]{2,1,0:T(2,128)} %broadcast_in_dim.16), calls=%async_computation.9 | async-start | bytes 425984 | tf_op jit(solution)/shard_map/all_to_all | solution.py:393
  276.5 7.5 %all-to-all-done.9.recv_ref = f32[16,2,1632]{2,1,0:T(2,128)S(1)} async-done(((f32[16,2,1632]{2,1,0:T(2,128)}), f32[16,2,1632]{2,1,0:T(2,128)S(1)}, u32[]{:S(2)}, u32[]{:S(2)}) %all-to-all-start.9) | async-done | bytes 208928 | tf_op jit(solution)/shard_map/all_to_all | solution.py:393
  284.7 20.1 %lift_project.3 = (f32[2304,272]{1,0:T(8,128)}, f32[16,2,272]{2,1,0:T(2,128)}, f32[2,1632]{1,0:T(2,128)}) custom-call(f32[144,2,8,1632]{3,2,1,0:T(8,128)} %get-tuple-element.28.spread_ref, f32[16,2,1632]{2,1,0:T(2,128)} %copy-done.3, f32[2,2,1632]{2,1,0:T(2,128)} %mean_ref.12, f32[2,2,1632]{2,1,0:T(2,128)} %var_ref.10, f32[2,2,1632]{2,1,0:T(2,128)} %gain_ref.10, ...), custom_call_target="tpu_custom_call" | custom-call | tf_op jit(solution)/shard_map/lift_project/pallas_call | solution.py:286
  304.9 4.5 %all-to-all-start.10 = ((f32[16,2,272]{2,1,0:T(2,128)}), f32[16,2,272]{2,1,0:T(2,128)S(1)}, u32[]{:S(2)}, u32[]{:S(2)}) async-start(f32[16,2,272]{2,1,0:T(2,128)} %get-tuple-element.31), calls=%async_computation.10 | async-start | bytes 98304 | tf_op jit(solution)/shard_map/all_to_all | solution.py:390
  310.2 6.7 %all-to-all-done.10 = f32[16,2,272]{2,1,0:T(2,128)S(1)} async-done(((f32[16,2,272]{2,1,0:T(2,128)}), f32[16,2,272]{2,1,0:T(2,128)S(1)}, u32[]{:S(2)}, u32[]{:S(2)}) %all-to-all-start.10) | async-done | bytes 34848 | tf_op jit(solution)/shard_map/all_to_all | solution.py:390
  317.6 3.5 %all-to-all-start.11 = ((f32[16,2,272]{2,1,0:T(2,128)}), f32[16,2,272]{2,1,0:T(2,128)S(1)}, u32[]{:S(2)}, u32[]{:S(2)}) async-start(f32[16,2,272]{2,1,0:T(2,128)} %broadcast_in_dim.17), calls=%async_computation.11 | async-start | bytes 98304 | tf_op jit(solution)/shard_map/all_to_all | solution.py:393
  321.7 5.8 %all-to-all-done.11.recv_ref = f32[16,2,272]{2,1,0:T(2,128)S(1)} async-done(((f32[16,2,272]{2,1,0:T(2,128)}), f32[16,2,272]{2,1,0:T(2,128)S(1)}, u32[]{:S(2)}, u32[]{:S(2)}) %all-to-all-start.11) | async-done | bytes 34848 | tf_op jit(solution)/shard_map/all_to_all | solution.py:393
  328.1 4.6 %block_output.3 = (bf16[2304,272]{1,0:T(8,128)(2,1)}, f32[2,272]{1,0:T(2,128)}) custom-call(bf16[2304,272]{1,0:T(8,128)(2,1)} %get-tuple-element.26.x_ref, f32[2304,272]{1,0:T(8,128)} %get-tuple-element.30.proj_ref, f32[16,2,272]{2,1,0:T(2,128)} %copy-done.6, f32[2,272]{1,0:T(2,128)} %mean_ref.13, f32[2,272]{1,0:T(2,128)} %var_ref.11, f32[2,272]{1,0:T(2,128)} %gain_ref.11, ...), custom_call_target="tpu_custom_call" | custom-call | tf_op jit(solution)/shard_map/block_output/pallas_call | solution.py:377
  (44 shorter events, 14.5 us)
Async XLA Ops:
  0.6 41.9 %copy-start.5 = (f32[2,25,1632]{2,0,1:T(2,128)S(1)}, f32[2,25,1632]{2,0,1:T(2,128)}, u32[]{:S(2)}) copy-start(f32[2,25,1632]{2,0,1:T(2,128)} %param.18) | copy-start | bytes 979204
  35.8 14.4 %all-to-all-start.1 = ((f32[16,2,1632]{2,1,0:T(2,128)}), f32[16,2,1632]{2,1,0:T(2,128)S(1)}, u32[]{:S(2)}, u32[]{:S(2)}) async-start(f32[16,2,1632]{2,1,0:T(2,128)} %broadcast_in_dim.12), calls=%async_computation.1 | async-start | bytes 425984 | tf_op jit(solution)/shard_map/all_to_all | solution.py:393
  43.3 73.3 %copy-start.1 = (f32[2,68,1632]{2,0,1:T(2,128)S(1)}, f32[2,68,1632]{2,0,1:T(2,128)}, u32[]{:S(2)}) copy-start(f32[2,68,1632]{2,0,1:T(2,128)} %param.21) | copy-start | bytes 2663428
  50.2 0.7 copy-start.2
  113.1 11.1 %all-to-all-start.3 = ((f32[16,2,1632]{2,1,0:T(2,128)}), f32[16,2,1632]{2,1,0:T(2,128)S(1)}, u32[]{:S(2)}, u32[]{:S(2)}) async-start(f32[16,2,1632]{2,1,0:T(2,128)} %broadcast_in_dim.13), calls=%async_computation.3 | async-start | bytes 425984 | tf_op jit(solution)/shard_map/all_to_all | solution.py:393
  116.6 3.6 %copy-start = (bf16[2,1632,272]{1,2,0:T(8,128)(2,1)S(1)}, bf16[2,1632,272]{1,2,0:T(8,128)(2,1)}, u32[]{:S(2)}) copy-start(bf16[2,1632,272]{1,2,0:T(8,128)(2,1)} %param.23) | copy-start | bytes 5326852
  124.2 0.7 copy-start.4
  211.1 65.3 %copy-start.7 = (f32[2,1632]{1,0:T(2,128)S(1)}, f32[2,1632]{1,0:T(2,128)}, u32[]{:S(2)}) copy-start(f32[2,1632]{1,0:T(2,128)} %get-tuple-element.33) | copy-start | bytes 39172
  211.1 65.4 %copy-start.8 = (f32[2,1632]{1,0:T(2,128)S(1)}, f32[2,1632]{1,0:T(2,128)}, u32[]{:S(2)}) copy-start(f32[2,1632]{1,0:T(2,128)} %get-tuple-element.34) | copy-start | bytes 39172
  272.9 11.1 %all-to-all-start.9 = ((f32[16,2,1632]{2,1,0:T(2,128)}), f32[16,2,1632]{2,1,0:T(2,128)S(1)}, u32[]{:S(2)}, u32[]{:S(2)}) async-start(f32[16,2,1632]{2,1,0:T(2,128)} %broadcast_in_dim.16), calls=%async_computation.9 | async-start | bytes 425984 | tf_op jit(solution)/shard_map/all_to_all | solution.py:393
  284.0 0.7 copy-start.3
  284.7 24.7 %copy-start.9 = (f32[2,1632]{1,0:T(2,128)S(1)}, f32[2,1632]{1,0:T(2,128)}, u32[]{:S(2)}) copy-start(f32[2,1632]{1,0:T(2,128)} %get-tuple-element.35) | copy-start | bytes 39172
  304.9 12.0 %all-to-all-start.10 = ((f32[16,2,272]{2,1,0:T(2,128)}), f32[16,2,272]{2,1,0:T(2,128)S(1)}, u32[]{:S(2)}, u32[]{:S(2)}) async-start(f32[16,2,272]{2,1,0:T(2,128)} %get-tuple-element.31), calls=%async_computation.10 | async-start | bytes 98304 | tf_op jit(solution)/shard_map/all_to_all | solution.py:390
  317.6 9.9 %all-to-all-start.11 = ((f32[16,2,272]{2,1,0:T(2,128)}), f32[16,2,272]{2,1,0:T(2,128)S(1)}, u32[]{:S(2)}, u32[]{:S(2)}) async-start(f32[16,2,272]{2,1,0:T(2,128)} %broadcast_in_dim.17), calls=%async_computation.11 | async-start | bytes 98304 | tf_op jit(solution)/shard_map/all_to_all | solution.py:393
  327.5 0.6 copy-start.6
  328.1 4.6 %copy-start.10 = (f32[2,272]{1,0:T(2,128)S(1)}, f32[2,272]{1,0:T(2,128)}, u32[]{:S(2)}) copy-start(f32[2,272]{1,0:T(2,128)} %get-tuple-element.37) | copy-start | bytes 6532

commit v2 on v1

--- a/solution.py
+++ b/solution.py
@@ -48,24 +48,22 @@
     stat_ref[...] = jnp.broadcast_to(pair[None], (members,) + pair.shape)
 
 
-def expand_moments(x_ref, w_ref, mean, stat_ref, chunk):
-    rows = x_ref.shape[0]
-    weight = w_ref[0]
-
-    def step(i, carry):
-        first, second = carry
-        start = pl.multiple_of(i * chunk, chunk)
-        values = jnp.dot(x_ref[pl.ds(start, chunk), :], weight, preferred_element_type=jnp.float32)
+def expand_moments(x_ref, w_ref, mean, stat_ref, parts):
+    chunk = x_ref.shape[0] // parts
+    first = second = None
+    for part in range(parts):
+        values = jnp.dot(
+            x_ref[part * chunk : (part + 1) * chunk, :], w_ref[0], preferred_element_type=jnp.float32
+        )
         centered = values - mean
-        return first + fold_rows(centered), second + fold_rows(centered * centered)
-
-    zero = jnp.zeros((8, weight.shape[1]), jnp.float32)
-    first, second = lax.fori_loop(0, rows // chunk, step, (zero, zero))
+        one, two = fold_rows(centered), fold_rows(centered * centered)
+        first = one if first is None else first + one
+        second = two if second is None else second + two
     store_stats(stat_ref, first, second)
 
 
-def moments_kernel(x_ref, w_ref, mean_ref, stat_ref, *, chunk):
-    expand_moments(x_ref, w_ref, mean_ref[0, 0:1], stat_ref, chunk)
+def moments_kernel(x_ref, w_ref, mean_ref, stat_ref, *, parts):
+    expand_moments(x_ref, w_ref, mean_ref[0, 0:1], stat_ref, parts)
 
 
 def moments_call(x, expand_weight, mid_mean, layer, members):
@@ -73,7 +71,7 @@
     mid = expand_weight.shape[2]
     steps = pl.cdiv(mid, WIDE)
     return pl.pallas_call(
-        functools.partial(moments_kernel, chunk=rows // 6),
+        functools.partial(moments_kernel, parts=3),
         grid=(steps,),
         in_specs=[
             pl.BlockSpec((rows, out), lambda j: (0, 0)),
@@ -87,68 +85,59 @@
 
 
 def depth_kernel_body(
-    x_ref, w_ref, dk_ref, recv_ref, mean_ref, var_ref, gain_ref, bias_ref, mean2_ref,
-    spread_ref, stat_ref, new_ref, act_ref, *, row_count, side, chunk,
+    x_ref, w_ref, dk_ref, recv_ref, mean_ref, var_ref, gain_ref, bias_ref,
+    spread_ref, stat_ref, new_ref, act_ref, tap_ref, *, row_count, side, parts, tail,
 ):
     j = pl.program_id(0)
     rows = x_ref.shape[0]
     reach = KERN // 2
-
-    @pl.when(j % 2 == 0)
-    def _():
-        scale, shift, new_mean, new_var = coefficients(
-            recv_ref[...], row_count, mean_ref[0, 0:1], var_ref[0, 0:1], gain_ref[0, 0:1], bias_ref[0, 0:1]
-        )
-        new_ref[...] = jnp.concatenate([new_mean, new_var], axis=0)
-        scale = 0.5 * scale
-        shift = 0.5 * shift
-        weight = w_ref[0]
-        cells = chunk // 16
-
-        def step(i, carry):
-            start = pl.multiple_of(i * chunk, chunk)
-            values = jnp.dot(x_ref[pl.ds(start, chunk), :], weight, preferred_element_type=jnp.float32)
-            active = half_silu(values * scale + shift).astype(jnp.bfloat16).astype(jnp.float32)
-            active = active.reshape(cells, 2, 8, WIDE)
-            at = pl.multiple_of(i * cells, cells)
-            for s in range(2):
-                for b in range(2):
-                    act_ref[s, b, pl.ds(at, cells)] = active[:, b, :, s * LANE : (s + 1) * LANE]
-            return carry
-
-        lax.fori_loop(0, rows // chunk, step, 0)
-
-    mean2 = mean2_ref[0, 1:2]
-    s = j % 2
-
-    def half(b, carry):
-        first, second = carry
+    scale, shift, new_mean, new_var = coefficients(
+        recv_ref[...], row_count, mean_ref[0, 0:1], var_ref[0, 0:1], gain_ref[0, 0:1], bias_ref[0, 0:1]
+    )
+    new_ref[...] = jnp.concatenate([new_mean, new_var], axis=0)
+    scale = 0.5 * scale
+    shift = 0.5 * shift
+    chunk = rows // parts
+    cells = chunk // 16
+    for part in range(parts):
+        values = jnp.dot(
+            x_ref[part * chunk : (part + 1) * chunk, :], w_ref[0], preferred_element_type=jnp.float32
+        )
+        active = half_silu(values * scale + shift).astype(jnp.bfloat16).reshape(cells, 16, WIDE)
+        for s in range(2):
+            act_ref[s, part * cells : (part + 1) * cells] = active[:, :, s * LANE : (s + 1) * LANE]
+
+    def lanes(s):
+        here = slice(s * LANE, (s + 1) * LANE)
+        mean = mean_ref[0, 1:2, here]
+        for t in range(KERN * KERN):
+            tap_ref[s, t] = jnp.broadcast_to(dk_ref[0, t : t + 1, here], (16, LANE)).astype(jnp.bfloat16)
+        first = jnp.zeros((16, LANE), jnp.float32)
+        second = jnp.zeros((16, LANE), jnp.float32)
         for h in range(side):
-            acc = [None] * side
-            for i in range(KERN):
-                r = h + i - reach
-                if r < 0 or r >= side:
-                    continue
-                line = [act_ref[s, b, r * side + w] for w in range(side)]
-                for k in range(KERN):
-                    tap = dk_ref[0, i * KERN + k : i * KERN + k + 1, :]
-                    tap = jnp.broadcast_to(tap, (8, LANE))
-                    for w in range(side):
-                        p = w + k - reach
-                        if p < 0 or p >= side:
-                            continue
-                        term = line[p] * tap
-                        acc[w] = term if acc[w] is None else acc[w] + term
             for w in range(side):
-                spread_ref[h * side + w, b] = acc[w]
-                centered = acc[w] - mean2
+                acc = None
+                for i in range(KERN):
+                    for k in range(KERN):
+                        r, p = h + i - reach, w + k - reach
+                        if 0 <= r < side and 0 <= p < side:
+                            cell = act_ref[s, r * side + p].astype(jnp.float32)
+                            term = cell * tap_ref[s, i * KERN + k].astype(jnp.float32)
+                            acc = term if acc is None else acc + term
+                spread_ref[h * side + w, :, here] = acc
+                centered = acc - mean
                 first = first + centered
                 second = second + centered * centered
-        return first, second
-
-    zero = jnp.zeros((8, LANE), jnp.float32)
-    first, second = lax.fori_loop(0, 2, half, (zero, zero))
-    store_stats(stat_ref, first, second)
+        pair = jnp.concatenate(
+            [jnp.sum(first, axis=0, keepdims=True), jnp.sum(second, axis=0, keepdims=True)], axis=0
+        )
+        stat_ref[:, :, here] = jnp.broadcast_to(pair[None], (stat_ref.shape[0],) + pair.shape)
+
+    lanes(0)
+    if tail > LANE:
+        lanes(1)
+    else:
+        pl.when(j < pl.num_programs(0) - 1)(lambda: lanes(1))
 
 
 def depth_call(x, expand_weight, depth_kernel, received, mid_mean, mid_var, mid_gain, mid_bias, layer, side, row_count):
@@ -156,32 +145,36 @@
     mid = expand_weight.shape[2]
     members = received.shape[0]
     cells = side * side
-    steps = pl.cdiv(mid, LANE)
-    pair = pl.BlockSpec((1, 2, WIDE), lambda j: (layer, 0, j // 2))
+    steps = pl.cdiv(mid, WIDE)
+    pair = pl.BlockSpec((1, 2, WIDE), lambda j: (layer, 0, j))
     return pl.pallas_call(
-        functools.partial(depth_kernel_body, row_count=row_count, side=side, chunk=rows // 12),
+        functools.partial(
+            depth_kernel_body, row_count=row_count, side=side, parts=3, tail=mid - (steps - 1) * WIDE
+        ),
         grid=(steps,),
         in_specs=[
             pl.BlockSpec((rows, out), lambda j: (0, 0)),
-            pl.BlockSpec((1, out, WIDE), lambda j: (layer, 0, j // 2)),
-            pl.BlockSpec((1, KERN * KERN, LANE), lambda j: (layer, 0, j)),
-            pl.BlockSpec((members, 2, WIDE), lambda j: (0, 0, j // 2)),
+            pl.BlockSpec((1, out, WIDE), lambda j: (layer, 0, j)),
+            pl.BlockSpec((1, KERN * KERN, WIDE), lambda j: (layer, 0, j)),
+            pl.BlockSpec((members, 2, WIDE), lambda j: (0, 0, j)),
             pair, pair, pair, pair,
-            pl.BlockSpec((1, 2, LANE), lambda j: (layer, 0, j)),
         ],
         out_specs=[
-            pl.BlockSpec((cells, 2, 8, LANE), lambda j: (0, 0, 0, j)),
-            pl.BlockSpec((members, 2, LANE), lambda j: (0, 0, j)),
-            pl.BlockSpec((2, WIDE), lambda j: (0, j // 2)),
+            pl.BlockSpec((cells, 16, WIDE), lambda j: (0, 0, j)),
+            pl.BlockSpec((members, 2, WIDE), lambda j: (0, 0, j)),
+            pl.BlockSpec((2, WIDE), lambda j: (0, j)),
         ],
         out_shape=[
-            jax.ShapeDtypeStruct((cells, 2, 8, mid), jnp.float32),
+            jax.ShapeDtypeStruct((cells, 16, mid), jnp.float32),
             jax.ShapeDtypeStruct((members, 2, mid), jnp.float32),
             jax.ShapeDtypeStruct((2, mid), jnp.float32),
         ],
-        scratch_shapes=[pltpu.VMEM((2, 2, cells, 8, LANE), jnp.float32)],
+        scratch_shapes=[
+            pltpu.VMEM((2, cells, 16, LANE), jnp.bfloat16),
+            pltpu.VMEM((2, KERN * KERN, 16, LANE), jnp.bfloat16),
+        ],
         name="depthwise",
-    )(x, expand_weight, depth_kernel, received, mid_mean, mid_var, mid_gain, mid_bias, mid_mean)
+    )(x, expand_weight, depth_kernel, received, mid_mean, mid_var, mid_gain, mid_bias)
 
 
 def lift_kernel(
@@ -204,14 +197,14 @@
         shift = 0.5 * shift
 
         def step(i, pooled):
-            at = pl.multiple_of(i * 4, 4)
-            values = spread_ref[pl.ds(at, 4)]
+            at = pl.multiple_of(i * 16, 16)
+            values = spread_ref[pl.ds(at, 16)]
             lifted = half_silu(values * scale + shift)
-            lift_ref[j, pl.ds(at, 4)] = lifted
+            lift_ref[j, pl.ds(at, 16)] = lifted
             return pooled + jnp.sum(lifted, axis=0)
 
-        pooled = lax.fori_loop(0, cells // 4, step, jnp.zeros((2, 8, WIDE), jnp.float32))
-        pool_ref[j] = (pooled * (1.0 / cells)).reshape(16, WIDE)
+        pooled = lax.fori_loop(0, cells // 16, step, jnp.zeros((16, WIDE), jnp.float32))
+        pool_ref[j] = pooled * (1.0 / cells)
 
     @pl.when(j == blocks)
     def _():
@@ -230,7 +223,7 @@
                 squeezed, w2_ref[0, :, k * WIDE : k * WIDE + size],
                 precision=lax.Precision.HIGHEST, preferred_element_type=jnp.float32,
             ) + b2_ref[layer : layer + 1, k * WIDE : k * WIDE + size]
-            gate_ref[k, :, :, :size] = jax.nn.sigmoid(grown).reshape(2, 8, size)
+            gate_ref[k, :, :size] = jax.nn.sigmoid(grown)
 
     @pl.when(j >= blocks)
     def _():
@@ -239,16 +232,10 @@
         last = mid - (blocks - 1) * WIDE
         for k in range(blocks):
             size = WIDE if k < blocks - 1 else last
-            gate = gate_ref[k, :, :, :size]
-
-            def step(i, carry):
-                at = pl.multiple_of(i * 4, 4)
-                lifted = lift_ref[k, pl.ds(base + at, 4), :, :, :size]
-                scaled = (lifted * gate).reshape(64, size).astype(jnp.bfloat16)
-                scaled_ref[pl.ds(pl.multiple_of(i * 64, 64), 64), k * WIDE : k * WIDE + size] = scaled
-                return carry
-
-            lax.fori_loop(0, group // 4, step, 0)
+            gate = gate_ref[k, :, :size]
+            lifted = lift_ref[k, pl.ds(base, group), :, :size]
+            scaled = (lifted * gate).reshape(group * 16, size).astype(jnp.bfloat16)
+            scaled_ref[:, k * WIDE : k * WIDE + size] = scaled
         projected = jnp.dot(scaled_ref[...], wp_ref[0], preferred_element_type=jnp.float32)
         proj_ref[...] = projected
         centered = projected - mean3_ref[layer : layer + 1, :]
@@ -274,7 +261,7 @@
     spread, received, mid_mean, mid_var, mid_gain, mid_bias,
     squeeze_weight, squeeze_bias, excite_weight, excite_bias, project_weight, out_mean, layer, row_count,
 ):
-    cells, _, _, mid = spread.shape
+    cells, _, mid = spread.shape
     members = received.shape[0]
     out = project_weight.shape[2]
     squeeze = squeeze_weight.shape[2]
@@ -289,7 +276,7 @@
         ),
         grid=(blocks + parts,),
         in_specs=[
-            pl.BlockSpec((cells, 2, 8, WIDE), lambda j: (0, 0, 0, here(j))),
+            pl.BlockSpec((cells, 16, WIDE), lambda j: (0, 0, here(j))),
             pl.BlockSpec((members, 2, WIDE), lambda j: (0, 0, here(j))),
             pair, pair, pair, pair,
             pl.BlockSpec((1, mid, squeeze), lambda j: (layer, 0, 0)),
@@ -310,9 +297,9 @@
             jax.ShapeDtypeStruct((2, mid), jnp.float32),
         ],
         scratch_shapes=[
-            pltpu.VMEM((blocks, cells, 2, 8, WIDE), jnp.float32),
+            pltpu.VMEM((blocks, cells, 16, WIDE), jnp.float32),
             pltpu.VMEM((blocks, 16, WIDE), jnp.float32),
-            pltpu.VMEM((blocks, 2, 8, WIDE), jnp.float32),
+            pltpu.VMEM((blocks, 16, WIDE), jnp.float32),
             pltpu.VMEM((rows // parts, mid), jnp.bfloat16),
             pltpu.VMEM((2, 8, out), jnp.float32),
         ],
@@ -324,7 +311,7 @@
 
 
 def output_kernel(
-    x_ref, proj_ref, recv_ref, mean_ref, var_ref, gain_ref, bias_ref, *rest, row_count, layer, chunk, follow
+    x_ref, proj_ref, recv_ref, mean_ref, var_ref, gain_ref, bias_ref, *rest, row_count, layer, parts, follow
 ):
     if follow:
         w_ref, mid_mean_ref, next_ref, new_ref, stat_ref = rest
@@ -339,16 +326,16 @@
         new_ref[...] = jnp.concatenate([new_mean, new_var], axis=0)
 
         def step(i, carry):
-            here = pl.ds(pl.multiple_of(i * 64, 64), 64)
+            here = pl.ds(pl.multiple_of(i * 128, 128), 128)
             total = x_ref[here, :].astype(jnp.float32) + proj_ref[here, :] * scale + shift
             next_ref[here, :] = total.astype(jnp.bfloat16)
             return carry
 
-        lax.fori_loop(0, x_ref.shape[0] // 64, step, 0)
+        lax.fori_loop(0, x_ref.shape[0] // 128, step, 0)
 
     if follow:
         pl.when(pl.program_id(0) == 0)(produce)
-        expand_moments(next_ref, w_ref, mid_mean_ref[0, 0:1], stat_ref, chunk)
+        expand_moments(next_ref, w_ref, mid_mean_ref[0, 0:1], stat_ref, parts)
     else:
         produce()
 
@@ -376,7 +363,7 @@
         operands += [expand_weight, mid_mean]
     return pl.pallas_call(
         functools.partial(
-            output_kernel, row_count=row_count, layer=layer, chunk=rows // 6, follow=follow is not None
+            output_kernel, row_count=row_count, layer=layer, parts=3, follow=follow is not None
         ),
         grid=(steps,),
         in_specs=in_specs,

time: 335 us -> 260 us (0.78)
  Pallas kernels: 167 us -> 91.4 us
    pallas_call x2, Pallas kernels: 92.2 us -> 34.7 us  [depth_call(): pl.pallas_call(functools.partial(depth_kernel_body, row_count=row_count,...]
    pallas_call x2, Pallas kernels: 20.9 us -> 14.5 us  [output_call(): pl.pallas_call(functools.partial(output_kernel, row_count=row_count, laye...]
    pallas_call x2, Pallas kernels: 40.3 us -> 34 us  [lift_call(): pl.pallas_call(functools.partial(lift_kernel, row_count=row_count, blocks...]
    pallas_call x1, Pallas kernels: 13.8 us -> 8.2 us  [moments_call(): pl.pallas_call(functools.partial(moments_kernel, parts=3), grid=(steps,),...]
where the time goes in v2:
time: 260 us; the launch traced here: 258 us
  blocking collectives  100 us (38%)
  Pallas kernels  91.4 us (35%)
  waiting for transfers between devices  28.3 us (11%)
  starting transfers between devices  21.8 us (8%)
  local copies, waits for them, and re-layouts  13.9 us (5%)
    all_to_all x5, blocking collectives, exchange(): sums = lax.all_to_all(stats, 'row', split_axis=0, concat_axis=0, tiled=True)  78.6 us
    pallas_call x2, Pallas kernels, depth_call(): pl.pallas_call(functools.partial(depth_kernel_body, row_count=row_count,...  34.7 us
    pallas_call x2, Pallas kernels, lift_call(): pl.pallas_call(functools.partial(lift_kernel, row_count=row_count, blocks...  34 us
    all_to_all x2, blocking collectives, exchange(): lax.all_to_all(copies, 'col', split_axis=0, concat_axis=0, tiled=True)  21.8 us
    all_to_all x4, waiting for transfers between devices, exchange(): lax.all_to_all(copies, 'col', split_axis=0, concat_axis=0, tiled=True)  21.5 us
    all_to_all x4, starting transfers between devices, exchange(): lax.all_to_all(copies, 'col', split_axis=0, concat_axis=0, tiled=True)  17.3 us
    pallas_call x2, Pallas kernels, output_call(): pl.pallas_call(functools.partial(output_kernel, row_count=row_count, laye...  14.5 us
    unnamed x28, local copies, waits for them, and re-layouts  10.9 us
  transfers between devices with their start and end apart: 5, of which 5 were waited for; matrix products, arithmetic and copies ran while one was open for 3% of the time, Pallas kernels for 0%

profile of v2, /device:TPU:1, one launch (start us, length us, event | category | flops | bytes accessed | tf_op | source)
XLA Modules:
  0.0 258.5 jit_solution(5217250836152455411)
XLA Ops:
  0.6 8.2 %expand_moments.1 = f32[16,2,1632]{2,1,0:T(2,128)} custom-call(bf16[2304,272]{1,0:T(8,128)(2,1)} %bitcast.24, bf16[2,272,1632]{2,1,0:T(8,128)(2,1)} %w_ref.5, f32[2,2,1632]{2,1,0:T(2,128)} %mean_ref.12), custom_call_target="tpu_custom_call" | custom-call | tf_op jit(solution)/shard_map/expand_moments/pallas_call | solution.py:73
  8.8 20.5 %all_to_all.60 = f32[16,2,1632]{2,1,0:T(2,128)S(1)} all-to-all(f32[16,2,1632]{2,1,0:T(2,128)} %expand_moments.1), channel_id=1, replica_groups=mesh['row'=16,'col'=16] {'row'}, dimensions={0} | all-to-all | bytes 417792 | tf_op jit(solution)/shard_map/all_to_all | solution.py:377
  30.2 6.8 %all-to-all-start.1 = ((f32[16,2,1632]{2,1,0:T(2,128)}), f32[16,2,1632]{2,1,0:T(2,128)S(1)}, u32[]{:S(2)}, u32[]{:S(2)}) async-start(f32[16,2,1632]{2,1,0:T(2,128)} %broadcast_in_dim.12), calls=%async_computation.1 | async-start | bytes 425984 | tf_op jit(solution)/shard_map/all_to_all | solution.py:380
  37.7 6.9 %all-to-all-done.1.recv_ref = f32[16,2,1632]{2,1,0:T(2,128)S(1)} async-done(((f32[16,2,1632]{2,1,0:T(2,128)}), f32[16,2,1632]{2,1,0:T(2,128)S(1)}, u32[]{:S(2)}, u32[]{:S(2)}) %all-to-all-start.1) | async-done | bytes 208928 | tf_op jit(solution)/shard_map/all_to_all | solution.py:380
  45.3 17.4 %depthwise.2 = (f32[144,16,1632]{2,1,0:T(8,128)}, f32[16,2,1632]{2,1,0:T(2,128)}, f32[2,1632]{1,0:T(2,128)}) custom-call(bf16[2304,272]{1,0:T(8,128)(2,1)} %bitcast.25, bf16[2,272,1632]{2,1,0:T(8,128)(2,1)} %w_ref.5, f32[2,25,1632]{2,1,0:T(8,128)} %copy.21.dk_ref, f32[16,2,1632]{2,1,0:T(2,128)} %copy-done.2, f32[2,2,1632]{2,1,0:T(2,128)} %mean_ref.12, ...), custom_call_target="tpu_custom_call" | custom-call | tf_op jit(solution)/shard_map/depthwise/pallas_call | solution.py:150
  62.6 15.3 %all_to_all.61 = f32[16,2,1632]{2,1,0:T(2,128)S(1)} all-to-all(f32[16,2,1632]{2,1,0:T(2,128)} %get-tuple-element.23), channel_id=1, replica_groups=mesh['row'=16,'col'=16] {'row'}, dimensions={0} | all-to-all | bytes 417792 | tf_op jit(solution)/shard_map/all_to_all | solution.py:377
  78.7 3.5 %all-to-all-start.3 = ((f32[16,2,1632]{2,1,0:T(2,128)}), f32[16,2,1632]{2,1,0:T(2,128)S(1)}, u32[]{:S(2)}, u32[]{:S(2)}) async-start(f32[16,2,1632]{2,1,0:T(2,128)} %broadcast_in_dim.13), calls=%async_computation.3 | async-start | bytes 425984 | tf_op jit(solution)/shard_map/all_to_all | solution.py:380
  85.9 2.6 %copy.24.wp_ref = bf16[2,1632,272]{2,1,0:T(8,128)(2,1)} copy(bf16[2,1632,272]{1,2,0:T(8,128)(2,1)S(1)} %copy-done) | data formatting | bytes 3551232 | tf_op args[7]
  90.6 17.0 %lift_project.2 = (f32[2304,272]{1,0:T(8,128)}, f32[16,2,272]{2,1,0:T(2,128)}, f32[2,1632]{1,0:T(2,128)}) custom-call(f32[144,16,1632]{2,1,0:T(8,128)} %get-tuple-element.22.spread_ref, f32[16,2,1632]{2,1,0:T(2,128)} %copy-done.4, f32[2,2,1632]{2,1,0:T(2,128)} %mean_ref.12, f32[2,2,1632]{2,1,0:T(2,128)} %var_ref.10, f32[2,2,1632]{2,1,0:T(2,128)} %gain_ref.10, ...), custom_call_target="tpu_custom_call" | custom-call | tf_op jit(solution)/shard_map/lift_project/pallas_call | solution.py:273
  107.6 12.0 %all_to_all.62 = f32[16,2,272]{2,1,0:T(2,128)S(1)} all-to-all(f32[16,2,272]{2,1,0:T(2,128)} %get-tuple-element.25), channel_id=1, replica_groups=mesh['row'=16,'col'=16] {'row'}, dimensions={0} | all-to-all | bytes 69632 | tf_op jit(solution)/shard_map/all_to_all | solution.py:377
  119.6 10.5 %all_to_all.63.recv_ref = f32[16,2,272]{2,1,0:T(2,128)} all-to-all(f32[16,2,272]{2,1,0:T(2,128)S(1)} %broadcast_in_dim.14), channel_id=1, replica_groups=mesh['row'=16,'col'=16] {'col'}, dimensions={0} | all-to-all | bytes 69632 | tf_op jit(solution)/shard_map/all_to_all | solution.py:380
  130.1 10.0 %block_output.2 = (bf16[2304,272]{1,0:T(8,128)(2,1)}, f32[2,272]{1,0:T(2,128)}, f32[16,2,1632]{2,1,0:T(2,128)}) custom-call(bf16[2304,272]{1,0:T(8,128)(2,1)} %bitcast.26, f32[2304,272]{1,0:T(8,128)} %get-tuple-element.24.proj_ref, f32[16,2,272]{2,1,0:T(2,128)} %all_to_all.63.recv_ref, f32[2,272]{1,0:T(2,128)} %mean_ref.13, f32[2,272]{1,0:T(2,128)} %var_ref.11, ...), custom_call_target="tpu_custom_call" | custom-call | tf_op jit(solution)/shard_map/block_output/pallas_call | solution.py:364
  140.1 15.7 %all_to_all.64 = f32[16,2,1632]{2,1,0:T(2,128)S(1)} all-to-all(f32[16,2,1632]{2,1,0:T(2,128)} %get-tuple-element.27), channel_id=1, replica_groups=mesh['row'=16,'col'=16] {'row'}, dimensions={0} | all-to-all | bytes 417792 | tf_op jit(solution)/shard_map/all_to_all | solution.py:377
  156.0 11.3 %all_to_all.65.recv_ref = f32[16,2,1632]{2,1,0:T(2,128)} all-to-all(f32[16,2,1632]{2,1,0:T(2,128)S(1)} %broadcast_in_dim.15), channel_id=1, replica_groups=mesh['row'=16,'col'=16] {'col'}, dimensions={0} | all-to-all | bytes 417792 | tf_op jit(solution)/shard_map/all_to_all | solution.py:380
  167.3 17.4 %depthwise.3 = (f32[144,16,1632]{2,1,0:T(8,128)}, f32[16,2,1632]{2,1,0:T(2,128)}, f32[2,1632]{1,0:T(2,128)}) custom-call(bf16[2304,272]{1,0:T(8,128)(2,1)} %get-tuple-element.26.x_ref, bf16[2,272,1632]{2,1,0:T(8,128)(2,1)} %w_ref.5, f32[2,25,1632]{2,1,0:T(8,128)} %copy.21.dk_ref, f32[16,2,1632]{2,1,0:T(2,128)} %all_to_all.65.recv_ref, ...), custom_call_target="tpu_custom_call" | custom-call | tf_op jit(solution)/shard_map/depthwise/pallas_call | solution.py:150
  184.6 15.1 %all_to_all.66 = f32[16,2,1632]{2,1,0:T(2,128)S(1)} all-to-all(f32[16,2,1632]{2,1,0:T(2,128)} %get-tuple-element.29), channel_id=1, replica_groups=mesh['row'=16,'col'=16] {'row'}, dimensions={0} | all-to-all | bytes 417792 | tf_op jit(solution)/shard_map/all_to_all | solution.py:377
  200.5 3.5 %all-to-all-start.9 = ((f32[16,2,1632]{2,1,0:T(2,128)}), f32[16,2,1632]{2,1,0:T(2,128)S(1)}, u32[]{:S(2)}, u32[]{:S(2)}) async-start(f32[16,2,1632]{2,1,0:T(2,128)} %broadcast_in_dim.16), calls=%async_computation.9 | async-start | bytes 425984 | tf_op jit(solution)/shard_map/all_to_all | solution.py:380
  204.1 7.6 %all-to-all-done.9.recv_ref = f32[16,2,1632]{2,1,0:T(2,128)S(1)} async-done(((f32[16,2,1632]{2,1,0:T(2,128)}), f32[16,2,1632]{2,1,0:T(2,128)S(1)}, u32[]{:S(2)}, u32[]{:S(2)}) %all-to-all-start.9) | async-done | bytes 208928 | tf_op jit(solution)/shard_map/all_to_all | solution.py:380
  212.3 17.0 %lift_project.3 = (f32[2304,272]{1,0:T(8,128)}, f32[16,2,272]{2,1,0:T(2,128)}, f32[2,1632]{1,0:T(2,128)}) custom-call(f32[144,16,1632]{2,1,0:T(8,128)} %get-tuple-element.28.spread_ref, f32[16,2,1632]{2,1,0:T(2,128)} %copy-done.3, f32[2,2,1632]{2,1,0:T(2,128)} %mean_ref.12, f32[2,2,1632]{2,1,0:T(2,128)} %var_ref.10, f32[2,2,1632]{2,1,0:T(2,128)} %gain_ref.10, ...), custom_call_target="tpu_custom_call" | custom-call | tf_op jit(solution)/shard_map/lift_project/pallas_call | solution.py:273
  229.4 4.5 %all-to-all-start.10 = ((f32[16,2,272]{2,1,0:T(2,128)}), f32[16,2,272]{2,1,0:T(2,128)S(1)}, u32[]{:S(2)}, u32[]{:S(2)}) async-start(f32[16,2,272]{2,1,0:T(2,128)} %get-tuple-element.31), calls=%async_computation.10 | async-start | bytes 98304 | tf_op jit(solution)/shard_map/all_to_all | solution.py:377
  234.7 6.7 %all-to-all-done.10 = f32[16,2,272]{2,1,0:T(2,128)S(1)} async-done(((f32[16,2,272]{2,1,0:T(2,128)}), f32[16,2,272]{2,1,0:T(2,128)S(1)}, u32[]{:S(2)}, u32[]{:S(2)}) %all-to-all-start.10) | async-done | bytes 34848 | tf_op jit(solution)/shard_map/all_to_all | solution.py:377
  242.1 3.5 %all-to-all-start.11 = ((f32[16,2,272]{2,1,0:T(2,128)}), f32[16,2,272]{2,1,0:T(2,128)S(1)}, u32[]{:S(2)}, u32[]{:S(2)}) async-start(f32[16,2,272]{2,1,0:T(2,128)} %broadcast_in_dim.17), calls=%async_computation.11 | async-start | bytes 98304 | tf_op jit(solution)/shard_map/all_to_all | solution.py:380
  246.2 5.8 %all-to-all-done.11.recv_ref = f32[16,2,272]{2,1,0:T(2,128)S(1)} async-done(((f32[16,2,272]{2,1,0:T(2,128)}), f32[16,2,272]{2,1,0:T(2,128)S(1)}, u32[]{:S(2)}, u32[]{:S(2)}) %all-to-all-start.11) | async-done | bytes 34848 | tf_op jit(solution)/shard_map/all_to_all | solution.py:380
  252.6 4.5 %block_output.3 = (bf16[2304,272]{1,0:T(8,128)(2,1)}, f32[2,272]{1,0:T(2,128)}) custom-call(bf16[2304,272]{1,0:T(8,128)(2,1)} %get-tuple-element.26.x_ref, f32[2304,272]{1,0:T(8,128)} %get-tuple-element.30.proj_ref, f32[16,2,272]{2,1,0:T(2,128)} %copy-done.6, f32[2,272]{1,0:T(2,128)} %mean_ref.13, f32[2,272]{1,0:T(2,128)} %var_ref.11, f32[2,272]{1,0:T(2,128)} %gain_ref.11, ...), custom_call_target="tpu_custom_call" | custom-call | tf_op jit(solution)/shard_map/block_output/pallas_call | solution.py:364
  (44 shorter events, 14.5 us)
Async XLA Ops:
  0.6 36.3 %copy-start.5 = (f32[2,25,1632]{2,0,1:T(2,128)S(1)}, f32[2,25,1632]{2,0,1:T(2,128)}, u32[]{:S(2)}) copy-start(f32[2,25,1632]{2,0,1:T(2,128)} %param.18) | copy-start | bytes 979204
  30.2 14.4 %all-to-all-start.1 = ((f32[16,2,1632]{2,1,0:T(2,128)}), f32[16,2,1632]{2,1,0:T(2,128)S(1)}, u32[]{:S(2)}, u32[]{:S(2)}) async-start(f32[16,2,1632]{2,1,0:T(2,128)} %broadcast_in_dim.12), calls=%async_computation.1 | async-start | bytes 425984 | tf_op jit(solution)/shard_map/all_to_all | solution.py:380
  37.7 44.5 %copy-start.1 = (f32[2,68,1632]{2,0,1:T(2,128)S(1)}, f32[2,68,1632]{2,0,1:T(2,128)}, u32[]{:S(2)}) copy-start(f32[2,68,1632]{2,0,1:T(2,128)} %param.21) | copy-start | bytes 2663428
  44.6 0.7 copy-start.2
  78.7 11.1 %all-to-all-start.3 = ((f32[16,2,1632]{2,1,0:T(2,128)}), f32[16,2,1632]{2,1,0:T(2,128)S(1)}, u32[]{:S(2)}, u32[]{:S(2)}) async-start(f32[16,2,1632]{2,1,0:T(2,128)} %broadcast_in_dim.13), calls=%async_computation.3 | async-start | bytes 425984 | tf_op jit(solution)/shard_map/all_to_all | solution.py:380
  82.3 3.6 %copy-start = (bf16[2,1632,272]{1,2,0:T(8,128)(2,1)S(1)}, bf16[2,1632,272]{1,2,0:T(8,128)(2,1)}, u32[]{:S(2)}) copy-start(bf16[2,1632,272]{1,2,0:T(8,128)(2,1)} %param.23) | copy-start | bytes 5326852
  89.9 0.7 copy-start.4
  167.3 36.8 %copy-start.7 = (f32[2,1632]{1,0:T(2,128)S(1)}, f32[2,1632]{1,0:T(2,128)}, u32[]{:S(2)}) copy-start(f32[2,1632]{1,0:T(2,128)} %get-tuple-element.33) | copy-start | bytes 39172
  167.3 36.8 %copy-start.8 = (f32[2,1632]{1,0:T(2,128)S(1)}, f32[2,1632]{1,0:T(2,128)}, u32[]{:S(2)}) copy-start(f32[2,1632]{1,0:T(2,128)} %get-tuple-element.34) | copy-start | bytes 39172
  200.5 11.1 %all-to-all-start.9 = ((f32[16,2,1632]{2,1,0:T(2,128)}), f32[16,2,1632]{2,1,0:T(2,128)S(1)}, u32[]{:S(2)}, u32[]{:S(2)}) async-start(f32[16,2,1632]{2,1,0:T(2,128)} %broadcast_in_dim.16), calls=%async_computation.9 | async-start | bytes 425984 | tf_op jit(solution)/shard_map/all_to_all | solution.py:380
  211.7 0.7 copy-start.3
  212.3 21.5 %copy-start.9 = (f32[2,1632]{1,0:T(2,128)S(1)}, f32[2,1632]{1,0:T(2,128)}, u32[]{:S(2)}) copy-start(f32[2,1632]{1,0:T(2,128)} %get-tuple-element.35) | copy-start | bytes 39172
  229.4 12.0 %all-to-all-start.10 = ((f32[16,2,272]{2,1,0:T(2,128)}), f32[16,2,272]{2,1,0:T(2,128)S(1)}, u32[]{:S(2)}, u32[]{:S(2)}) async-start(f32[16,2,272]{2,1,0:T(2,128)} %get-tuple-element.31), calls=%async_computation.10 | async-start | bytes 98304 | tf_op jit(solution)/shard_map/all_to_all | solution.py:377
  242.1 9.9 %all-to-all-start.11 = ((f32[16,2,272]{2,1,0:T(2,128)}), f32[16,2,272]{2,1,0:T(2,128)S(1)}, u32[]{:S(2)}, u32[]{:S(2)}) async-start(f32[16,2,272]{2,1,0:T(2,128)} %broadcast_in_dim.17), calls=%async_computation.11 | async-start | bytes 98304 | tf_op jit(solution)/shard_map/all_to_all | solution.py:380
  252.0 0.6 copy-start.6
  252.6 4.5 %copy-start.10 = (f32[2,272]{1,0:T(2,128)S(1)}, f32[2,272]{1,0:T(2,128)}, u32[]{:S(2)}) copy-start(f32[2,272]{1,0:T(2,128)} %get-tuple-element.37) | copy-start | bytes 6532

commit v3 on v0

v3 whole, which is shorter than its diff:
```python
import functools
import jax
import jax.numpy as jnp
from jax import lax
from jax.experimental import pallas as pl
from jax.experimental.pallas import tpu as pltpu
from jax.sharding import PartitionSpec as P

KERN = 5
LAYERS = 2
EPSILON = 0.001
RATIO_MAX = 3.0
SHIFT_MAX = 5.0
MOMENTUM = 0.01
LANE = 128
WIDE = 256
MIB = 1 << 20


def coefficients(sums, row_count, run_mean, run_var, gain, bias):
    offset = sums[0] / row_count
    batch_var = sums[1] / row_count - offset * offset
    batch_mean = run_mean + offset
    batch_sigma = jnp.sqrt(batch_var + EPSILON)
    run_sigma = jnp.sqrt(run_var + EPSILON)
    scale_ratio = jnp.clip(batch_sigma / run_sigma, 1.0 / RATIO_MAX, RATIO_MAX)
    shift_clip = jnp.clip(offset / run_sigma, -SHIFT_MAX, SHIFT_MAX)
    gain_scale = gain * scale_ratio / batch_sigma
    gain_shift = bias + gain * shift_clip - batch_mean * gain_scale
    new_mean = run_mean + MOMENTUM * offset
    new_var = run_var + MOMENTUM * (batch_var - run_var)
    return jnp.stack([gain_scale, gain_shift]), new_mean, new_var


def half_silu(half):
    return half + half * jnp.tanh(half)


def fold_rows(block):
    return jnp.sum(block.reshape(block.shape[0] // 8, 8, block.shape[1]), axis=0)


def stat_copies(first, second, members):
    pair = jnp.concatenate(
        [jnp.sum(first, axis=0, keepdims=True), jnp.sum(second, axis=0, keepdims=True)], axis=0
    )
    return jnp.broadcast_to(pair[None], (members,) + pair.shape)


def call(kernel, name, out_shape, scratch, limit, *operands):
    return pl.pallas_call(
        kernel,
        in_specs=[pl.BlockSpec(memory_space=pltpu.VMEM)] * len(operands),
        out_specs=[pl.BlockSpec(memory_space=pltpu.VMEM)] * len(out_shape),
        out_shape=out_shape,
        scratch_shapes=scratch,
        compiler_params=pltpu.CompilerParams(vmem_limit_bytes=limit * MIB),
        name=name,
    )(*operands)


def expand_moments(x_ref, w_ref, mean_ref, stat_ref, layer, parts):
    rows = x_ref.shape[0]
    mid = w_ref.shape[2]
    chunk = rows // parts

    def lanes(here):
        mean = mean_ref[layer, 0:1, here]
        first = second = None
        for part in range(parts):
            values = jnp.dot(
                x_ref[part * chunk : (part + 1) * chunk, :], w_ref[layer, :, here],
                preferred_element_type=jnp.float32,
            )
            centered = values - mean
            one, two = fold_rows(centered), fold_rows(centered * centered)
            first = one if first is None else first + one
            second = two if second is None else second + two
        stat_ref[:, :, here] = stat_copies(first, second, stat_ref.shape[0])

    def step(j, carry):
        lanes(pl.ds(pl.multiple_of(j * WIDE, WIDE), WIDE))
        return carry

    full = mid // WIDE
    lax.fori_loop(0, full, step, 0)
    if mid > full * WIDE:
        lanes(slice(full * WIDE, mid))


def moments_kernel(x_ref, w_ref, mean_ref, stat_ref, *, layer, parts):
    expand_moments(x_ref, w_ref, mean_ref, stat_ref, layer, parts)


def moments_call(x, expand_weight, mid_mean, layer, members):
    mid = expand_weight.shape[2]
    return call(
        functools.partial(moments_kernel, layer=layer, parts=3),
        "expand_moments",
        [jax.ShapeDtypeStruct((members, 2, mid), jnp.float32)],
        [], 24, x, expand_weight, mid_mean,
    )[0]


def depth_kernel_body(
    x_ref, w_ref, dk_ref, coef_ref, mean_ref, spread_ref, stat_ref, act_ref, tap_ref, *, layer, side, parts
):
    rows = x_ref.shape[0]
    mid = stat_ref.shape[2]
    blocks = spread_ref.shape[0]
    reach = KERN // 2
    chunk = rows // parts
    cells = chunk // 16

    def activate(start, width):
        here = pl.ds(start, width)
        scale = 0.5 * coef_ref[0:1, here]
        shift = 0.5 * coef_ref[1:2, here]
        for part in range(parts):
            values = jnp.dot(
                x_ref[part * chunk : (part + 1) * chunk, :], w_ref[layer, :, here],
                preferred_element_type=jnp.float32,
            )
            active = half_silu(values * scale + shift).astype(jnp.bfloat16).reshape(cells, 16, width)
            for s in range(width // LANE):
                act_ref[s, part * cells : (part + 1) * cells] = active[:, :, s * LANE : (s + 1) * LANE]

    def spread_block(s, block, start, size):
        here = pl.ds(start, LANE)
        mean = mean_ref[layer, 1:2, here]
        for t in range(KERN * KERN):
            tap_ref[s, t] = jnp.broadcast_to(dk_ref[layer, t : t + 1, here], (16, LANE)).astype(jnp.bfloat16)
        first = jnp.zeros((16, LANE), jnp.float32)
        second = jnp.zeros((16, LANE), jnp.float32)
        for h in range(side):
            for w in range(side):
                acc = None
                for i in range(KERN):
                    for k in range(KERN):
                        r, p = h + i - reach, w + k - reach
                        if 0 <= r < side and 0 <= p < side:
                            cell = act_ref[s, r * side + p].astype(jnp.float32)
                            term = cell * tap_ref[s, i * KERN + k].astype(jnp.float32)
                            acc = term if acc is None else acc + term
                spread_ref[block, h * side + w] = acc
                centered = acc - mean
                first = first + centered
                second = second + centered * centered
        copies = stat_copies(first, second, stat_ref.shape[0])
        stat_ref[:, :, pl.ds(start, size)] = copies[:, :, :size]

    def step(j, carry):
        start = pl.multiple_of(j * WIDE, WIDE)
        activate(start, WIDE)
        spread_block(0, 2 * j, start, LANE)
        spread_block(1, 2 * j + 1, pl.multiple_of(start + LANE, LANE), LANE)
        return carry

    lax.fori_loop(0, blocks // 2, step, 0)
    if blocks % 2:
        start = (blocks - 1) * LANE
        activate(start, LANE)
        spread_block(0, blocks - 1, start, mid - start)


def depth_call(x, expand_padded, kernel_padded, coef, mean_padded, mid, members, layer, side):
    blocks = expand_padded.shape[2] // LANE
    cells = side * side
    return call(
        functools.partial(depth_kernel_body, layer=layer, side=side, parts=3),
        "depthwise",
        [
            jax.ShapeDtypeStruct((blocks, cells, 16, LANE), jnp.float32),
            jax.ShapeDtypeStruct((members, 2, mid), jnp.float32),
        ],
        [
            pltpu.VMEM((2, cells, 16, LANE), jnp.bfloat16),
            pltpu.VMEM((2, KERN * KERN, 16, LANE), jnp.bfloat16),
        ],
        28, x, expand_padded, kernel_padded, coef, mean_padded,
    )


def lift_kernel(
    spread_ref, coef_ref, w1_ref, b1_ref, w2_ref, b2_ref, wp_ref, mean3_ref, proj_ref, stat_ref,
    lift_ref, pool_ref, gate_ref, scaled_ref, *, layer, parts,
):
    blocks, cells = spread_ref.shape[0], spread_ref.shape[1]
    mid = w1_ref.shape[1]
    at = slice(layer, layer + 1)
    batch = 24

    def block_step(j, carry):
        here = pl.ds(pl.multiple_of(j * LANE, LANE), LANE)
        scale = 0.5 * coef_ref[0:1, here]
        shift = 0.5 * coef_ref[1:2, here]

        def step(i, pooled):
            cell = pl.multiple_of(i * batch, batch)
            lifted = half_silu(spread_ref[j, pl.ds(cell, batch)] * scale + shift)
            lift_ref[j, pl.ds(cell, batch)] = lifted
            return pooled + jnp.sum(lifted, axis=0)

        pooled = lax.fori_loop(0, cells // batch, step, jnp.zeros((16, LANE), jnp.float32))
        pool_ref[:, here] = pooled * (1.0 / cells)
        return carry

    lax.fori_loop(0, blocks, block_step, 0)

    squeezed = b1_ref[at, :] + jnp.dot(
        pool_ref[:, :mid], w1_ref[layer], precision=lax.Precision.HIGHEST, preferred_element_type=jnp.float32
    )
    squeezed = half_silu(0.5 * squeezed)
    grown = b2_ref[at, :] + jnp.dot(
        squeezed, w2_ref[layer], precision=lax.Precision.HIGHEST, preferred_element_type=jnp.float32
    )
    gate_ref[:, :mid] = 0.5 + 0.5 * jnp.tanh(0.5 * grown)

    group = cells // parts
    out = proj_ref.shape[1]

    def part_step(part, carry):
        first, second = carry
        base = pl.multiple_of(part * group, group)
        for k in range(blocks):
            size = min(LANE, mid - k * LANE)
            gate = gate_ref[:, k * LANE : k * LANE + size]
            scaled = (lift_ref[k, pl.ds(base, group), :, :size] * gate).reshape(group * 16, size)
            scaled_ref[:, k * LANE : k * LANE + size] = scaled.astype(jnp.bfloat16)
        projected = jnp.dot(scaled_ref[...], wp_ref[layer], preferred_element_type=jnp.float32)
        proj_ref[pl.ds(pl.multiple_of(part * group * 16, group * 16), group * 16), :] = projected
        centered = projected - mean3_ref[at, :]
        return first + fold_rows(centered), second + fold_rows(centered * centered)

    zero = jnp.zeros((8, out), jnp.float32)
    first, second = lax.fori_loop(0, parts, part_step, (zero, zero))
    stat_ref[...] = stat_copies(first, second, stat_ref.shape[0])


def lift_call(
    spread, coef, squeeze_weight, squeeze_bias, excite_weight, excite_bias, project_weight, out_mean, layer, members
):
    blocks, cells = spread.shape[:2]
    mid, out = project_weight.shape[1:]
    parts = 3
    rows = cells * 16
    return call(
        functools.partial(lift_kernel, layer=layer, parts=parts),
        "lift_project",
        [
            jax.ShapeDtypeStruct((rows, out), jnp.float32),
            jax.ShapeDtypeStruct((members, 2, out), jnp.float32),
        ],
        [
            pltpu.VMEM((blocks, cells, 16, LANE), jnp.float32),
            pltpu.VMEM((16, blocks * LANE), jnp.float32),
            pltpu.VMEM((16, blocks * LANE), jnp.float32),
            pltpu.VMEM((rows // parts, mid), jnp.bfloat16),
        ],
        44, spread, coef, squeeze_weight, squeeze_bias, excite_weight, excite_bias, project_weight, out_mean,
    )


def output_kernel(x_ref, proj_ref, coef_ref, *rest, layer, parts):
    if len(rest) > 1:
        w_ref, mid_mean_ref, next_ref, stat_ref = rest
    else:
        (next_ref,) = rest
    scale = coef_ref[0:1, :]
    shift = coef_ref[1:2, :]

    def step(i, carry):
        here = pl.ds(pl.multiple_of(i * 192, 192), 192)
        total = x_ref[here, :].astype(jnp.float32) + proj_ref[here, :] * scale + shift
        next_ref[here, :] = total.astype(jnp.bfloat16)
        return carry

    lax.fori_loop(0, x_ref.shape[0] // 192, step, 0)
    if len(rest) > 1:
        expand_moments(next_ref, w_ref, mid_mean_ref, stat_ref, layer + 1, parts)


def output_call(x, projected, coef, layer, members, follow=None):
    rows, out = x.shape
    out_shape = [jax.ShapeDtypeStruct((rows, out), jnp.bfloat16)]
    operands = [x, projected, coef]
    if follow is not None:
        out_shape.append(jax.ShapeDtypeStruct((members, 2, follow[0].shape[2]), jnp.float32))
        operands += list(follow)
    return call(
        functools.partial(output_kernel, layer=layer, parts=3), "block_output", out_shape, [], 24, *operands
    )


def exchange(stats):
    sums = lax.all_to_all(stats, "row", split_axis=0, concat_axis=0, tiled=True)
    total = jnp.sum(sums, axis=0)
    copies = jnp.broadcast_to(total[None], (lax.axis_size("col"),) + total.shape)
    return jnp.sum(lax.all_to_all(copies, "col", split_axis=0, concat_axis=0, tiled=True), axis=0)


def per_device(
    images, expand_weight, depth_kernel, squeeze_weight, squeeze_bias, excite_weight, excite_bias,
    project_weight, mid_gain, mid_bias, out_gain, out_bias, mid_mean, mid_var, out_mean, out_var,
):
    batch, side, _, out = images.shape
    mid = expand_weight.shape[2]
    members = lax.axis_size("row")
    row_count = float(batch * side * side * members * lax.axis_size("col"))
    spare = -mid % LANE
    widen = lambda a: jnp.pad(a, [(0, 0)] * (a.ndim - 1) + [(0, spare)])
    current = jnp.transpose(images, (1, 2, 0, 3)).reshape(side * side * batch, out)
    mean_new, var_new, out_mean_new, out_var_new = [], [], [], []
    stats = moments_call(current, expand_weight, mid_mean, 0, members)
    expand_padded, kernel_padded, mean_padded = widen(expand_weight), widen(depth_kernel), widen(mid_mean)
    for layer in range(LAYERS):
        settle = lambda sums, k: coefficients(
            sums, row_count, mid_mean[layer, k], mid_var[layer, k], mid_gain[layer, k], mid_bias[layer, k]
        )
        coef, mean_a, var_a = settle(exchange(stats), 0)
        spread, stats = depth_call(
            current, expand_padded, kernel_padded, widen(coef), mean_padded, mid, members, layer, side
        )
        coef, mean_b, var_b = settle(exchange(stats), 1)
        projected, stats = lift_call(
            spread, widen(coef), squeeze_weight, squeeze_bias, excite_weight, excite_bias,
            project_weight, out_mean, layer, members,
        )
        coef, mean_c, var_c = coefficients(
            exchange(stats), row_count, out_mean[layer], out_var[layer], out_gain[layer], out_bias[layer]
        )
        if layer + 1 < LAYERS:
            current, stats = output_call(current, projected, coef, layer, members, (expand_weight, mid_mean))
        else:
            (current,) = output_call(current, projected, coef, layer, members)
        mean_new.append(jnp.stack([mean_a, mean_b]))
        var_new.append(jnp.stack([var_a, var_b]))
        out_mean_new.append(mean_c)
        out_var_new.append(var_c)
    block_output = jnp.transpose(current.reshape(side, side, batch, out), (2, 0, 1, 3))
    return (
        block_output, jnp.stack(mean_new), jnp.stack(var_new), jnp.stack(out_mean_new), jnp.stack(out_var_new)
    )


def solution(mesh):
    split = P(("row", "col"), None, None, None)
    return jax.shard_map(
        per_device, mesh=mesh, in_specs=(split,) + (P(),) * 15, out_specs=(split, P(), P(), P(), P()), check_vma=False
    )
```

time: 350 us -> 300 us (0.86)
  other arithmetic: 144 us -> 29.2 us
  blocking collectives: 14.8 us -> 109 us
  Pallas kernels: 0 us -> 71.3 us
  waiting for transfers between devices: 85.3 us -> 19.1 us
  matrix products: 37.2 us -> 0 us
  local copies, waits for them, and re-layouts: 14.4 us -> 48.8 us
  starting transfers between devices: 52.4 us -> 19 us
    reduce_sum x16 -> x12, other arithmetic: 118 us -> 9.94 us  [the longest x6 5.74 us: exchange(): jnp.sum(lax.all_to_all(copies, 'col', split_axis=0, concat_axis=0, tiled=...]
    all_to_all x1 -> x8, blocking collectives: 14.8 us -> 109 us  [the longest x5 76.7 us: exchange(): sums = lax.all_to_all(stats, 'row', split_axis=0, concat_axis=0, tiled=True)]
    pallas_call x0 -> x7, Pallas kernels: none -> 71.3 us  [call(): pl.pallas_call(kernel, in_specs=[pl.BlockSpec(memory_space=pltpu.VMEM)] *...]
    all_to_all x11 -> x4, waiting for transfers between devices: 85.3 us -> 19.1 us  [the longest x3 13.7 us: exchange(): lax.all_to_all(copies, 'col', split_axis=0, concat_axis=0, tiled=True)]
    unnamed x28 -> x64, local copies, waits for them, and re-layouts: 1.63 us -> 43.8 us
    dot_general x8 -> x0, matrix products: 37.2 us -> none  [the longest x4 35.4 us: project_rows(): product = jnp.dot(flat_rows, matrix, preferred_element_type=jnp.float32)]
    all_to_all x11 -> x4, starting transfers between devices: 52.4 us -> 19 us  [the longest x3 14.4 us: exchange(): lax.all_to_all(copies, 'col', split_axis=0, concat_axis=0, tiled=True)]
    convert_element_type x4 -> x0, other arithmetic: 22.5 us -> none  [the longest x2 15.6 us: per_device(): jax.nn.silu(expanded * first_coef[0] + first_coef[1]).astype(jnp.bfloat16)]
  transfers between devices with their start and end apart: 11 -> 4, of which waited for: 11 -> 4; matrix products, arithmetic and copies ran while one was open for 1% -> 4% of each run, Pallas kernels for 0% -> 0%
where the time goes in v3:
time: 300 us; the launch traced here: 297 us
  blocking collectives  109 us (36%)
  Pallas kernels  71.3 us (24%)
  local copies, waits for them, and re-layouts  48.8 us (16%)
  other arithmetic  29.2 us (10%)
  waiting for transfers between devices  19.1 us (6%)
  starting transfers between devices  19 us (6%)
    all_to_all x5, blocking collectives, exchange(): sums = lax.all_to_all(stats, 'row', split_axis=0, concat_axis=0, tiled=True)  76.7 us
    pallas_call x7, Pallas kernels, call(): pl.pallas_call(kernel, in_specs=[pl.BlockSpec(memory_space=pltpu.VMEM)] *...  71.3 us
    unnamed x64, local copies, waits for them, and re-layouts  43.8 us
    all_to_all x3, blocking collectives, exchange(): lax.all_to_all(copies, 'col', split_axis=0, concat_axis=0, tiled=True)  32.4 us
    all_to_all x3, starting transfers between devices, exchange(): lax.all_to_all(copies, 'col', split_axis=0, concat_axis=0, tiled=True)  14.4 us
    all_to_all x3, waiting for transfers between devices, exchange(): lax.all_to_all(copies, 'col', split_axis=0, concat_axis=0, tiled=True)  13.7 us
    div x6, other arithmetic, coefficients(): gain_scale = gain * scale_ratio / batch_sigma  7.72 us
    add x6, other arithmetic, coefficients(): new_var = run_var + MOMENTUM * (batch_var - run_var)  6.18 us
  transfers between devices with their start and end apart: 4, of which 4 were waited for; matrix products, arithmetic and copies ran while one was open for 4% of the time, Pallas kernels for 0%

profile of v3, /device:TPU:1, one launch (start us, length us, event | category | flops | bytes accessed | tf_op | source)
XLA Modules:
  0.0 297.4 jit_solution(11379576574890573836)
XLA Ops:
  4.3 5.4 %expand_moments.1 = f32[16,2,1632]{2,1,0:T(2,128)S(1)} custom-call(bf16[2304,272]{1,0:T(8,128)(2,1)S(1)} %bitcast.154, bf16[2,272,1632]{2,1,0:T(8,128)(2,1)S(1)} %copy-done, f32[2,2,1632]{2,1,0:T(2,128)S(1)} %copy-done.21), custom_call_target="tpu_custom_call" | custom-call | tf_op jit(solution)/shard_map/expand_moments/pallas_call | solution.py:51
  9.7 20.5 %all_to_all.60 = f32[16,2,1632]{2,1,0:T(2,128)S(1)} all-to-all(f32[16,2,1632]{2,1,0:T(2,128)S(1)} %expand_moments.1), channel_id=1, replica_groups=mesh['row'=16,'col'=16] {'row'}, dimensions={0} | all-to-all | bytes 417792 | tf_op jit(solution)/shard_map/all_to_all | solution.py:296
  31.0 6.8 %all-to-all-start.1 = ((f32[16,2,1632]{2,1,0:T(2,128)}), f32[16,2,1632]{2,1,0:T(2,128)S(1)}, u32[]{:S(2)}, u32[]{:S(2)}) async-start(f32[16,2,1632]{2,1,0:T(2,128)} %broadcast_in_dim.12), calls=%async_computation.1 | async-start | bytes 425984 | tf_op jit(solution)/shard_map/all_to_all | solution.py:299
  39.3 6.2 %all-to-all-done.1 = f32[16,2,1632]{2,1,0:T(2,128)S(1)} async-done(((f32[16,2,1632]{2,1,0:T(2,128)}), f32[16,2,1632]{2,1,0:T(2,128)S(1)}, u32[]{:S(2)}, u32[]{:S(2)}) %all-to-all-start.1) | async-done | bytes 208928 | tf_op jit(solution)/shard_map/all_to_all | solution.py:299
  49.9 13.7 %depthwise.2 = (f32[13,144,16,128]{3,2,1,0:T(8,128)S(1)}, f32[16,2,1632]{2,1,0:T(2,128)S(1)}) custom-call(bf16[2304,272]{1,0:T(8,128)(2,1)S(1)} %bitcast.155, bf16[2,272,1664]{2,1,0:T(8,128)(2,1)S(1)} %copy-done.3, f32[2,25,1664]{2,1,0:T(8,128)S(1)} %pad.26.dk_ref, f32[2,1664]{1,0:T(2,128)S(1)} %select_maximum_fusion.3.coef_ref, f32[2,2,1664]{2,1,0:T(2,128)S(1)} %pad.28.mean_ref), custom_call_target="tpu_custom_call" | custom-call | tf_op jit(solution)/shard_map/depthwise/pallas_call | solution.py:51
  63.6 5.4 %copy-done.8 = f32[13,144,16,128]{3,2,1,0:T(8,128)} copy-done((f32[13,144,16,128]{3,2,1,0:T(8,128)}, f32[13,144,16,128]{3,2,1,0:T(8,128)S(1)}, u32[]{:S(2)}) %copy-start.8) | copy-done | bytes 15335448
  69.0 14.5 %all_to_all.61 = f32[16,2,1632]{2,1,0:T(2,128)S(1)} all-to-all(f32[16,2,1632]{2,1,0:T(2,128)S(1)} %get-tuple-element.16), channel_id=1, replica_groups=mesh['row'=16,'col'=16] {'row'}, dimensions={0} | all-to-all | bytes 417792 | tf_op jit(solution)/shard_map/all_to_all | solution.py:296
  84.3 4.2 %all-to-all-start.3 = ((f32[16,2,1632]{2,1,0:T(2,128)}), f32[16,2,1632]{2,1,0:T(2,128)}, u32[]{:S(2)}, u32[]{:S(2)}) async-start(f32[16,2,1632]{2,1,0:T(2,128)} %broadcast_in_dim.13), calls=%async_computation.3 | async-start | bytes 425984 | tf_op jit(solution)/shard_map/all_to_all | solution.py:299
  90.4 4.4 %copy.40.wp_ref = bf16[2,1632,272]{2,1,0:T(8,128)(2,1)S(1)} copy(bf16[2,1632,272]{1,2,0:T(8,128)(2,1)} %param.23) | data formatting | bytes 3551232 | tf_op args[7]
  102.5 15.0 %lift_project.2 = (f32[2304,272]{1,0:T(8,128)S(1)}, f32[16,2,272]{2,1,0:T(2,128)S(1)}) custom-call(f32[13,144,16,128]{3,2,1,0:T(8,128)} %copy-done.8, f32[2,1664]{1,0:T(2,128)S(1)} %select_maximum_fusion.2.coef_ref, f32[2,1632,68]{2,1,0:T(8,128)S(1)} %copy-done.10, f32[2,68]{1,0:T(2,128)S(1)} %copy-done.25, f32[2,68,1632]{2,1,0:T(8,128)S(1)} %copy.39.w2_ref, ...), custom_call_target="tpu_custom_call" | custom-call | tf_op jit(solution)/shard_map/lift_project/pallas_call | solution.py:51
  119.2 11.6 %all_to_all.62 = f32[16,2,272]{2,1,0:T(2,128)} all-to-all(f32[16,2,272]{2,1,0:T(2,128)S(1)} %get-tuple-element.18), channel_id=1, replica_groups=mesh['row'=16,'col'=16] {'row'}, dimensions={0} | all-to-all | bytes 69632 | tf_op jit(solution)/shard_map/all_to_all | solution.py:296
  132.9 10.2 %all_to_all.63 = f32[16,2,272]{2,1,0:T(2,128)} all-to-all(f32[16,2,272]{2,1,0:T(2,128)S(1)} %broadcast_in_dim.14), channel_id=1, replica_groups=mesh['row'=16,'col'=16] {'col'}, dimensions={0} | all-to-all | bytes 69632 | tf_op jit(solution)/shard_map/all_to_all | solution.py:299
  152.2 6.0 %block_output.2 = (bf16[2304,272]{1,0:T(8,128)(2,1)S(1)}, f32[16,2,1632]{2,1,0:T(2,128)S(1)}) custom-call(bf16[2304,272]{1,0:T(8,128)(2,1)S(1)} %bitcast.156, f32[2304,272]{1,0:T(8,128)S(1)} %copy-done.18, f32[2,272]{1,0:T(2,128)S(1)} %pad_maximum_fusion.2.coef_ref, bf16[2,272,1632]{2,1,0:T(8,128)(2,1)S(1)} %copy-done.2, f32[2,2,1632]{2,1,0:T(2,128)S(1)} %copy-done.22), custom_call_target="tpu_custom_call" | custom-call | tf_op jit(solution)/shard_map/block_output/pallas_call | solution.py:51
  159.4 15.5 %all_to_all.64 = f32[16,2,1632]{2,1,0:T(2,128)} all-to-all(f32[16,2,1632]{2,1,0:T(2,128)S(1)} %get-tuple-element.20), channel_id=1, replica_groups=mesh['row'=16,'col'=16] {'row'}, dimensions={0} | all-to-all | bytes 417792 | tf_op jit(solution)/shard_map/all_to_all | solution.py:296
  177.3 11.3 %all_to_all.65 = f32[16,2,1632]{2,1,0:T(2,128)} all-to-all(f32[16,2,1632]{2,1,0:T(2,128)S(1)} %broadcast_in_dim.15), channel_id=1, replica_groups=mesh['row'=16,'col'=16] {'col'}, dimensions={0} | all-to-all | bytes 417792 | tf_op jit(solution)/shard_map/all_to_all | solution.py:299
  197.0 13.7 %depthwise.3 = (f32[13,144,16,128]{3,2,1,0:T(8,128)S(1)}, f32[16,2,1632]{2,1,0:T(2,128)S(1)}) custom-call(bf16[2304,272]{1,0:T(8,128)(2,1)S(1)} %copy-done.13, bf16[2,272,1664]{2,1,0:T(8,128)(2,1)S(1)} %copy-done.4, f32[2,25,1664]{2,1,0:T(8,128)S(1)} %copy-done.16, f32[2,1664]{1,0:T(2,128)S(1)} %select_maximum_fusion.1.coef_ref, f32[2,2,1664]{2,1,0:T(2,128)S(1)} %pad.28.mean_ref), custom_call_target="tpu_custom_call" | custom-call | tf_op jit(solution)/shard_map/depthwise/pallas_call | solution.py:51
  210.8 5.4 %copy-done.9 = f32[13,144,16,128]{3,2,1,0:T(8,128)} copy-done((f32[13,144,16,128]{3,2,1,0:T(8,128)}, f32[13,144,16,128]{3,2,1,0:T(8,128)S(1)}, u32[]{:S(2)}) %copy-start.9) | copy-done | bytes 15335448
  216.1 14.7 %all_to_all.66 = f32[16,2,1632]{2,1,0:T(2,128)} all-to-all(f32[16,2,1632]{2,1,0:T(2,128)S(1)} %get-tuple-element.22), channel_id=1, replica_groups=mesh['row'=16,'col'=16] {'row'}, dimensions={0} | all-to-all | bytes 417792 | tf_op jit(solution)/shard_map/all_to_all | solution.py:296
  231.9 10.9 %all_to_all.67 = f32[16,2,1632]{2,1,0:T(2,128)} all-to-all(f32[16,2,1632]{2,1,0:T(2,128)S(1)} %broadcast_in_dim.16), channel_id=1, replica_groups=mesh['row'=16,'col'=16] {'col'}, dimensions={0} | all-to-all | bytes 417792 | tf_op jit(solution)/shard_map/all_to_all | solution.py:299
  248.0 15.6 %lift_project.3 = (f32[2304,272]{1,0:T(8,128)S(1)}, f32[16,2,272]{2,1,0:T(2,128)}) custom-call(f32[13,144,16,128]{3,2,1,0:T(8,128)} %copy-done.9, f32[2,1664]{1,0:T(2,128)S(1)} %select_maximum_fusion.coef_ref, f32[2,1632,68]{2,1,0:T(8,128)S(1)} %copy-done.11, f32[2,68]{1,0:T(2,128)S(1)} %copy-done.25, f32[2,68,1632]{2,1,0:T(8,128)S(1)} %copy.39.w2_ref, ...), custom_call_target="tpu_custom_call" | custom-call | tf_op jit(solution)/shard_map/lift_project/pallas_call | solution.py:51
  265.4 4.6 %all-to-all-start.10 = ((f32[16,2,272]{2,1,0:T(2,128)}), f32[16,2,272]{2,1,0:T(2,128)S(1)}, u32[]{:S(2)}, u32[]{:S(2)}) async-start(f32[16,2,272]{2,1,0:T(2,128)} %get-tuple-element.24), calls=%async_computation.10 | async-start | bytes 98304 | tf_op jit(solution)/shard_map/all_to_all | solution.py:296
  272.1 5.4 %all-to-all-done.10 = f32[16,2,272]{2,1,0:T(2,128)S(1)} async-done(((f32[16,2,272]{2,1,0:T(2,128)}), f32[16,2,272]{2,1,0:T(2,128)S(1)}, u32[]{:S(2)}, u32[]{:S(2)}) %all-to-all-start.10) | async-done | bytes 34848 | tf_op jit(solution)/shard_map/all_to_all | solution.py:296
  278.1 3.5 %all-to-all-start.11 = ((f32[16,2,272]{2,1,0:T(2,128)}), f32[16,2,272]{2,1,0:T(2,128)S(1)}, u32[]{:S(2)}, u32[]{:S(2)}) async-start(f32[16,2,272]{2,1,0:T(2,128)} %broadcast_in_dim.17), calls=%async_computation.11 | async-start | bytes 98304 | tf_op jit(solution)/shard_map/all_to_all | solution.py:299
  282.3 5.8 %all-to-all-done.11 = f32[16,2,272]{2,1,0:T(2,128)S(1)} async-done(((f32[16,2,272]{2,1,0:T(2,128)}), f32[16,2,272]{2,1,0:T(2,128)S(1)}, u32[]{:S(2)}, u32[]{:S(2)}) %all-to-all-start.11) | async-done | bytes 34848 | tf_op jit(solution)/shard_map/all_to_all | solution.py:299
  (107 shorter events, 66.4 us)
Async XLA Ops:
  0.6 1.5 copy-start
  4.3 33.4 %copy-start.22 = (f32[2,2,1632]{2,1,0:T(2,128)S(1)}, f32[2,2,1632]{2,1,0:T(2,128)}, u32[]{:S(2)}) copy-start(f32[2,2,1632]{2,1,0:T(2,128)} %rest_1_.1) | copy-start | bytes 78340
  4.3 33.4 %copy-start.28 = (f32[2,25,1632]{2,0,1:T(2,128)S(1)}, f32[2,25,1632]{2,0,1:T(2,128)}, u32[]{:S(2)}) copy-start(f32[2,25,1632]{2,0,1:T(2,128)} %param.18) | copy-start | bytes 979204
  9.7 28.2 %copy-start.1 = (bf16[2,272,1632]{2,1,0:T(8,128)(2,1)S(1)}, bf16[2,272,1632]{2,1,0:T(8,128)(2,1)}, u32[]{:S(2)}) copy-start(bf16[2,272,1632]{2,1,0:T(8,128)(2,1)} %rest_0_.1) | copy-start | bytes 5326852
  31.0 14.4 %all-to-all-start.1 = ((f32[16,2,1632]{2,1,0:T(2,128)}), f32[16,2,1632]{2,1,0:T(2,128)S(1)}, u32[]{:S(2)}, u32[]{:S(2)}) async-start(f32[16,2,1632]{2,1,0:T(2,128)} %broadcast_in_dim.12), calls=%async_computation.1 | async-start | bytes 425984 | tf_op jit(solution)/shard_map/all_to_all | solution.py:299
  37.9 9.0 %copy-start.15 = (f32[2,25,1664]{2,1,0:T(8,128)}, f32[2,25,1664]{2,1,0:T(8,128)S(1)}, u32[]{:S(2)}) copy-start(f32[2,25,1664]{2,1,0:T(8,128)S(1)} %pad.26.dk_ref) | copy-start | bytes 998404
  37.9 7.6 %copy-start.29 = (f32[2,2,1632]{2,1,0:T(2,128)S(1)}, f32[2,2,1632]{2,1,0:T(2,128)}, u32[]{:S(2)}) copy-start(f32[2,2,1632]{2,1,0:T(2,128)} %param.29) | copy-start | bytes 78340
  46.9 1.5 copy-start.3
  49.9 38.6 %copy-start.26 = (f32[2,68,1632]{2,0,1:T(2,128)S(1)}, f32[2,68,1632]{2,0,1:T(2,128)}, u32[]{:S(2)}) copy-start(f32[2,68,1632]{2,0,1:T(2,128)} %param.21) | copy-start | bytes 2663428
  63.6 5.4 %copy-start.8 = (f32[13,144,16,128]{3,2,1,0:T(8,128)}, f32[13,144,16,128]{3,2,1,0:T(8,128)S(1)}, u32[]{:S(2)}) copy-start(f32[13,144,16,128]{3,2,1,0:T(8,128)S(1)} %get-tuple-element.15.spread_ref) | copy-start | bytes 46006276
  69.0 19.6 %copy-start.27 = (f32[2,1632,68]{1,0,2:T(2,128)S(1)}, f32[2,1632,68]{1,0,2:T(2,128)}, u32[]{:S(2)}) copy-start(f32[2,1632,68]{1,0,2:T(2,128)} %param.19) | copy-start | bytes 2663428
  84.3 12.2 %all-to-all-start.3 = ((f32[16,2,1632]{2,1,0:T(2,128)}), f32[16,2,1632]{2,1,0:T(2,128)}, u32[]{:S(2)}, u32[]{:S(2)}) async-start(f32[16,2,1632]{2,1,0:T(2,128)} %broadcast_in_dim.13), calls=%async_computation.3 | async-start | bytes 425984 | tf_op jit(solution)/shard_map/all_to_all | solution.py:299
  90.4 10.6 %copy-start.23 = (f32[2,1632]{1,0:T(2,128)S(1)}, f32[2,1632]{1,0:T(2,128)}, u32[]{:S(2)}) copy-start(f32[2,1632]{1,0:T(2,128)} %b2_ref.3) | copy-start | bytes 39172
  90.4 10.6 %copy-start.24 = (f32[2,272]{1,0:T(2,128)S(1)}, f32[2,272]{1,0:T(2,128)}, u32[]{:S(2)}) copy-start(f32[2,272]{1,0:T(2,128)} %mean3_ref.3) | copy-start | bytes 6532
  90.4 10.6 %copy-start.25 = (f32[2,68]{1,0:T(2,128)S(1)}, f32[2,68]{1,0:T(2,128)}, u32[]{:S(2)}) copy-start(f32[2,68]{1,0:T(2,128)} %b1_ref.3) | copy-start | bytes 1636
  117.5 1.8 copy-start.17
  147.2 1.5 copy-start.2
  150.2 2.0 copy-start.18
  193.0 1.5 copy-start.4
  210.7 5.4 %copy-start.9 = (f32[13,144,16,128]{3,2,1,0:T(8,128)}, f32[13,144,16,128]{3,2,1,0:T(8,128)S(1)}, u32[]{:S(2)}) copy-start(f32[13,144,16,128]{3,2,1,0:T(8,128)S(1)} %get-tuple-element.21.spread_ref) | copy-start | bytes 46006276
  263.6 1.8 copy-start.19
  265.4 12.1 %all-to-all-start.10 = ((f32[16,2,272]{2,1,0:T(2,128)}), f32[16,2,272]{2,1,0:T(2,128)S(1)}, u32[]{:S(2)}, u32[]{:S(2)}) async-start(f32[16,2,272]{2,1,0:T(2,128)} %get-tuple-element.24), calls=%async_computation.10 | async-start | bytes 98304 | tf_op jit(solution)/shard_map/all_to_all | solution.py:296
  278.1 9.9 %all-to-all-start.11 = ((f32[16,2,272]{2,1,0:T(2,128)}), f32[16,2,272]{2,1,0:T(2,128)S(1)}, u32[]{:S(2)}, u32[]{:S(2)}) async-start(f32[16,2,272]{2,1,0:T(2,128)} %broadcast_in_dim.17), calls=%async_computation.11 | async-start | bytes 98304 | tf_op jit(solution)/shard_map/all_to_all | solution.py:299
  293.6 2.0 copy-start.20
  (10 other events, 13.2 us)

commit v4 on v3

v4 whole, which is shorter than its diff:
```python
import functools
import jax
import jax.numpy as jnp
from jax import lax
from jax.experimental import pallas as pl
from jax.experimental.pallas import tpu as pltpu
from jax.sharding import PartitionSpec as P

KERN = 5
LAYERS = 2
EPSILON = 0.001
RATIO_MAX = 3.0
SHIFT_MAX = 5.0
MOMENTUM = 0.01
LANE = 128
WIDE = 256
MIB = 1 << 20


def coefficients(received, row_count, run_mean, run_var, gain, bias):
    offset = received[0:1] / row_count
    batch_var = received[1:2] / row_count - offset * offset
    batch_mean = run_mean + offset
    batch_sigma = jnp.sqrt(batch_var + EPSILON)
    run_sigma = jnp.sqrt(run_var + EPSILON)
    scale_ratio = jnp.clip(batch_sigma / run_sigma, 1.0 / RATIO_MAX, RATIO_MAX)
    shift_clip = jnp.clip(offset / run_sigma, -SHIFT_MAX, SHIFT_MAX)
    gain_scale = gain * scale_ratio / batch_sigma
    gain_shift = bias + gain * shift_clip - batch_mean * gain_scale
    new_mean = run_mean + MOMENTUM * offset
    new_var = run_var + MOMENTUM * (batch_var - run_var)
    return gain_scale, gain_shift, new_mean, new_var


def settle(recv_ref, param_ref, at, coef_ref, new_ref, row_count):
    size = recv_ref.shape[1]
    coef_ref[...] = jnp.zeros(coef_ref.shape, jnp.float32)
    coef_ref[:, :size] = recv_ref[...]
    index, half = at
    mean, var, gain, bias = [param_ref[4 * index + n : 4 * index + n + 1, :] for n in range(4)]
    scale, shift, new_mean, new_var = coefficients(coef_ref[...], row_count, mean, var, gain, bias)
    coef_ref[...] = half * jnp.concatenate([scale, shift], axis=0)
    new_ref[...] = jnp.concatenate([new_mean, new_var], axis=0)[:, :size]


def start_copies(pairs, sems):
    copies = [pltpu.make_async_copy(source, target, sems.at[n]) for n, (source, target) in enumerate(pairs)]
    for copy in copies:
        copy.start()
    return copies


def half_silu(half):
    return half + half * jnp.tanh(half)


def fold_rows(block):
    return jnp.sum(block.reshape(block.shape[0] // 8, 8, block.shape[1]), axis=0)


def stat_copies(first, second, members):
    pair = jnp.concatenate(
        [jnp.sum(first, axis=0, keepdims=True), jnp.sum(second, axis=0, keepdims=True)], axis=0
    )
    return jnp.broadcast_to(pair[None], (members,) + pair.shape)


def call(kernel, name, in_vmem, outs, scratch, limit, *operands):
    spec = lambda inside: pl.BlockSpec(memory_space=pltpu.VMEM if inside else pltpu.HBM)
    return pl.pallas_call(
        kernel,
        in_specs=[spec(n in in_vmem) for n in range(len(operands))],
        out_specs=[spec(inside) for _, inside in outs],
        out_shape=[shape for shape, _ in outs],
        scratch_shapes=scratch,
        compiler_params=pltpu.CompilerParams(vmem_limit_bytes=62 * MIB),
        name=name,
    )(*operands)


def expand_moments(x_ref, w_ref, mean_ref, stat_ref, parts):
    rows = x_ref.shape[0]
    mid = w_ref.shape[1]
    chunk = rows // parts

    def lanes(here):
        mean = mean_ref[0:1, here]
        first = second = None
        for part in range(parts):
            values = jnp.dot(
                x_ref[part * chunk : (part + 1) * chunk, :], w_ref[:, here],
                preferred_element_type=jnp.float32,
            )
            centered = values - mean
            one, two = fold_rows(centered), fold_rows(centered * centered)
            first = one if first is None else first + one
            second = two if second is None else second + two
        stat_ref[:, :, here] = stat_copies(first, second, stat_ref.shape[0])

    def step(j, carry):
        lanes(pl.ds(pl.multiple_of(j * WIDE, WIDE), WIDE))
        return carry

    full = mid // WIDE
    lax.fori_loop(0, full, step, 0)
    if mid > full * WIDE:
        lanes(slice(full * WIDE, mid))


def moments_kernel(x_hbm, w_hbm, mean_hbm, stat_ref, x_ref, w_ref, mean_ref, sems, *, layer, parts):
    pairs = [(x_hbm, x_ref), (w_hbm.at[layer], w_ref), (mean_hbm.at[layer], mean_ref)]
    for copy in start_copies(pairs, sems):
        copy.wait()
    expand_moments(x_ref, w_ref, mean_ref, stat_ref, parts)


def moments_call(x, expand_weight, mid_mean, layer, members):
    _, out, mid = expand_weight.shape
    return call(
        functools.partial(moments_kernel, layer=layer, parts=3),
        "expand_moments", (),
        [(jax.ShapeDtypeStruct((members, 2, mid), jnp.float32), True)],
        [
            pltpu.VMEM(x.shape, x.dtype),
            pltpu.VMEM((out, mid), expand_weight.dtype),
            pltpu.VMEM((2, mid), jnp.float32),
            pltpu.SemaphoreType.DMA((3,)),
        ],
        20, x, expand_weight, mid_mean,
    )[0]


def depth_kernel_body(
    x_hbm, w_hbm, dk_hbm, param_hbm, recv_hbm, spread_hbm, stat_ref, new_ref,
    recv_ref, spread_ref, x_ref, w_ref, dk_ref, param_ref, coef_ref, act_ref, tap_ref, in_sems, out_sems,
    *, layer, side, parts, row_count,
):
    copies = start_copies(
        [
            (recv_hbm, recv_ref), (param_hbm, param_ref), (x_hbm, x_ref), (w_hbm.at[layer], w_ref),
            (dk_hbm.at[layer], dk_ref),
        ],
        in_sems,
    )
    for copy in copies[:2]:
        copy.wait()
    settle(recv_ref, param_ref, (2 * layer, 0.5), coef_ref, new_ref, row_count)
    for copy in copies[2:]:
        copy.wait()
    rows = x_ref.shape[0]
    mid = stat_ref.shape[2]
    blocks = spread_ref.shape[0]
    reach = KERN // 2
    chunk = rows // parts
    cells = chunk // 16

    def leave(block):
        return pltpu.make_async_copy(spread_ref.at[block], spread_hbm.at[block], out_sems.at[block])

    def activate(start, width):
        here = pl.ds(start, width)
        scale = coef_ref[0:1, here]
        shift = coef_ref[1:2, here]
        for part in range(parts):
            values = jnp.dot(
                x_ref[part * chunk : (part + 1) * chunk, :], w_ref[:, here],
                preferred_element_type=jnp.float32,
            )
            active = half_silu(values * scale + shift).astype(jnp.bfloat16).reshape(cells, 16, width)
            for s in range(width // LANE):
                act_ref[s, part * cells : (part + 1) * cells] = active[:, :, s * LANE : (s + 1) * LANE]

    def spread_block(s, block, start, size):
        here = pl.ds(start, LANE)
        mean = param_ref[8 * layer + 4 : 8 * layer + 5, here]
        for t in range(KERN * KERN):
            tap_ref[s, t] = jnp.broadcast_to(dk_ref[t : t + 1, here], (16, LANE)).astype(jnp.bfloat16)
        first = jnp.zeros((16, LANE), jnp.float32)
        second = jnp.zeros((16, LANE), jnp.float32)
        for h in range(side):
            for w in range(side):
                acc = None
                for i in range(KERN):
                    for k in range(KERN):
                        r, p = h + i - reach, w + k - reach
                        if 0 <= r < side and 0 <= p < side:
                            cell = act_ref[s, r * side + p].astype(jnp.float32)
                            term = cell * tap_ref[s, i * KERN + k].astype(jnp.float32)
                            acc = term if acc is None else acc + term
                spread_ref[block, h * side + w] = acc
                centered = acc - mean
                first = first + centered
                second = second + centered * centered
        copies = stat_copies(first, second, stat_ref.shape[0])
        stat_ref[:, :, pl.ds(start, size)] = copies[:, :, :size]
        leave(block).start()

    def step(j, carry):
        start = pl.multiple_of(j * WIDE, WIDE)
        activate(start, WIDE)
        spread_block(0, 2 * j, start, LANE)
        spread_block(1, 2 * j + 1, pl.multiple_of(start + LANE, LANE), LANE)
        return carry

    lax.fori_loop(0, blocks // 2, step, 0)
    if blocks % 2:
        start = (blocks - 1) * LANE
        activate(start, LANE)
        spread_block(0, blocks - 1, start, mid - start)
    for block in range(blocks):
        leave(block).wait()


def depth_call(x, expand_padded, kernel_padded, params, received, members, layer, side, row_count):
    _, out, padded = expand_padded.shape
    mid = received.shape[1]
    blocks = padded // LANE
    field = (blocks, side * side, 16, LANE)
    return call(
        functools.partial(depth_kernel_body, layer=layer, side=side, parts=3, row_count=row_count),
        "depthwise", (),
        [
            (jax.ShapeDtypeStruct(field, jnp.float32), False),
            (jax.ShapeDtypeStruct((members, 2, mid), jnp.float32), True),
            (jax.ShapeDtypeStruct((2, mid), jnp.float32), True),
        ],
        [
            pltpu.VMEM(received.shape, jnp.float32),
            pltpu.VMEM(field, jnp.float32),
            pltpu.VMEM(x.shape, x.dtype),
            pltpu.VMEM((out, padded), expand_padded.dtype),
            pltpu.VMEM(kernel_padded.shape[1:], jnp.float32),
            pltpu.VMEM(params.shape, jnp.float32),
            pltpu.VMEM((2, padded), jnp.float32),
            pltpu.VMEM((2,) + field[1:], jnp.bfloat16),
            pltpu.VMEM((2, KERN * KERN, 16, LANE), jnp.bfloat16),
            pltpu.SemaphoreType.DMA((5,)),
            pltpu.SemaphoreType.DMA((blocks,)),
        ],
        32, x, expand_padded, kernel_padded, params, received,
    )


def lift_kernel(
    spread_hbm, param_hbm, w1_hbm, b1_hbm, w2_hbm, b2_hbm, wp_hbm, mean3_hbm, recv_hbm,
    proj_hbm, stat_ref, new_ref,
    recv_ref, lift_ref, param_ref, w1_ref, b1_ref, w2_ref, b2_ref, wp_ref, mean3_ref,
    coef_ref, pool_ref, gate_ref, scaled_ref, proj_ref, in_sems, sems, out_sems, *, layer, parts, row_count,
):
    blocks, cells = lift_ref.shape[0], lift_ref.shape[1]
    mid = w1_ref.shape[0]

    def enter(block):
        return pltpu.make_async_copy(spread_hbm.at[block], lift_ref.at[block], in_sems.at[block])

    copies = start_copies([(recv_hbm, recv_ref), (param_hbm, param_ref)], sems)
    for block in range(blocks):
        enter(block).start()
    pairs = [
        (w1_hbm.at[layer], w1_ref), (b1_hbm, b1_ref), (w2_hbm.at[layer], w2_ref), (b2_hbm, b2_ref),
        (wp_hbm.at[layer], wp_ref), (mean3_hbm, mean3_ref),
    ]
    weights = [pltpu.make_async_copy(source, target, sems.at[n + 2]) for n, (source, target) in enumerate(pairs)]
    for copy in weights:
        copy.start()
    for copy in copies:
        copy.wait()
    settle(recv_ref, param_ref, (2 * layer + 1, 0.5), coef_ref, new_ref, row_count)
    at = slice(layer, layer + 1)
    batch = 24

    def block_step(j, carry):
        here = pl.ds(pl.multiple_of(j * LANE, LANE), LANE)
        scale = coef_ref[0:1, here]
        shift = coef_ref[1:2, here]
        enter(j).wait()

        def step(i, pooled):
            cell = pl.multiple_of(i * batch, batch)
            lifted = half_silu(lift_ref[j, pl.ds(cell, batch)] * scale + shift)
            lift_ref[j, pl.ds(cell, batch)] = lifted
            return pooled + jnp.sum(lifted, axis=0)

        pooled = lax.fori_loop(0, cells // batch, step, jnp.zeros((16, LANE), jnp.float32))
        pool_ref[:, here] = pooled * (1.0 / cells)
        return carry

    lax.fori_loop(0, blocks, block_step, 0)
    for copy in weights:
        copy.wait()

    squeezed = b1_ref[at, :] + jnp.dot(
        pool_ref[:, :mid], w1_ref[...], precision=lax.Precision.HIGHEST, preferred_element_type=jnp.float32
    )
    squeezed = half_silu(0.5 * squeezed)
    grown = b2_ref[at, :] + jnp.dot(
        squeezed, w2_ref[...], precision=lax.Precision.HIGHEST, preferred_element_type=jnp.float32
    )
    gate_ref[:, :mid] = 0.5 + 0.5 * jnp.tanh(0.5 * grown)

    group = cells // parts
    out = proj_ref.shape[2]

    def leave(part):
        return pltpu.make_async_copy(proj_ref.at[part], proj_hbm.at[part], out_sems.at[part])

    def part_step(part, carry):
        first, second = carry
        base = pl.multiple_of(part * group, group)
        for k in range(blocks):
            size = min(LANE, mid - k * LANE)
            gate = gate_ref[:, k * LANE : k * LANE + size]
            scaled = (lift_ref[k, pl.ds(base, group), :, :size] * gate).reshape(group * 16, size)
            scaled_ref[:, k * LANE : k * LANE + size] = scaled.astype(jnp.bfloat16)
        projected = jnp.dot(scaled_ref[...], wp_ref[...], preferred_element_type=jnp.float32)
        proj_ref[part] = projected
        leave(part).start()
        centered = projected - mean3_ref[at, :]
        return first + fold_rows(centered), second + fold_rows(centered * centered)

    zero = jnp.zeros((8, out), jnp.float32)
    first, second = lax.fori_loop(0, parts, part_step, (zero, zero))
    stat_ref[...] = stat_copies(first, second, stat_ref.shape[0])
    for part in range(parts):
        leave(part).wait()


def lift_call(
    spread, params, squeeze_weight, squeeze_bias, excite_weight, excite_bias, project_weight, out_mean,
    received, members, layer, row_count,
):
    blocks, cells = spread.shape[:2]
    mid, out = project_weight.shape[1:]
    parts = 3
    rows = cells * 16
    return call(
        functools.partial(lift_kernel, layer=layer, parts=parts, row_count=row_count),
        "lift_project", (),
        [
            (jax.ShapeDtypeStruct((parts, rows // parts, out), jnp.float32), False),
            (jax.ShapeDtypeStruct((members, 2, out), jnp.float32), True),
            (jax.ShapeDtypeStruct((2, mid), jnp.float32), True),
        ],
        [
            pltpu.VMEM(received.shape, jnp.float32),
            pltpu.VMEM(spread.shape, jnp.float32),
            pltpu.VMEM(params.shape, jnp.float32),
            pltpu.VMEM(squeeze_weight.shape[1:], jnp.float32),
            pltpu.VMEM(squeeze_bias.shape, jnp.float32),
            pltpu.VMEM(excite_weight.shape[1:], jnp.float32),
            pltpu.VMEM(excite_bias.shape, jnp.float32),
            pltpu.VMEM(project_weight.shape[1:], project_weight.dtype),
            pltpu.VMEM(out_mean.shape, jnp.float32),
            pltpu.VMEM((2, blocks * LANE), jnp.float32),
            pltpu.VMEM((16, blocks * LANE), jnp.float32),
            pltpu.VMEM((16, blocks * LANE), jnp.float32),
            pltpu.VMEM((rows // parts, mid), jnp.bfloat16),
            pltpu.VMEM((parts, rows // parts, out), jnp.float32),
            pltpu.SemaphoreType.DMA((blocks,)),
            pltpu.SemaphoreType.DMA((8,)),
            pltpu.SemaphoreType.DMA((parts,)),
        ],
        40, spread, params, squeeze_weight, squeeze_bias, excite_weight, excite_bias, project_weight, out_mean,
        received,
    )


def output_kernel(x_hbm, proj_hbm, param_hbm, recv_hbm, *rest, layer, parts, row_count, follow):
    if follow:
        w_hbm, mid_mean_hbm, next_hbm, new_ref, stat_ref = rest[:5]
        w_ref, mid_mean_ref, in_sems, more_sems, out_sems = rest[10:]
        recv_ref, x_ref, proj_ref, param_ref, coef_ref = rest[5:10]
    else:
        next_hbm, new_ref, recv_ref, x_ref, proj_ref, param_ref, coef_ref, in_sems, out_sems = rest
    copies = start_copies([(recv_hbm, recv_ref), (param_hbm, param_ref), (x_hbm, x_ref)], in_sems)
    enter = [
        pltpu.make_async_copy(proj_hbm.at[part], proj_ref.at[part], in_sems.at[3 + part]) for part in range(parts)
    ]
    for copy in enter:
        copy.start()
    if follow:
        more = start_copies([(w_hbm.at[layer + 1], w_ref), (mid_mean_hbm.at[layer + 1], mid_mean_ref)], more_sems)
    for copy in copies[:2]:
        copy.wait()
    settle(recv_ref, param_ref, (layer, 1.0), coef_ref, new_ref, row_count)
    copies[2].wait()
    scale = coef_ref[0:1, :]
    shift = coef_ref[1:2, :]
    size = proj_ref.shape[1]
    leave = [
        pltpu.make_async_copy(
            x_ref.at[part * size : (part + 1) * size], next_hbm.at[part * size : (part + 1) * size], out_sems.at[part]
        )
        for part in range(parts)
    ]
    for part in range(parts):
        enter[part].wait()

        def step(i, carry):
            inner = pl.ds(pl.multiple_of(i * 192, 192), 192)
            here = pl.ds(pl.multiple_of(part * size + i * 192, 192), 192)
            total = x_ref[here, :].astype(jnp.float32) + proj_ref[part, inner, :] * scale + shift
            x_ref[here, :] = total.astype(jnp.bfloat16)
            return carry

        lax.fori_loop(0, size // 192, step, 0)
        leave[part].start()
    if follow:
        for copy in more:
            copy.wait()
        expand_moments(x_ref, w_ref, mid_mean_ref, stat_ref, 3)
    for copy in leave:
        copy.wait()


def output_call(x, projected, params, received, members, layer, row_count, follow=None):
    rows, out = x.shape
    parts = projected.shape[0]
    outs = [
        (jax.ShapeDtypeStruct((rows, out), jnp.bfloat16), False),
        (jax.ShapeDtypeStruct((2, out), jnp.float32), True),
    ]
    scratch = [
        pltpu.VMEM(received.shape, jnp.float32),
        pltpu.VMEM((rows, out), jnp.bfloat16),
        pltpu.VMEM(projected.shape, jnp.float32),
        pltpu.VMEM(params.shape, jnp.float32),
        pltpu.VMEM((2, out), jnp.float32),
    ]
    sems = [pltpu.SemaphoreType.DMA((3 + parts,)), pltpu.SemaphoreType.DMA((parts,))]
    operands = [x, projected, params, received]
    if follow is not None:
        mid = follow[0].shape[2]
        outs.append((jax.ShapeDtypeStruct((members, 2, mid), jnp.float32), True))
        scratch += [pltpu.VMEM((out, mid), jnp.bfloat16), pltpu.VMEM((2, mid), jnp.float32)]
        sems.insert(1, pltpu.SemaphoreType.DMA((2,)))
        operands += list(follow)
    return call(
        functools.partial(
            output_kernel, layer=layer, parts=parts, row_count=row_count, follow=follow is not None
        ),
        "block_output", (), outs, scratch + sems, 24, *operands,
    )


def exchange(stats):
    sums = lax.all_to_all(stats, "row", split_axis=0, concat_axis=0, tiled=True)
    total = jnp.sum(sums, axis=0)
    copies = jnp.broadcast_to(total[None], (lax.axis_size("col"),) + total.shape)
    return jnp.sum(lax.all_to_all(copies, "col", split_axis=0, concat_axis=0, tiled=True), axis=0)


def per_device(
    images, expand_weight, depth_kernel, squeeze_weight, squeeze_bias, excite_weight, excite_bias,
    project_weight, mid_gain, mid_bias, out_gain, out_bias, mid_mean, mid_var, out_mean, out_var,
):
    batch, side, _, out = images.shape
    mid = expand_weight.shape[2]
    members = lax.axis_size("row")
    row_count = float(batch * side * side * members * lax.axis_size("col"))
    spare = -mid % LANE
    widen = lambda a: jnp.pad(a, [(0, 0)] * (a.ndim - 1) + [(0, spare)])
    current = jnp.transpose(images, (1, 2, 0, 3)).reshape(side * side * batch, out)
    stats = moments_call(current, expand_weight, mid_mean, 0, members)
    expand_padded, kernel_padded = widen(expand_weight), widen(depth_kernel)
    params = jnp.stack([mid_mean, mid_var, mid_gain, mid_bias], axis=2)
    params = widen(params.reshape(LAYERS * 2 * 4, mid))
    out_params = jnp.stack([out_mean, out_var, out_gain, out_bias], axis=1).reshape(LAYERS * 4, out)
    mid_new, out_new = [], []
    for layer in range(LAYERS):
        spread, stats, first_new = depth_call(
            current, expand_padded, kernel_padded, params, exchange(stats), members, layer, side, row_count
        )
        projected, stats, second_new = lift_call(
            spread, params, squeeze_weight, squeeze_bias, excite_weight, excite_bias,
            project_weight, out_mean, exchange(stats), members, layer, row_count,
        )
        follow = (expand_weight, mid_mean) if layer + 1 < LAYERS else None
        results = output_call(current, projected, out_params, exchange(stats), members, layer, row_count, follow)
        current, third_new = results[0], results[1]
        if follow is not None:
            stats = results[2]
        mid_new.append(jnp.stack([first_new, second_new]))
        out_new.append(third_new)
    mid_new = jnp.stack(mid_new)
    out_new = jnp.stack(out_new)
    block_output = jnp.transpose(current.reshape(side, side, batch, out), (2, 0, 1, 3))
    return block_output, mid_new[:, :, 0], mid_new[:, :, 1], out_new[:, 0], out_new[:, 1]


def solution(mesh):
    split = P(("row", "col"), None, None, None)
    return jax.shard_map(
        per_device, mesh=mesh, in_specs=(split,) + (P(),) * 15, out_specs=(split, P(), P(), P(), P()), check_vma=False
    )
```

time: 300 us -> 257 us (0.86)
  local copies, waits for them, and re-layouts: 48.8 us -> 13.9 us
  other arithmetic: 29.2 us -> 5.91 us
  blocking collectives: 109 us -> 89.4 us
  Pallas kernels: 71.3 us -> 87.8 us
  waiting for transfers between devices: 19.1 us -> 32.4 us
  starting transfers between devices: 19 us -> 25.5 us
    unnamed x64 -> x40, local copies, waits for them, and re-layouts: 43.8 us -> 6.77 us
    all_to_all x3 -> x1, blocking collectives: 32.4 us -> 10.6 us  [exchange(): lax.all_to_all(copies, 'col', split_axis=0, concat_axis=0, tiled=True)]
    pallas_call x7, Pallas kernels: 71.3 us -> 87.8 us  [call(): pl.pallas_call(kernel, in_specs=[spec(n in in_vmem) for n in range(len(op...]
    all_to_all x3 -> x5, waiting for transfers between devices: 13.7 us -> 25.6 us  [exchange(): lax.all_to_all(copies, 'col', split_axis=0, concat_axis=0, tiled=True)]
    div x6 -> x0, other arithmetic: 7.72 us -> none  [coefficients(): gain_scale = gain * scale_ratio / batch_sigma]
    all_to_all x3 -> x5, starting transfers between devices: 14.4 us -> 21 us  [exchange(): lax.all_to_all(copies, 'col', split_axis=0, concat_axis=0, tiled=True)]
    add x6 -> x0, other arithmetic: 6.18 us -> none  [coefficients(): new_var = run_var + MOMENTUM * (batch_var - run_var)]
    reduce_sum x6, other arithmetic: 4.21 us -> 0.37 us  [exchange(): total = jnp.sum(sums, axis=0)]
  transfers between devices with their start and end apart: 4 -> 6, of which waited for: 4 -> 6; matrix products, arithmetic and copies ran while one was open for 4% -> 4% of each run, Pallas kernels for 0% -> 0%
where the time goes in v4:
time: 257 us; the launch traced here: 256 us
  blocking collectives  89.4 us (35%)
  Pallas kernels  87.8 us (34%)
  waiting for transfers between devices  32.4 us (13%)
  starting transfers between devices  25.5 us (10%)
  local copies, waits for them, and re-layouts  13.9 us (5%)
  other arithmetic  5.91 us (2%)
    pallas_call x7, Pallas kernels, call(): pl.pallas_call(kernel, in_specs=[spec(n in in_vmem) for n in range(len(op...  87.8 us
    all_to_all x5, blocking collectives, exchange(): sums = lax.all_to_all(stats, 'row', split_axis=0, concat_axis=0, tiled=True)  78.9 us
    all_to_all x5, waiting for transfers between devices, exchange(): lax.all_to_all(copies, 'col', split_axis=0, concat_axis=0, tiled=True)  25.6 us
    all_to_all x5, starting transfers between devices, exchange(): lax.all_to_all(copies, 'col', split_axis=0, concat_axis=0, tiled=True)  21 us
    all_to_all x1, blocking collectives, exchange(): lax.all_to_all(copies, 'col', split_axis=0, concat_axis=0, tiled=True)  10.6 us
    unnamed x40, local copies, waits for them, and re-layouts  6.77 us
    all_to_all x1, waiting for transfers between devices, exchange(): sums = lax.all_to_all(stats, 'row', split_axis=0, concat_axis=0, tiled=True)  6.73 us
  transfers between devices with their start and end apart: 6, of which 6 were waited for; matrix products, arithmetic and copies ran while one was open for 4% of the time, Pallas kernels for 0%

profile of v4, /device:TPU:1, one launch (start us, length us, event | category | flops | bytes accessed | tf_op | source)
XLA Modules:
  0.0 255.8 jit_solution(6133497934575155116)
XLA Ops:
  0.7 7.8 %expand_moments.1 = f32[16,2,1632]{2,1,0:T(2,128)} custom-call(bf16[2304,272]{1,0:T(8,128)(2,1)} %bitcast.32, bf16[2,272,1632]{2,1,0:T(8,128)(2,1)} %rest_0_.1, f32[2,2,1632]{2,1,0:T(2,128)} %rest_1_.1), custom_call_target="tpu_custom_call" | custom-call | tf_op jit(solution)/shard_map/expand_moments/pallas_call | solution.py:70
  8.5 20.7 %all_to_all.60 = f32[16,2,1632]{2,1,0:T(2,128)S(1)} all-to-all(f32[16,2,1632]{2,1,0:T(2,128)} %expand_moments.1), channel_id=1, replica_groups=mesh['row'=16,'col'=16] {'row'}, dimensions={0} | all-to-all | bytes 417792 | tf_op jit(solution)/shard_map/all_to_all | solution.py:447
  30.0 6.8 %all-to-all-start.1 = ((f32[16,2,1632]{2,1,0:T(2,128)}), f32[16,2,1632]{2,1,0:T(2,128)S(1)}, u32[]{:S(2)}, u32[]{:S(2)}) async-start(f32[16,2,1632]{2,1,0:T(2,128)} %broadcast_in_dim.12), calls=%async_computation.1 | async-start | bytes 425984 | tf_op jit(solution)/shard_map/all_to_all | solution.py:450
  39.8 4.6 %all-to-all-done.1 = f32[16,2,1632]{2,1,0:T(2,128)S(1)} async-done(((f32[16,2,1632]{2,1,0:T(2,128)}), f32[16,2,1632]{2,1,0:T(2,128)S(1)}, u32[]{:S(2)}, u32[]{:S(2)}) %all-to-all-start.1) | async-done | bytes 208928 | tf_op jit(solution)/shard_map/all_to_all | solution.py:450
  45.1 18.8 %depthwise.2 = (f32[13,144,16,128]{3,2,1,0:T(8,128)}, f32[16,2,1632]{2,1,0:T(2,128)}, f32[2,1632]{1,0:T(2,128)}) custom-call(bf16[2304,272]{1,0:T(8,128)(2,1)} %bitcast.33, bf16[2,272,1664]{2,1,0:T(8,128)(2,1)} %pad.12.w_hbm, f32[2,25,1664]{2,1,0:T(8,128)} %pad.13.dk_hbm, f32[16,1664]{1,0:T(8,128)} %pad.14.param_hbm, f32[2,1632]{1,0:T(2,128)} %reduce_sum.109.recv_hbm), custom_call_target="tpu_custom_call" | custom-call | tf_op jit(solution)/shard_map/depthwise/pallas_call | solution.py:70
  63.9 15.3 %all_to_all.61 = f32[16,2,1632]{2,1,0:T(2,128)S(1)} all-to-all(f32[16,2,1632]{2,1,0:T(2,128)} %get-tuple-element.23), channel_id=1, replica_groups=mesh['row'=16,'col'=16] {'row'}, dimensions={0} | all-to-all | bytes 417792 | tf_op jit(solution)/shard_map/all_to_all | solution.py:447
  80.0 3.5 %all-to-all-start.3 = ((f32[16,2,1632]{2,1,0:T(2,128)}), f32[16,2,1632]{2,1,0:T(2,128)S(1)}, u32[]{:S(2)}, u32[]{:S(2)}) async-start(f32[16,2,1632]{2,1,0:T(2,128)} %broadcast_in_dim.13), calls=%async_computation.3 | async-start | bytes 425984 | tf_op jit(solution)/shard_map/all_to_all | solution.py:450
  91.8 14.5 %lift_project.2 = (f32[3,768,272]{2,1,0:T(8,128)}, f32[16,2,272]{2,1,0:T(2,128)}, f32[2,1632]{1,0:T(2,128)}) custom-call(f32[13,144,16,128]{3,2,1,0:T(8,128)} %get-tuple-element.22.spread_hbm, f32[16,1664]{1,0:T(8,128)} %pad.14.param_hbm, f32[2,1632,68]{2,1,0:T(8,128)} %copy.43.w1_hbm, f32[2,68]{1,0:T(2,128)} %b1_hbm.3, f32[2,68,1632]{2,1,0:T(8,128)} %copy.44.w2_hbm, ...), custom_call_target="tpu_custom_call" | custom-call | tf_op jit(solution)/shard_map/lift_project/pallas_call | solution.py:70
  106.4 12.0 %all_to_all.62 = f32[16,2,272]{2,1,0:T(2,128)S(1)} all-to-all(f32[16,2,272]{2,1,0:T(2,128)} %get-tuple-element.25), channel_id=1, replica_groups=mesh['row'=16,'col'=16] {'row'}, dimensions={0} | all-to-all | bytes 69632 | tf_op jit(solution)/shard_map/all_to_all | solution.py:447
  119.0 3.6 %all-to-all-start.5 = ((f32[16,2,272]{2,1,0:T(2,128)}), f32[16,2,272]{2,1,0:T(2,128)S(1)}, u32[]{:S(2)}, u32[]{:S(2)}) async-start(f32[16,2,272]{2,1,0:T(2,128)} %broadcast_in_dim.14), calls=%async_computation.5 | async-start | bytes 98304 | tf_op jit(solution)/shard_map/all_to_all | solution.py:450
  123.4 5.6 %all-to-all-done.5 = f32[16,2,272]{2,1,0:T(2,128)S(1)} async-done(((f32[16,2,272]{2,1,0:T(2,128)}), f32[16,2,272]{2,1,0:T(2,128)S(1)}, u32[]{:S(2)}, u32[]{:S(2)}) %all-to-all-start.5) | async-done | bytes 34848 | tf_op jit(solution)/shard_map/all_to_all | solution.py:450
  129.6 9.2 %block_output.2 = (bf16[2304,272]{1,0:T(8,128)(2,1)}, f32[2,272]{1,0:T(2,128)}, f32[16,2,1632]{2,1,0:T(2,128)}) custom-call(bf16[2304,272]{1,0:T(8,128)(2,1)} %bitcast.34, f32[3,768,272]{2,1,0:T(8,128)} %get-tuple-element.24.proj_hbm, f32[8,272]{1,0:T(8,128)} %reshape.30.param_hbm, f32[2,272]{1,0:T(2,128)} %reduce_sum.113.recv_hbm, ...), custom_call_target="tpu_custom_call" | custom-call | tf_op jit(solution)/shard_map/block_output/pallas_call | solution.py:70
  138.7 15.7 %all_to_all.63 = f32[16,2,1632]{2,1,0:T(2,128)S(1)} all-to-all(f32[16,2,1632]{2,1,0:T(2,128)} %get-tuple-element.27), channel_id=1, replica_groups=mesh['row'=16,'col'=16] {'row'}, dimensions={0} | all-to-all | bytes 417792 | tf_op jit(solution)/shard_map/all_to_all | solution.py:447
  154.6 10.6 %all_to_all.64 = f32[16,2,1632]{2,1,0:T(2,128)S(1)} all-to-all(f32[16,2,1632]{2,1,0:T(2,128)S(1)} %broadcast_in_dim.15), channel_id=1, replica_groups=mesh['row'=16,'col'=16] {'col'}, dimensions={0} | all-to-all | bytes 417792 | tf_op jit(solution)/shard_map/all_to_all | solution.py:450
  165.9 18.7 %depthwise.3 = (f32[13,144,16,128]{3,2,1,0:T(8,128)}, f32[16,2,1632]{2,1,0:T(2,128)}, f32[2,1632]{1,0:T(2,128)}) custom-call(bf16[2304,272]{1,0:T(8,128)(2,1)} %get-tuple-element.26.x_hbm, bf16[2,272,1664]{2,1,0:T(8,128)(2,1)} %pad.12.w_hbm, f32[2,25,1664]{2,1,0:T(8,128)} %pad.13.dk_hbm, f32[16,1664]{1,0:T(8,128)} %pad.14.param_hbm, ...), custom_call_target="tpu_custom_call" | custom-call | tf_op jit(solution)/shard_map/depthwise/pallas_call | solution.py:70
  184.6 15.2 %all_to_all.65 = f32[16,2,1632]{2,1,0:T(2,128)S(1)} all-to-all(f32[16,2,1632]{2,1,0:T(2,128)} %get-tuple-element.29), channel_id=1, replica_groups=mesh['row'=16,'col'=16] {'row'}, dimensions={0} | all-to-all | bytes 417792 | tf_op jit(solution)/shard_map/all_to_all | solution.py:447
  200.7 3.5 %all-to-all-start.9 = ((f32[16,2,1632]{2,1,0:T(2,128)}), f32[16,2,1632]{2,1,0:T(2,128)S(1)}, u32[]{:S(2)}, u32[]{:S(2)}) async-start(f32[16,2,1632]{2,1,0:T(2,128)} %broadcast_in_dim.16), calls=%async_computation.9 | async-start | bytes 425984 | tf_op jit(solution)/shard_map/all_to_all | solution.py:450
  204.2 7.5 %all-to-all-done.9 = f32[16,2,1632]{2,1,0:T(2,128)S(1)} async-done(((f32[16,2,1632]{2,1,0:T(2,128)}), f32[16,2,1632]{2,1,0:T(2,128)S(1)}, u32[]{:S(2)}, u32[]{:S(2)}) %all-to-all-start.9) | async-done | bytes 208928 | tf_op jit(solution)/shard_map/all_to_all | solution.py:450
  212.5 14.5 %lift_project.3 = (f32[3,768,272]{2,1,0:T(8,128)}, f32[16,2,272]{2,1,0:T(2,128)}, f32[2,1632]{1,0:T(2,128)}) custom-call(f32[13,144,16,128]{3,2,1,0:T(8,128)} %get-tuple-element.28.spread_hbm, f32[16,1664]{1,0:T(8,128)} %pad.14.param_hbm, f32[2,1632,68]{2,1,0:T(8,128)} %copy.43.w1_hbm, f32[2,68]{1,0:T(2,128)} %b1_hbm.3, f32[2,68,1632]{2,1,0:T(8,128)} %copy.44.w2_hbm, ...), custom_call_target="tpu_custom_call" | custom-call | tf_op jit(solution)/shard_map/lift_project/pallas_call | solution.py:70
  226.9 4.5 %all-to-all-start.10 = ((f32[16,2,272]{2,1,0:T(2,128)}), f32[16,2,272]{2,1,0:T(2,128)S(1)}, u32[]{:S(2)}, u32[]{:S(2)}) async-start(f32[16,2,272]{2,1,0:T(2,128)} %get-tuple-element.31), calls=%async_computation.10 | async-start | bytes 98304 | tf_op jit(solution)/shard_map/all_to_all | solution.py:447
  232.2 6.7 %all-to-all-done.10 = f32[16,2,272]{2,1,0:T(2,128)S(1)} async-done(((f32[16,2,272]{2,1,0:T(2,128)}), f32[16,2,272]{2,1,0:T(2,128)S(1)}, u32[]{:S(2)}, u32[]{:S(2)}) %all-to-all-start.10) | async-done | bytes 34848 | tf_op jit(solution)/shard_map/all_to_all | solution.py:447
  239.6 3.5 %all-to-all-start.11 = ((f32[16,2,272]{2,1,0:T(2,128)}), f32[16,2,272]{2,1,0:T(2,128)S(1)}, u32[]{:S(2)}, u32[]{:S(2)}) async-start(f32[16,2,272]{2,1,0:T(2,128)} %broadcast_in_dim.17), calls=%async_computation.11 | async-start | bytes 98304 | tf_op jit(solution)/shard_map/all_to_all | solution.py:450
  243.8 5.8 %all-to-all-done.11 = f32[16,2,272]{2,1,0:T(2,128)S(1)} async-done(((f32[16,2,272]{2,1,0:T(2,128)}), f32[16,2,272]{2,1,0:T(2,128)S(1)}, u32[]{:S(2)}, u32[]{:S(2)}) %all-to-all-start.11) | async-done | bytes 34848 | tf_op jit(solution)/shard_map/all_to_all | solution.py:450
  250.2 4.2 %block_output.3 = (bf16[2304,272]{1,0:T(8,128)(2,1)}, f32[2,272]{1,0:T(2,128)}) custom-call(bf16[2304,272]{1,0:T(8,128)(2,1)} %get-tuple-element.26.x_hbm, f32[3,768,272]{2,1,0:T(8,128)} %get-tuple-element.30.proj_hbm, f32[8,272]{1,0:T(8,128)} %reshape.30.param_hbm, f32[2,272]{1,0:T(2,128)} %reduce_sum.119.recv_hbm), custom_call_target="tpu_custom_call" | custom-call | tf_op jit(solution)/shard_map/block_output/pallas_call | solution.py:70
  (72 shorter events, 21.9 us)
Async XLA Ops:
  0.6 36.1 %copy-start.5 = (f32[2,2,1632]{2,1,0:T(2,128)S(1)}, f32[2,2,1632]{2,1,0:T(2,128)}, u32[]{:S(2)}) copy-start(f32[2,2,1632]{2,1,0:T(2,128)} %rest_1_.1) | copy-start | bytes 78340
  0.6 36.1 %copy-start.7 = (f32[2,2,1632]{2,1,0:T(2,128)S(1)}, f32[2,2,1632]{2,1,0:T(2,128)}, u32[]{:S(2)}) copy-start(f32[2,2,1632]{2,1,0:T(2,128)} %param.25) | copy-start | bytes 78340
  0.7 36.1 %copy-start.8 = (f32[2,2,1632]{2,1,0:T(2,128)S(1)}, f32[2,2,1632]{2,1,0:T(2,128)}, u32[]{:S(2)}) copy-start(f32[2,2,1632]{2,1,0:T(2,128)} %param.24) | copy-start | bytes 78340
  0.7 36.1 %copy-start.9 = (f32[2,2,1632]{2,1,0:T(2,128)S(1)}, f32[2,2,1632]{2,1,0:T(2,128)}, u32[]{:S(2)}) copy-start(f32[2,2,1632]{2,1,0:T(2,128)} %param.29) | copy-start | bytes 78340
  8.5 29.1 %copy-start = (bf16[2,272,1632]{2,1,0:T(8,128)(2,1)S(1)}, bf16[2,272,1632]{2,1,0:T(8,128)(2,1)}, u32[]{:S(2)}) copy-start(bf16[2,272,1632]{2,1,0:T(8,128)(2,1)} %rest_0_.1) | copy-start | bytes 5326852
  30.0 14.4 %all-to-all-start.1 = ((f32[16,2,1632]{2,1,0:T(2,128)}), f32[16,2,1632]{2,1,0:T(2,128)S(1)}, u32[]{:S(2)}, u32[]{:S(2)}) async-start(f32[16,2,1632]{2,1,0:T(2,128)} %broadcast_in_dim.12), calls=%async_computation.1 | async-start | bytes 425984 | tf_op jit(solution)/shard_map/all_to_all | solution.py:450
  37.6 1.4 copy-start.4
  45.1 38.5 %copy-start.1 = (bf16[2,1632,272]{1,2,0:T(8,128)(2,1)S(1)}, bf16[2,1632,272]{1,2,0:T(8,128)(2,1)}, u32[]{:S(2)}) copy-start(bf16[2,1632,272]{1,2,0:T(8,128)(2,1)} %param.23) | copy-start | bytes 5326852
  80.0 11.1 %all-to-all-start.3 = ((f32[16,2,1632]{2,1,0:T(2,128)}), f32[16,2,1632]{2,1,0:T(2,128)S(1)}, u32[]{:S(2)}, u32[]{:S(2)}) async-start(f32[16,2,1632]{2,1,0:T(2,128)} %broadcast_in_dim.13), calls=%async_computation.3 | async-start | bytes 425984 | tf_op jit(solution)/shard_map/all_to_all | solution.py:450
  83.5 2.7 %copy-start.2 = (f32[2,1632,68]{1,0,2:T(2,128)S(1)}, f32[2,1632,68]{1,0,2:T(2,128)}, u32[]{:S(2)}) copy-start(f32[2,1632,68]{1,0,2:T(2,128)} %param.19) | copy-start | bytes 2663428
  86.3 1.7 copy-start.3
  91.8 30.9 %copy-start.6 = (f32[2,272]{1,0:T(2,128)S(1)}, f32[2,272]{1,0:T(2,128)}, u32[]{:S(2)}) copy-start(f32[2,272]{1,0:T(2,128)} %mean3_hbm.3) | copy-start | bytes 6532
  91.8 30.9 %copy-start.13 = (f32[2,272]{1,0:T(2,128)S(1)}, f32[2,272]{1,0:T(2,128)}, u32[]{:S(2)}) copy-start(f32[2,272]{1,0:T(2,128)} %param.27) | copy-start | bytes 6532
  91.8 30.9 %copy-start.14 = (f32[2,272]{1,0:T(2,128)S(1)}, f32[2,272]{1,0:T(2,128)}, u32[]{:S(2)}) copy-start(f32[2,272]{1,0:T(2,128)} %param.26) | copy-start | bytes 6532
  91.8 30.9 %copy-start.15 = (f32[2,272]{1,0:T(2,128)S(1)}, f32[2,272]{1,0:T(2,128)}, u32[]{:S(2)}) copy-start(f32[2,272]{1,0:T(2,128)} %param.31) | copy-start | bytes 6532
  119.0 9.9 %all-to-all-start.5 = ((f32[16,2,272]{2,1,0:T(2,128)}), f32[16,2,272]{2,1,0:T(2,128)S(1)}, u32[]{:S(2)}, u32[]{:S(2)}) async-start(f32[16,2,272]{2,1,0:T(2,128)} %broadcast_in_dim.14), calls=%async_computation.5 | async-start | bytes 98304 | tf_op jit(solution)/shard_map/all_to_all | solution.py:450
  165.9 38.3 %copy-start.10 = (f32[2,1632]{1,0:T(2,128)S(1)}, f32[2,1632]{1,0:T(2,128)}, u32[]{:S(2)}) copy-start(f32[2,1632]{1,0:T(2,128)} %get-tuple-element.33) | copy-start | bytes 39172
  165.9 38.3 %copy-start.11 = (f32[2,1632]{1,0:T(2,128)S(1)}, f32[2,1632]{1,0:T(2,128)}, u32[]{:S(2)}) copy-start(f32[2,1632]{1,0:T(2,128)} %get-tuple-element.34) | copy-start | bytes 39172
  200.7 11.1 %all-to-all-start.9 = ((f32[16,2,1632]{2,1,0:T(2,128)}), f32[16,2,1632]{2,1,0:T(2,128)S(1)}, u32[]{:S(2)}, u32[]{:S(2)}) async-start(f32[16,2,1632]{2,1,0:T(2,128)} %broadcast_in_dim.16), calls=%async_computation.9 | async-start | bytes 425984 | tf_op jit(solution)/shard_map/all_to_all | solution.py:450
  212.4 19.0 %copy-start.12 = (f32[2,1632]{1,0:T(2,128)S(1)}, f32[2,1632]{1,0:T(2,128)}, u32[]{:S(2)}) copy-start(f32[2,1632]{1,0:T(2,128)} %get-tuple-element.35) | copy-start | bytes 39172
  226.9 12.0 %all-to-all-start.10 = ((f32[16,2,272]{2,1,0:T(2,128)}), f32[16,2,272]{2,1,0:T(2,128)S(1)}, u32[]{:S(2)}, u32[]{:S(2)}) async-start(f32[16,2,272]{2,1,0:T(2,128)} %get-tuple-element.31), calls=%async_computation.10 | async-start | bytes 98304 | tf_op jit(solution)/shard_map/all_to_all | solution.py:447
  239.6 10.0 %all-to-all-start.11 = ((f32[16,2,272]{2,1,0:T(2,128)}), f32[16,2,272]{2,1,0:T(2,128)S(1)}, u32[]{:S(2)}, u32[]{:S(2)}) async-start(f32[16,2,272]{2,1,0:T(2,128)} %broadcast_in_dim.17), calls=%async_computation.11 | async-start | bytes 98304 | tf_op jit(solution)/shard_map/all_to_all | solution.py:450
  250.2 4.3 %copy-start.16 = (f32[2,272]{1,0:T(2,128)S(1)}, f32[2,272]{1,0:T(2,128)}, u32[]{:S(2)}) copy-start(f32[2,272]{1,0:T(2,128)} %get-tuple-element.37) | copy-start | bytes 6532

commit v5 on v4

--- a/solution.py
+++ b/solution.py
@@ -15,6 +15,7 @@
 LANE = 128
 WIDE = 256
 MIB = 1 << 20
+GROUP = 1
 
 
 def coefficients(received, row_count, run_mean, run_var, gain, bias):
@@ -178,19 +179,25 @@
         first = jnp.zeros((16, LANE), jnp.float32)
         second = jnp.zeros((16, LANE), jnp.float32)
         for h in range(side):
-            for w in range(side):
-                acc = None
+            for base in range(0, side, GROUP):
+                group = range(base, base + GROUP)
+                acc = {w: None for w in group}
                 for i in range(KERN):
-                    for k in range(KERN):
-                        r, p = h + i - reach, w + k - reach
-                        if 0 <= r < side and 0 <= p < side:
-                            cell = act_ref[s, r * side + p].astype(jnp.float32)
-                            term = cell * tap_ref[s, i * KERN + k].astype(jnp.float32)
-                            acc = term if acc is None else acc + term
-                spread_ref[block, h * side + w] = acc
-                centered = acc - mean
-                first = first + centered
-                second = second + centered * centered
+                    r = h + i - reach
+                    if not 0 <= r < side:
+                        continue
+                    for p in range(max(0, base - reach), min(side, base + GROUP + reach)):
+                        cell = act_ref[s, r * side + p].astype(jnp.float32)
+                        for w in group:
+                            k = p - w + reach
+                            if 0 <= k < KERN:
+                                term = cell * tap_ref[s, i * KERN + k].astype(jnp.float32)
+                                acc[w] = term if acc[w] is None else acc[w] + term
+                for w in group:
+                    spread_ref[block, h * side + w] = acc[w].astype(spread_ref.dtype)
+                    centered = acc[w] - mean
+                    first = first + centered
+                    second = second + centered * centered
         copies = stat_copies(first, second, stat_ref.shape[0])
         stat_ref[:, :, pl.ds(start, size)] = copies[:, :, :size]
         leave(block).start()
@@ -220,13 +227,13 @@
         functools.partial(depth_kernel_body, layer=layer, side=side, parts=3, row_count=row_count),
         "depthwise", (),
         [
-            (jax.ShapeDtypeStruct(field, jnp.float32), False),
+            (jax.ShapeDtypeStruct(field, jnp.bfloat16), False),
             (jax.ShapeDtypeStruct((members, 2, mid), jnp.float32), True),
             (jax.ShapeDtypeStruct((2, mid), jnp.float32), True),
         ],
         [
             pltpu.VMEM(received.shape, jnp.float32),
-            pltpu.VMEM(field, jnp.float32),
+            pltpu.VMEM(field, jnp.bfloat16),
             pltpu.VMEM(x.shape, x.dtype),
             pltpu.VMEM((out, padded), expand_padded.dtype),
             pltpu.VMEM(kernel_padded.shape[1:], jnp.float32),
@@ -244,14 +251,14 @@
 def lift_kernel(
     spread_hbm, param_hbm, w1_hbm, b1_hbm, w2_hbm, b2_hbm, wp_hbm, mean3_hbm, recv_hbm,
     proj_hbm, stat_ref, new_ref,
-    recv_ref, lift_ref, param_ref, w1_ref, b1_ref, w2_ref, b2_ref, wp_ref, mean3_ref,
+    recv_ref, spread_ref, lift_ref, param_ref, w1_ref, b1_ref, w2_ref, b2_ref, wp_ref, mean3_ref,
     coef_ref, pool_ref, gate_ref, scaled_ref, proj_ref, in_sems, sems, out_sems, *, layer, parts, row_count,
 ):
     blocks, cells = lift_ref.shape[0], lift_ref.shape[1]
     mid = w1_ref.shape[0]
 
     def enter(block):
-        return pltpu.make_async_copy(spread_hbm.at[block], lift_ref.at[block], in_sems.at[block])
+        return pltpu.make_async_copy(spread_hbm.at[block], spread_ref.at[block], in_sems.at[block])
 
     copies = start_copies([(recv_hbm, recv_ref), (param_hbm, param_ref)], sems)
     for block in range(blocks):
@@ -277,7 +284,7 @@
 
         def step(i, pooled):
             cell = pl.multiple_of(i * batch, batch)
-            lifted = half_silu(lift_ref[j, pl.ds(cell, batch)] * scale + shift)
+            lifted = half_silu(spread_ref[j, pl.ds(cell, batch)].astype(jnp.float32) * scale + shift)
             lift_ref[j, pl.ds(cell, batch)] = lifted
             return pooled + jnp.sum(lifted, axis=0)
 
@@ -343,6 +350,7 @@
         ],
         [
             pltpu.VMEM(received.shape, jnp.float32),
+            pltpu.VMEM(spread.shape, spread.dtype),
             pltpu.VMEM(spread.shape, jnp.float32),
             pltpu.VMEM(params.shape, jnp.float32),
             pltpu.VMEM(squeeze_weight.shape[1:], jnp.float32),
@@ -371,7 +379,8 @@
         w_ref, mid_mean_ref, in_sems, more_sems, out_sems = rest[10:]
         recv_ref, x_ref, proj_ref, param_ref, coef_ref = rest[5:10]
     else:
-        next_hbm, new_ref, recv_ref, x_ref, proj_ref, param_ref, coef_ref, in_sems, out_sems = rest
+        earlier_ref, next_hbm, means_ref, vars_ref, new_ref, recv_ref, x_ref, proj_ref = rest[:8]
+        param_ref, coef_ref, in_sems, out_sems = rest[8:]
     copies = start_copies([(recv_hbm, recv_ref), (param_hbm, param_ref), (x_hbm, x_ref)], in_sems)
     enter = [
         pltpu.make_async_copy(proj_hbm.at[part], proj_ref.at[part], in_sems.at[3 + part]) for part in range(parts)
@@ -405,6 +414,11 @@
 
         lax.fori_loop(0, size // 192, step, 0)
         leave[part].start()
+    if not follow:
+        means_ref[:layer] = earlier_ref[0]
+        means_ref[layer:] = new_ref[0:1]
+        vars_ref[:layer] = earlier_ref[1]
+        vars_ref[layer:] = new_ref[1:2]
     if follow:
         for copy in more:
             copy.wait()
@@ -413,13 +427,10 @@
         copy.wait()
 
 
-def output_call(x, projected, params, received, members, layer, row_count, follow=None):
+def output_call(x, projected, params, received, members, layer, row_count, follow=None, earlier=None):
     rows, out = x.shape
     parts = projected.shape[0]
-    outs = [
-        (jax.ShapeDtypeStruct((rows, out), jnp.bfloat16), False),
-        (jax.ShapeDtypeStruct((2, out), jnp.float32), True),
-    ]
+    outs = [(jax.ShapeDtypeStruct((rows, out), jnp.bfloat16), False)]
     scratch = [
         pltpu.VMEM(received.shape, jnp.float32),
         pltpu.VMEM((rows, out), jnp.bfloat16),
@@ -431,15 +442,22 @@
     operands = [x, projected, params, received]
     if follow is not None:
         mid = follow[0].shape[2]
+        outs.append((jax.ShapeDtypeStruct((2, out), jnp.float32), True))
         outs.append((jax.ShapeDtypeStruct((members, 2, mid), jnp.float32), True))
         scratch += [pltpu.VMEM((out, mid), jnp.bfloat16), pltpu.VMEM((2, mid), jnp.float32)]
         sems.insert(1, pltpu.SemaphoreType.DMA((2,)))
         operands += list(follow)
+        inside = ()
+    else:
+        outs += [(jax.ShapeDtypeStruct((LAYERS, out), jnp.float32), True)] * 2
+        scratch.insert(0, pltpu.VMEM((2, out), jnp.float32))
+        operands.append(earlier)
+        inside = (4,)
     return call(
         functools.partial(
             output_kernel, layer=layer, parts=parts, row_count=row_count, follow=follow is not None
         ),
-        "block_output", (), outs, scratch + sems, 24, *operands,
+        "block_output", inside, outs, scratch + sems, 24, *operands,
     )
 
 
@@ -475,17 +493,21 @@
             spread, params, squeeze_weight, squeeze_bias, excite_weight, excite_bias,
             project_weight, out_mean, exchange(stats), members, layer, row_count,
         )
-        follow = (expand_weight, mid_mean) if layer + 1 < LAYERS else None
-        results = output_call(current, projected, out_params, exchange(stats), members, layer, row_count, follow)
-        current, third_new = results[0], results[1]
-        if follow is not None:
-            stats = results[2]
+        received = exchange(stats)
+        if layer + 1 < LAYERS:
+            current, third_new, stats = output_call(
+                current, projected, out_params, received, members, layer, row_count, (expand_weight, mid_mean)
+            )
+            out_new.append(third_new)
+        else:
+            earlier = jnp.stack(out_new, axis=1)
+            current, out_mean_new, out_var_new = output_call(
+                current, projected, out_params, received, members, layer, row_count, None, earlier
+            )
         mid_new.append(jnp.stack([first_new, second_new]))
-        out_new.append(third_new)
     mid_new = jnp.stack(mid_new)
-    out_new = jnp.stack(out_new)
     block_output = jnp.transpose(current.reshape(side, side, batch, out), (2, 0, 1, 3))
-    return block_output, mid_new[:, :, 0], mid_new[:, :, 1], out_new[:, 0], out_new[:, 1]
+    return block_output, mid_new[:, :, 0], mid_new[:, :, 1], out_mean_new, out_var_new
 
 
 def solution(mesh):

time: 257 us -> 256 us (level)
    unnamed x40 -> x39, local copies, waits for them, and re-layouts: 6.77 us -> 6.17 us
where the time goes in v5:
time: 256 us; the launch traced here: 254 us
  blocking collectives  89.5 us (35%)
  Pallas kernels  87.6 us (34%)
  waiting for transfers between devices  31.8 us (12%)
  starting transfers between devices  25.5 us (10%)
  local copies, waits for them, and re-layouts  13.8 us (5%)
  other arithmetic  5.15 us (2%)
    pallas_call x7, Pallas kernels, call(): pl.pallas_call(kernel, in_specs=[spec(n in in_vmem) for n in range(len(op...  87.6 us
    all_to_all x5, blocking collectives, exchange(): sums = lax.all_to_all(stats, 'row', split_axis=0, concat_axis=0, tiled=True)  78.9 us
    all_to_all x5, waiting for transfers between devices, exchange(): lax.all_to_all(copies, 'col', split_axis=0, concat_axis=0, tiled=True)  25.1 us
    all_to_all x5, starting transfers between devices, exchange(): lax.all_to_all(copies, 'col', split_axis=0, concat_axis=0, tiled=True)  21 us
    all_to_all x1, blocking collectives, exchange(): lax.all_to_all(copies, 'col', split_axis=0, concat_axis=0, tiled=True)  10.6 us
    all_to_all x1, waiting for transfers between devices, exchange(): sums = lax.all_to_all(stats, 'row', split_axis=0, concat_axis=0, tiled=True)  6.73 us
    unnamed x39, local copies, waits for them, and re-layouts  6.17 us
  transfers between devices with their start and end apart: 6, of which 6 were waited for; matrix products, arithmetic and copies ran while one was open for 4% of the time, Pallas kernels for 0%

profile of v5, /device:TPU:1, one launch (start us, length us, event | category | flops | bytes accessed | tf_op | source)
XLA Modules:
  0.0 254.4 jit_solution(6079358150314104203)
XLA Ops:
  0.7 7.8 %expand_moments.1 = f32[16,2,1632]{2,1,0:T(2,128)} custom-call(bf16[2304,272]{1,0:T(8,128)(2,1)} %bitcast.26, bf16[2,272,1632]{2,1,0:T(8,128)(2,1)} %rest_0_.1, f32[2,2,1632]{2,1,0:T(2,128)} %rest_1_.1), custom_call_target="tpu_custom_call" | custom-call | tf_op jit(solution)/shard_map/expand_moments/pallas_call | solution.py:71
  8.5 20.7 %all_to_all.60 = f32[16,2,1632]{2,1,0:T(2,128)S(1)} all-to-all(f32[16,2,1632]{2,1,0:T(2,128)} %expand_moments.1), channel_id=1, replica_groups=mesh['row'=16,'col'=16] {'row'}, dimensions={0} | all-to-all | bytes 417792 | tf_op jit(solution)/shard_map/all_to_all | solution.py:465
  30.0 6.8 %all-to-all-start.1 = ((f32[16,2,1632]{2,1,0:T(2,128)}), f32[16,2,1632]{2,1,0:T(2,128)S(1)}, u32[]{:S(2)}, u32[]{:S(2)}) async-start(f32[16,2,1632]{2,1,0:T(2,128)} %broadcast_in_dim.12), calls=%async_computation.1 | async-start | bytes 425984 | tf_op jit(solution)/shard_map/all_to_all | solution.py:468
  39.8 4.6 %all-to-all-done.1 = f32[16,2,1632]{2,1,0:T(2,128)S(1)} async-done(((f32[16,2,1632]{2,1,0:T(2,128)}), f32[16,2,1632]{2,1,0:T(2,128)S(1)}, u32[]{:S(2)}, u32[]{:S(2)}) %all-to-all-start.1) | async-done | bytes 208928 | tf_op jit(solution)/shard_map/all_to_all | solution.py:468
  45.1 18.8 %depthwise.2 = (bf16[13,144,16,128]{3,2,1,0:T(8,128)(2,1)}, f32[16,2,1632]{2,1,0:T(2,128)}, f32[2,1632]{1,0:T(2,128)}) custom-call(bf16[2304,272]{1,0:T(8,128)(2,1)} %bitcast.27, bf16[2,272,1664]{2,1,0:T(8,128)(2,1)} %pad.12.w_hbm, f32[2,25,1664]{2,1,0:T(8,128)} %pad.13.dk_hbm, f32[16,1664]{1,0:T(8,128)} %pad.14.param_hbm, f32[2,1632]{1,0:T(2,128)} %reduce_sum.109.recv_hbm), custom_call_target="tpu_custom_call" | custom-call | tf_op jit(solution)/shard_map/depthwise/pallas_call | solution.py:71
  63.9 15.3 %all_to_all.61 = f32[16,2,1632]{2,1,0:T(2,128)S(1)} all-to-all(f32[16,2,1632]{2,1,0:T(2,128)} %get-tuple-element.24), channel_id=1, replica_groups=mesh['row'=16,'col'=16] {'row'}, dimensions={0} | all-to-all | bytes 417792 | tf_op jit(solution)/shard_map/all_to_all | solution.py:465
  80.0 3.5 %all-to-all-start.3 = ((f32[16,2,1632]{2,1,0:T(2,128)}), f32[16,2,1632]{2,1,0:T(2,128)S(1)}, u32[]{:S(2)}, u32[]{:S(2)}) async-start(f32[16,2,1632]{2,1,0:T(2,128)} %broadcast_in_dim.13), calls=%async_computation.3 | async-start | bytes 425984 | tf_op jit(solution)/shard_map/all_to_all | solution.py:468
  91.8 14.1 %lift_project.2 = (f32[3,768,272]{2,1,0:T(8,128)}, f32[16,2,272]{2,1,0:T(2,128)}, f32[2,1632]{1,0:T(2,128)}) custom-call(bf16[13,144,16,128]{3,2,1,0:T(8,128)(2,1)} %get-tuple-element.23.spread_hbm, f32[16,1664]{1,0:T(8,128)} %pad.14.param_hbm, f32[2,1632,68]{2,1,0:T(8,128)} %copy.43.w1_hbm, f32[2,68]{1,0:T(2,128)} %b1_hbm.3, f32[2,68,1632]{2,1,0:T(8,128)} %copy.44.w2_hbm, ...), custom_call_target="tpu_custom_call" | custom-call | tf_op jit(solution)/shard_map/lift_project/pallas_call | solution.py:71
  105.9 12.0 %all_to_all.62 = f32[16,2,272]{2,1,0:T(2,128)S(1)} all-to-all(f32[16,2,272]{2,1,0:T(2,128)} %get-tuple-element.26), channel_id=1, replica_groups=mesh['row'=16,'col'=16] {'row'}, dimensions={0} | all-to-all | bytes 69632 | tf_op jit(solution)/shard_map/all_to_all | solution.py:465
  118.6 3.7 %all-to-all-start.5 = ((f32[16,2,272]{2,1,0:T(2,128)}), f32[16,2,272]{2,1,0:T(2,128)S(1)}, u32[]{:S(2)}, u32[]{:S(2)}) async-start(f32[16,2,272]{2,1,0:T(2,128)} %broadcast_in_dim.14), calls=%async_computation.5 | async-start | bytes 98304 | tf_op jit(solution)/shard_map/all_to_all | solution.py:468
  122.9 5.6 %all-to-all-done.5 = f32[16,2,272]{2,1,0:T(2,128)S(1)} async-done(((f32[16,2,272]{2,1,0:T(2,128)}), f32[16,2,272]{2,1,0:T(2,128)S(1)}, u32[]{:S(2)}, u32[]{:S(2)}) %all-to-all-start.5) | async-done | bytes 34848 | tf_op jit(solution)/shard_map/all_to_all | solution.py:468
  129.1 9.2 %block_output.2 = (bf16[2304,272]{1,0:T(8,128)(2,1)}, f32[2,272]{1,0:T(2,128)}, f32[16,2,1632]{2,1,0:T(2,128)}) custom-call(bf16[2304,272]{1,0:T(8,128)(2,1)} %bitcast.28, f32[3,768,272]{2,1,0:T(8,128)} %get-tuple-element.25.proj_hbm, f32[8,272]{1,0:T(8,128)} %reshape.30.param_hbm, f32[2,272]{1,0:T(2,128)} %reduce_sum.113.recv_hbm, ...), custom_call_target="tpu_custom_call" | custom-call | tf_op jit(solution)/shard_map/block_output/pallas_call | solution.py:71
  138.3 15.7 %all_to_all.63 = f32[16,2,1632]{2,1,0:T(2,128)S(1)} all-to-all(f32[16,2,1632]{2,1,0:T(2,128)} %get-tuple-element.28), channel_id=1, replica_groups=mesh['row'=16,'col'=16] {'row'}, dimensions={0} | all-to-all | bytes 417792 | tf_op jit(solution)/shard_map/all_to_all | solution.py:465
  154.2 10.6 %all_to_all.64 = f32[16,2,1632]{2,1,0:T(2,128)S(1)} all-to-all(f32[16,2,1632]{2,1,0:T(2,128)S(1)} %broadcast_in_dim.15), channel_id=1, replica_groups=mesh['row'=16,'col'=16] {'col'}, dimensions={0} | all-to-all | bytes 417792 | tf_op jit(solution)/shard_map/all_to_all | solution.py:468
  165.4 18.7 %depthwise.3 = (bf16[13,144,16,128]{3,2,1,0:T(8,128)(2,1)}, f32[16,2,1632]{2,1,0:T(2,128)}, f32[2,1632]{1,0:T(2,128)}) custom-call(bf16[2304,272]{1,0:T(8,128)(2,1)} %get-tuple-element.27.x_hbm, bf16[2,272,1664]{2,1,0:T(8,128)(2,1)} %pad.12.w_hbm, f32[2,25,1664]{2,1,0:T(8,128)} %pad.13.dk_hbm, f32[16,1664]{1,0:T(8,128)} %pad.14.param_hbm, ...), custom_call_target="tpu_custom_call" | custom-call | tf_op jit(solution)/shard_map/depthwise/pallas_call | solution.py:71
  184.1 15.2 %all_to_all.65 = f32[16,2,1632]{2,1,0:T(2,128)S(1)} all-to-all(f32[16,2,1632]{2,1,0:T(2,128)} %get-tuple-element.30), channel_id=1, replica_groups=mesh['row'=16,'col'=16] {'row'}, dimensions={0} | all-to-all | bytes 417792 | tf_op jit(solution)/shard_map/all_to_all | solution.py:465
  200.2 3.5 %all-to-all-start.9 = ((f32[16,2,1632]{2,1,0:T(2,128)}), f32[16,2,1632]{2,1,0:T(2,128)S(1)}, u32[]{:S(2)}, u32[]{:S(2)}) async-start(f32[16,2,1632]{2,1,0:T(2,128)} %broadcast_in_dim.16), calls=%async_computation.9 | async-start | bytes 425984 | tf_op jit(solution)/shard_map/all_to_all | solution.py:468
  204.3 7.0 %all-to-all-done.9 = f32[16,2,1632]{2,1,0:T(2,128)S(1)} async-done(((f32[16,2,1632]{2,1,0:T(2,128)}), f32[16,2,1632]{2,1,0:T(2,128)S(1)}, u32[]{:S(2)}, u32[]{:S(2)}) %all-to-all-start.9) | async-done | bytes 208928 | tf_op jit(solution)/shard_map/all_to_all | solution.py:468
  212.0 14.1 %lift_project.3 = (f32[3,768,272]{2,1,0:T(8,128)}, f32[16,2,272]{2,1,0:T(2,128)}, f32[2,1632]{1,0:T(2,128)}) custom-call(bf16[13,144,16,128]{3,2,1,0:T(8,128)(2,1)} %get-tuple-element.29.spread_hbm, f32[16,1664]{1,0:T(8,128)} %pad.14.param_hbm, f32[2,1632,68]{2,1,0:T(8,128)} %copy.43.w1_hbm, f32[2,68]{1,0:T(2,128)} %b1_hbm.3, f32[2,68,1632]{2,1,0:T(8,128)} %copy.44.w2_hbm, ...), custom_call_target="tpu_custom_call" | custom-call | tf_op jit(solution)/shard_map/lift_project/pallas_call | solution.py:71
  226.1 4.5 %all-to-all-start.10 = ((f32[16,2,272]{2,1,0:T(2,128)}), f32[16,2,272]{2,1,0:T(2,128)S(1)}, u32[]{:S(2)}, u32[]{:S(2)}) async-start(f32[16,2,272]{2,1,0:T(2,128)} %get-tuple-element.32), calls=%async_computation.10 | async-start | bytes 98304 | tf_op jit(solution)/shard_map/all_to_all | solution.py:465
  231.4 6.7 %all-to-all-done.10 = f32[16,2,272]{2,1,0:T(2,128)S(1)} async-done(((f32[16,2,272]{2,1,0:T(2,128)}), f32[16,2,272]{2,1,0:T(2,128)S(1)}, u32[]{:S(2)}, u32[]{:S(2)}) %all-to-all-start.10) | async-done | bytes 34848 | tf_op jit(solution)/shard_map/all_to_all | solution.py:465
  238.8 3.5 %all-to-all-start.11 = ((f32[16,2,272]{2,1,0:T(2,128)}), f32[16,2,272]{2,1,0:T(2,128)S(1)}, u32[]{:S(2)}, u32[]{:S(2)}) async-start(f32[16,2,272]{2,1,0:T(2,128)} %broadcast_in_dim.17), calls=%async_computation.11 | async-start | bytes 98304 | tf_op jit(solution)/shard_map/all_to_all | solution.py:468
  242.9 5.8 %all-to-all-done.11 = f32[16,2,272]{2,1,0:T(2,128)S(1)} async-done(((f32[16,2,272]{2,1,0:T(2,128)}), f32[16,2,272]{2,1,0:T(2,128)S(1)}, u32[]{:S(2)}, u32[]{:S(2)}) %all-to-all-start.11) | async-done | bytes 34848 | tf_op jit(solution)/shard_map/all_to_all | solution.py:468
  249.3 4.9 %block_output.3 = (bf16[2304,272]{1,0:T(8,128)(2,1)}, f32[2,272]{1,0:T(2,128)}, f32[2,272]{1,0:T(2,128)}) custom-call(bf16[2304,272]{1,0:T(8,128)(2,1)} %get-tuple-element.27.x_hbm, f32[3,768,272]{2,1,0:T(8,128)} %get-tuple-element.31.proj_hbm, f32[8,272]{1,0:T(8,128)} %reshape.30.param_hbm, f32[2,272]{1,0:T(2,128)} %reduce_sum.119.recv_hbm, ...), custom_call_target="tpu_custom_call" | custom-call | tf_op jit(solution)/shard_map/block_output/pallas_call | solution.py:71
  (71 shorter events, 21.1 us)
Async XLA Ops:
  0.6 36.1 %copy-start.5 = (f32[2,2,1632]{2,1,0:T(2,128)S(1)}, f32[2,2,1632]{2,1,0:T(2,128)}, u32[]{:S(2)}) copy-start(f32[2,2,1632]{2,1,0:T(2,128)} %rest_1_.1) | copy-start | bytes 78340
  0.6 36.1 %copy-start.7 = (f32[2,2,1632]{2,1,0:T(2,128)S(1)}, f32[2,2,1632]{2,1,0:T(2,128)}, u32[]{:S(2)}) copy-start(f32[2,2,1632]{2,1,0:T(2,128)} %param.25) | copy-start | bytes 78340
  0.7 36.1 %copy-start.8 = (f32[2,2,1632]{2,1,0:T(2,128)S(1)}, f32[2,2,1632]{2,1,0:T(2,128)}, u32[]{:S(2)}) copy-start(f32[2,2,1632]{2,1,0:T(2,128)} %param.24) | copy-start | bytes 78340
  0.7 36.1 %copy-start.9 = (f32[2,2,1632]{2,1,0:T(2,128)S(1)}, f32[2,2,1632]{2,1,0:T(2,128)}, u32[]{:S(2)}) copy-start(f32[2,2,1632]{2,1,0:T(2,128)} %param.29) | copy-start | bytes 78340
  8.5 29.1 %copy-start = (bf16[2,272,1632]{2,1,0:T(8,128)(2,1)S(1)}, bf16[2,272,1632]{2,1,0:T(8,128)(2,1)}, u32[]{:S(2)}) copy-start(bf16[2,272,1632]{2,1,0:T(8,128)(2,1)} %rest_0_.1) | copy-start | bytes 5326852
  30.0 14.4 %all-to-all-start.1 = ((f32[16,2,1632]{2,1,0:T(2,128)}), f32[16,2,1632]{2,1,0:T(2,128)S(1)}, u32[]{:S(2)}, u32[]{:S(2)}) async-start(f32[16,2,1632]{2,1,0:T(2,128)} %broadcast_in_dim.12), calls=%async_computation.1 | async-start | bytes 425984 | tf_op jit(solution)/shard_map/all_to_all | solution.py:468
  37.6 1.4 copy-start.4
  45.1 38.4 %copy-start.1 = (bf16[2,1632,272]{1,2,0:T(8,128)(2,1)S(1)}, bf16[2,1632,272]{1,2,0:T(8,128)(2,1)}, u32[]{:S(2)}) copy-start(bf16[2,1632,272]{1,2,0:T(8,128)(2,1)} %param.23) | copy-start | bytes 5326852
  80.0 11.1 %all-to-all-start.3 = ((f32[16,2,1632]{2,1,0:T(2,128)}), f32[16,2,1632]{2,1,0:T(2,128)S(1)}, u32[]{:S(2)}, u32[]{:S(2)}) async-start(f32[16,2,1632]{2,1,0:T(2,128)} %broadcast_in_dim.13), calls=%async_computation.3 | async-start | bytes 425984 | tf_op jit(solution)/shard_map/all_to_all | solution.py:468
  83.5 2.7 %copy-start.2 = (f32[2,1632,68]{1,0,2:T(2,128)S(1)}, f32[2,1632,68]{1,0,2:T(2,128)}, u32[]{:S(2)}) copy-start(f32[2,1632,68]{1,0,2:T(2,128)} %param.19) | copy-start | bytes 2663428
  86.2 1.7 copy-start.3
  91.8 30.5 %copy-start.6 = (f32[2,272]{1,0:T(2,128)S(1)}, f32[2,272]{1,0:T(2,128)}, u32[]{:S(2)}) copy-start(f32[2,272]{1,0:T(2,128)} %mean3_hbm.3) | copy-start | bytes 6532
  91.8 30.5 %copy-start.13 = (f32[2,272]{1,0:T(2,128)S(1)}, f32[2,272]{1,0:T(2,128)}, u32[]{:S(2)}) copy-start(f32[2,272]{1,0:T(2,128)} %param.27) | copy-start | bytes 6532
  91.8 30.5 %copy-start.14 = (f32[2,272]{1,0:T(2,128)S(1)}, f32[2,272]{1,0:T(2,128)}, u32[]{:S(2)}) copy-start(f32[2,272]{1,0:T(2,128)} %param.26) | copy-start | bytes 6532
  91.8 30.5 %copy-start.15 = (f32[2,272]{1,0:T(2,128)S(1)}, f32[2,272]{1,0:T(2,128)}, u32[]{:S(2)}) copy-start(f32[2,272]{1,0:T(2,128)} %param.31) | copy-start | bytes 6532
  118.6 9.9 %all-to-all-start.5 = ((f32[16,2,272]{2,1,0:T(2,128)}), f32[16,2,272]{2,1,0:T(2,128)S(1)}, u32[]{:S(2)}, u32[]{:S(2)}) async-start(f32[16,2,272]{2,1,0:T(2,128)} %broadcast_in_dim.14), calls=%async_computation.5 | async-start | bytes 98304 | tf_op jit(solution)/shard_map/all_to_all | solution.py:468
  165.4 38.3 %copy-start.10 = (f32[2,1632]{1,0:T(2,128)S(1)}, f32[2,1632]{1,0:T(2,128)}, u32[]{:S(2)}) copy-start(f32[2,1632]{1,0:T(2,128)} %get-tuple-element.35) | copy-start | bytes 39172
  165.4 38.3 %copy-start.11 = (f32[2,1632]{1,0:T(2,128)S(1)}, f32[2,1632]{1,0:T(2,128)}, u32[]{:S(2)}) copy-start(f32[2,1632]{1,0:T(2,128)} %get-tuple-element.36) | copy-start | bytes 39172
  165.4 38.3 %copy-start.16 = (f32[2,272]{1,0:T(2,128)S(1)}, f32[2,272]{1,0:T(2,128)}, u32[]{:S(2)}) copy-start(f32[2,272]{1,0:T(2,128)} %get-tuple-element.33) | copy-start | bytes 6532
  200.2 11.1 %all-to-all-start.9 = ((f32[16,2,1632]{2,1,0:T(2,128)}), f32[16,2,1632]{2,1,0:T(2,128)S(1)}, u32[]{:S(2)}, u32[]{:S(2)}) async-start(f32[16,2,1632]{2,1,0:T(2,128)} %broadcast_in_dim.16), calls=%async_computation.9 | async-start | bytes 425984 | tf_op jit(solution)/shard_map/all_to_all | solution.py:468
  212.0 18.6 %copy-start.12 = (f32[2,1632]{1,0:T(2,128)S(1)}, f32[2,1632]{1,0:T(2,128)}, u32[]{:S(2)}) copy-start(f32[2,1632]{1,0:T(2,128)} %get-tuple-element.37) | copy-start | bytes 39172
  226.1 12.0 %all-to-all-start.10 = ((f32[16,2,272]{2,1,0:T(2,128)}), f32[16,2,272]{2,1,0:T(2,128)S(1)}, u32[]{:S(2)}, u32[]{:S(2)}) async-start(f32[16,2,272]{2,1,0:T(2,128)} %get-tuple-element.32), calls=%async_computation.10 | async-start | bytes 98304 | tf_op jit(solution)/shard_map/all_to_all | solution.py:465
  238.8 9.9 %all-to-all-start.11 = ((f32[16,2,272]{2,1,0:T(2,128)}), f32[16,2,272]{2,1,0:T(2,128)S(1)}, u32[]{:S(2)}, u32[]{:S(2)}) async-start(f32[16,2,272]{2,1,0:T(2,128)} %broadcast_in_dim.17), calls=%async_computation.11 | async-start | bytes 98304 | tf_op jit(solution)/shard_map/all_to_all | solution.py:468

commit v6 on v5

--- a/solution.py
+++ b/solution.py
@@ -15,7 +15,6 @@
 LANE = 128
 WIDE = 256
 MIB = 1 << 20
-GROUP = 1
 
 
 def coefficients(received, row_count, run_mean, run_var, gain, bias):
@@ -132,120 +131,94 @@
 
 
 def depth_kernel_body(
-    x_hbm, w_hbm, dk_hbm, param_hbm, recv_hbm, spread_hbm, stat_ref, new_ref,
-    recv_ref, spread_ref, x_ref, w_ref, dk_ref, param_ref, coef_ref, act_ref, tap_ref, in_sems, out_sems,
-    *, layer, side, parts, row_count,
+    x_ref, w_ref, dk_ref, recv_ref, param_ref, spread_ref, stat_ref, new_ref, act_ref, tap_ref,
+    *, layer, row_count, side, parts, tail,
 ):
-    copies = start_copies(
-        [
-            (recv_hbm, recv_ref), (param_hbm, param_ref), (x_hbm, x_ref), (w_hbm.at[layer], w_ref),
-            (dk_hbm.at[layer], dk_ref),
-        ],
-        in_sems,
-    )
-    for copy in copies[:2]:
-        copy.wait()
-    settle(recv_ref, param_ref, (2 * layer, 0.5), coef_ref, new_ref, row_count)
-    for copy in copies[2:]:
-        copy.wait()
+    j = pl.program_id(0)
     rows = x_ref.shape[0]
-    mid = stat_ref.shape[2]
-    blocks = spread_ref.shape[0]
     reach = KERN // 2
+    mean, var, gain, bias = [param_ref[8 * layer + n : 8 * layer + n + 1, :] for n in range(4)]
+    scale, shift, new_mean, new_var = coefficients(recv_ref[...], row_count, mean, var, gain, bias)
+    new_ref[...] = jnp.concatenate([new_mean, new_var], axis=0)
+    scale = 0.5 * scale
+    shift = 0.5 * shift
     chunk = rows // parts
     cells = chunk // 16
-
-    def leave(block):
-        return pltpu.make_async_copy(spread_ref.at[block], spread_hbm.at[block], out_sems.at[block])
-
-    def activate(start, width):
-        here = pl.ds(start, width)
-        scale = coef_ref[0:1, here]
-        shift = coef_ref[1:2, here]
-        for part in range(parts):
-            values = jnp.dot(
-                x_ref[part * chunk : (part + 1) * chunk, :], w_ref[:, here],
-                preferred_element_type=jnp.float32,
-            )
-            active = half_silu(values * scale + shift).astype(jnp.bfloat16).reshape(cells, 16, width)
-            for s in range(width // LANE):
-                act_ref[s, part * cells : (part + 1) * cells] = active[:, :, s * LANE : (s + 1) * LANE]
-
-    def spread_block(s, block, start, size):
-        here = pl.ds(start, LANE)
+    for part in range(parts):
+        values = jnp.dot(
+            x_ref[part * chunk : (part + 1) * chunk, :], w_ref[0], preferred_element_type=jnp.float32
+        )
+        active = half_silu(values * scale + shift).astype(jnp.bfloat16).reshape(cells, 16, WIDE)
+        for s in range(2):
+            act_ref[s, part * cells : (part + 1) * cells] = active[:, :, s * LANE : (s + 1) * LANE]
+
+    def lanes(s):
+        here = slice(s * LANE, (s + 1) * LANE)
         mean = param_ref[8 * layer + 4 : 8 * layer + 5, here]
         for t in range(KERN * KERN):
-            tap_ref[s, t] = jnp.broadcast_to(dk_ref[t : t + 1, here], (16, LANE)).astype(jnp.bfloat16)
+            tap_ref[s, t] = jnp.broadcast_to(dk_ref[0, t : t + 1, here], (16, LANE)).astype(jnp.bfloat16)
         first = jnp.zeros((16, LANE), jnp.float32)
         second = jnp.zeros((16, LANE), jnp.float32)
         for h in range(side):
-            for base in range(0, side, GROUP):
-                group = range(base, base + GROUP)
-                acc = {w: None for w in group}
+            for w in range(side):
+                acc = None
                 for i in range(KERN):
-                    r = h + i - reach
-                    if not 0 <= r < side:
-                        continue
-                    for p in range(max(0, base - reach), min(side, base + GROUP + reach)):
-                        cell = act_ref[s, r * side + p].astype(jnp.float32)
-                        for w in group:
-                            k = p - w + reach
-                            if 0 <= k < KERN:
-                                term = cell * tap_ref[s, i * KERN + k].astype(jnp.float32)
-                                acc[w] = term if acc[w] is None else acc[w] + term
-                for w in group:
-                    spread_ref[block, h * side + w] = acc[w].astype(spread_ref.dtype)
-                    centered = acc[w] - mean
-                    first = first + centered
-                    second = second + centered * centered
-        copies = stat_copies(first, second, stat_ref.shape[0])
-        stat_ref[:, :, pl.ds(start, size)] = copies[:, :, :size]
-        leave(block).start()
-
-    def step(j, carry):
-        start = pl.multiple_of(j * WIDE, WIDE)
-        activate(start, WIDE)
-        spread_block(0, 2 * j, start, LANE)
-        spread_block(1, 2 * j + 1, pl.multiple_of(start + LANE, LANE), LANE)
-        return carry
-
-    lax.fori_loop(0, blocks // 2, step, 0)
-    if blocks % 2:
-        start = (blocks - 1) * LANE
-        activate(start, LANE)
-        spread_block(0, blocks - 1, start, mid - start)
-    for block in range(blocks):
-        leave(block).wait()
-
-
-def depth_call(x, expand_padded, kernel_padded, params, received, members, layer, side, row_count):
-    _, out, padded = expand_padded.shape
-    mid = received.shape[1]
-    blocks = padded // LANE
-    field = (blocks, side * side, 16, LANE)
-    return call(
-        functools.partial(depth_kernel_body, layer=layer, side=side, parts=3, row_count=row_count),
-        "depthwise", (),
-        [
-            (jax.ShapeDtypeStruct(field, jnp.bfloat16), False),
-            (jax.ShapeDtypeStruct((members, 2, mid), jnp.float32), True),
-            (jax.ShapeDtypeStruct((2, mid), jnp.float32), True),
-        ],
-        [
-            pltpu.VMEM(received.shape, jnp.float32),
-            pltpu.VMEM(field, jnp.bfloat16),
-            pltpu.VMEM(x.shape, x.dtype),
-            pltpu.VMEM((out, padded), expand_padded.dtype),
-            pltpu.VMEM(kernel_padded.shape[1:], jnp.float32),
-            pltpu.VMEM(params.shape, jnp.float32),
-            pltpu.VMEM((2, padded), jnp.float32),
-            pltpu.VMEM((2,) + field[1:], jnp.bfloat16),
+                    for k in range(KERN):
+                        r, p = h + i - reach, w + k - reach
+                        if 0 <= r < side and 0 <= p < side:
+                            cell = act_ref[s, r * side + p].astype(jnp.float32)
+                            term = cell * tap_ref[s, i * KERN + k].astype(jnp.float32)
+                            acc = term if acc is None else acc + term
+                spread_ref[s, h * side + w] = acc.astype(spread_ref.dtype)
+                centered = acc - mean
+                first = first + centered
+                second = second + centered * centered
+        pair = jnp.concatenate(
+            [jnp.sum(first, axis=0, keepdims=True), jnp.sum(second, axis=0, keepdims=True)], axis=0
+        )
+        stat_ref[:, :, here] = jnp.broadcast_to(pair[None], (stat_ref.shape[0],) + pair.shape)
+
+    lanes(0)
+    if tail > LANE:
+        lanes(1)
+    else:
+        pl.when(j < pl.num_programs(0) - 1)(lambda: lanes(1))
+
+
+def depth_call(x, expand_weight, depth_kernel, params, received, members, layer, side, row_count):
+    rows, out = x.shape
+    mid = expand_weight.shape[2]
+    cells = side * side
+    steps = pl.cdiv(mid, WIDE)
+    return pl.pallas_call(
+        functools.partial(
+            depth_kernel_body, layer=layer, row_count=row_count, side=side, parts=3, tail=mid - (steps - 1) * WIDE
+        ),
+        grid=(steps,),
+        in_specs=[
+            pl.BlockSpec((rows, out), lambda j: (0, 0)),
+            pl.BlockSpec((1, out, WIDE), lambda j: (layer, 0, j)),
+            pl.BlockSpec((1, KERN * KERN, WIDE), lambda j: (layer, 0, j)),
+            pl.BlockSpec((2, WIDE), lambda j: (0, j)),
+            pl.BlockSpec((params.shape[0], WIDE), lambda j: (0, j)),
+        ],
+        out_specs=[
+            pl.BlockSpec((2, cells, 16, LANE), lambda j: (j, 0, 0, 0)),
+            pl.BlockSpec((members, 2, WIDE), lambda j: (0, 0, j)),
+            pl.BlockSpec((2, WIDE), lambda j: (0, j)),
+        ],
+        out_shape=[
+            jax.ShapeDtypeStruct((pl.cdiv(mid, LANE), cells, 16, LANE), jnp.bfloat16),
+            jax.ShapeDtypeStruct((members, 2, mid), jnp.float32),
+            jax.ShapeDtypeStruct((2, mid), jnp.float32),
+        ],
+        scratch_shapes=[
+            pltpu.VMEM((2, cells, 16, LANE), jnp.bfloat16),
             pltpu.VMEM((2, KERN * KERN, 16, LANE), jnp.bfloat16),
-            pltpu.SemaphoreType.DMA((5,)),
-            pltpu.SemaphoreType.DMA((blocks,)),
-        ],
-        32, x, expand_padded, kernel_padded, params, received,
-    )
+        ],
+        compiler_params=pltpu.CompilerParams(vmem_limit_bytes=62 * MIB),
+        name="depthwise",
+    )(x, expand_weight, depth_kernel, received, params)
 
 
 def lift_kernel(
@@ -480,14 +453,13 @@
     widen = lambda a: jnp.pad(a, [(0, 0)] * (a.ndim - 1) + [(0, spare)])
     current = jnp.transpose(images, (1, 2, 0, 3)).reshape(side * side * batch, out)
     stats = moments_call(current, expand_weight, mid_mean, 0, members)
-    expand_padded, kernel_padded = widen(expand_weight), widen(depth_kernel)
     params = jnp.stack([mid_mean, mid_var, mid_gain, mid_bias], axis=2)
     params = widen(params.reshape(LAYERS * 2 * 4, mid))
     out_params = jnp.stack([out_mean, out_var, out_gain, out_bias], axis=1).reshape(LAYERS * 4, out)
     mid_new, out_new = [], []
     for layer in range(LAYERS):
         spread, stats, first_new = depth_call(
-            current, expand_padded, kernel_padded, params, exchange(stats), members, layer, side, row_count
+            current, expand_weight, depth_kernel, params, exchange(stats), members, layer, side, row_count
         )
         projected, stats, second_new = lift_call(
             spread, params, squeeze_weight, squeeze_bias, excite_weight, excite_bias,

time: 256 us -> 253 us (0.988)
  Pallas kernels: 87.6 us -> 84.3 us
    pallas_call x7 -> x5, Pallas kernels: 87.6 us -> 50.1 us  [call(): pl.pallas_call(kernel, in_specs=[spec(n in in_vmem) for n in range(len(op...]
    pallas_call x0 -> x2, Pallas kernels: none -> 34.2 us  [depth_call(): pl.pallas_call(functools.partial(depth_kernel_body, layer=layer, row_coun...]
    unnamed x39 -> x35, local copies, waits for them, and re-layouts: 6.17 us -> 7.79 us
where the time goes in v6:
time: 253 us; the launch traced here: 252 us
  blocking collectives  89.4 us (35%)
  Pallas kernels  84.3 us (33%)
  waiting for transfers between devices  32.6 us (13%)
  starting transfers between devices  26 us (10%)
  local copies, waits for them, and re-layouts  13.2 us (5%)
  other arithmetic  5.16 us (2%)
    all_to_all x5, blocking collectives, exchange(): sums = lax.all_to_all(stats, 'row', split_axis=0, concat_axis=0, tiled=True)  78.8 us
    pallas_call x5, Pallas kernels, call(): pl.pallas_call(kernel, in_specs=[spec(n in in_vmem) for n in range(len(op...  50.1 us
    pallas_call x2, Pallas kernels, depth_call(): pl.pallas_call(functools.partial(depth_kernel_body, layer=layer, row_coun...  34.2 us
    all_to_all x5, waiting for transfers between devices, exchange(): lax.all_to_all(copies, 'col', split_axis=0, concat_axis=0, tiled=True)  25.9 us
    all_to_all x5, starting transfers between devices, exchange(): lax.all_to_all(copies, 'col', split_axis=0, concat_axis=0, tiled=True)  21.5 us
    all_to_all x1, blocking collectives, exchange(): lax.all_to_all(copies, 'col', split_axis=0, concat_axis=0, tiled=True)  10.6 us
    unnamed x35, local copies, waits for them, and re-layouts  7.79 us
    all_to_all x1, waiting for transfers between devices, exchange(): sums = lax.all_to_all(stats, 'row', split_axis=0, concat_axis=0, tiled=True)  6.73 us
  transfers between devices with their start and end apart: 6, of which 6 were waited for; matrix products, arithmetic and copies ran while one was open for 4% of the time, Pallas kernels for 0%

profile of v6, /device:TPU:1, one launch (start us, length us, event | category | flops | bytes accessed | tf_op | source)
XLA Modules:
  0.0 251.8 jit_solution(15864073393891609213)
XLA Ops:
  0.7 7.8 %expand_moments.1 = f32[16,2,1632]{2,1,0:T(2,128)} custom-call(bf16[2304,272]{1,0:T(8,128)(2,1)} %bitcast.26, bf16[2,272,1632]{2,1,0:T(8,128)(2,1)} %w_ref.3, f32[2,2,1632]{2,1,0:T(2,128)} %rest_1_.1), custom_call_target="tpu_custom_call" | custom-call | tf_op jit(solution)/shard_map/expand_moments/pallas_call | solution.py:70
  8.5 20.7 %all_to_all.60 = f32[16,2,1632]{2,1,0:T(2,128)S(1)} all-to-all(f32[16,2,1632]{2,1,0:T(2,128)} %expand_moments.1), channel_id=1, replica_groups=mesh['row'=16,'col'=16] {'row'}, dimensions={0} | all-to-all | bytes 417792 | tf_op jit(solution)/shard_map/all_to_all | solution.py:438
  30.0 6.8 %all-to-all-start.1 = ((f32[16,2,1632]{2,1,0:T(2,128)}), f32[16,2,1632]{2,1,0:T(2,128)S(1)}, u32[]{:S(2)}, u32[]{:S(2)}) async-start(f32[16,2,1632]{2,1,0:T(2,128)} %broadcast_in_dim.12), calls=%async_computation.1 | async-start | bytes 425984 | tf_op jit(solution)/shard_map/all_to_all | solution.py:441
  38.4 6.0 %all-to-all-done.1 = f32[16,2,1632]{2,1,0:T(2,128)S(1)} async-done(((f32[16,2,1632]{2,1,0:T(2,128)}), f32[16,2,1632]{2,1,0:T(2,128)S(1)}, u32[]{:S(2)}, u32[]{:S(2)}) %all-to-all-start.1) | async-done | bytes 208928 | tf_op jit(solution)/shard_map/all_to_all | solution.py:441
  45.1 17.1 %depthwise.2 = (bf16[13,144,16,128]{3,2,1,0:T(8,128)(2,1)}, f32[16,2,1632]{2,1,0:T(2,128)}, f32[2,1632]{1,0:T(2,128)}) custom-call(bf16[2304,272]{1,0:T(8,128)(2,1)} %bitcast.27, bf16[2,272,1632]{2,1,0:T(8,128)(2,1)} %w_ref.3, f32[2,25,1632]{2,1,0:T(8,128)} %copy.43.dk_ref, f32[2,1632]{1,0:T(2,128)} %reduce_sum.109.recv_ref, f32[16,1664]{1,0:T(8,128)} %pad.4.param_ref.param_hbm), custom_call_target="tpu_custom_call" | custom-call | tf_op jit(solution)/shard_map/depthwise/pallas_call | solution.py:193
  62.2 15.3 %all_to_all.61 = f32[16,2,1632]{2,1,0:T(2,128)S(1)} all-to-all(f32[16,2,1632]{2,1,0:T(2,128)} %get-tuple-element.24), channel_id=1, replica_groups=mesh['row'=16,'col'=16] {'row'}, dimensions={0} | all-to-all | bytes 417792 | tf_op jit(solution)/shard_map/all_to_all | solution.py:438
  78.3 3.5 %all-to-all-start.3 = ((f32[16,2,1632]{2,1,0:T(2,128)}), f32[16,2,1632]{2,1,0:T(2,128)S(1)}, u32[]{:S(2)}, u32[]{:S(2)}) async-start(f32[16,2,1632]{2,1,0:T(2,128)} %broadcast_in_dim.13), calls=%async_computation.3 | async-start | bytes 425984 | tf_op jit(solution)/shard_map/all_to_all | solution.py:441
  90.1 14.2 %lift_project.2 = (f32[3,768,272]{2,1,0:T(8,128)}, f32[16,2,272]{2,1,0:T(2,128)}, f32[2,1632]{1,0:T(2,128)}) custom-call(bf16[13,144,16,128]{3,2,1,0:T(8,128)(2,1)} %get-tuple-element.23.spread_hbm, f32[16,1664]{1,0:T(8,128)} %pad.4.param_ref.param_hbm, f32[2,1632,68]{2,1,0:T(8,128)} %copy.45.w1_hbm, f32[2,68]{1,0:T(2,128)} %b1_hbm.3, ...), custom_call_target="tpu_custom_call" | custom-call | tf_op jit(solution)/shard_map/lift_project/pallas_call | solution.py:70
  104.2 12.0 %all_to_all.62 = f32[16,2,272]{2,1,0:T(2,128)S(1)} all-to-all(f32[16,2,272]{2,1,0:T(2,128)} %get-tuple-element.26), channel_id=1, replica_groups=mesh['row'=16,'col'=16] {'row'}, dimensions={0} | all-to-all | bytes 69632 | tf_op jit(solution)/shard_map/all_to_all | solution.py:438
  116.9 4.2 %all-to-all-start.5 = ((f32[16,2,272]{2,1,0:T(2,128)}), f32[16,2,272]{2,1,0:T(2,128)S(1)}, u32[]{:S(2)}, u32[]{:S(2)}) async-start(f32[16,2,272]{2,1,0:T(2,128)} %broadcast_in_dim.14), calls=%async_computation.5 | async-start | bytes 98304 | tf_op jit(solution)/shard_map/all_to_all | solution.py:441
  121.8 5.8 %all-to-all-done.5 = f32[16,2,272]{2,1,0:T(2,128)S(1)} async-done(((f32[16,2,272]{2,1,0:T(2,128)}), f32[16,2,272]{2,1,0:T(2,128)S(1)}, u32[]{:S(2)}, u32[]{:S(2)}) %all-to-all-start.5) | async-done | bytes 34848 | tf_op jit(solution)/shard_map/all_to_all | solution.py:441
  128.2 9.2 %block_output.2 = (bf16[2304,272]{1,0:T(8,128)(2,1)}, f32[2,272]{1,0:T(2,128)}, f32[16,2,1632]{2,1,0:T(2,128)}) custom-call(bf16[2304,272]{1,0:T(8,128)(2,1)} %bitcast.28, f32[3,768,272]{2,1,0:T(8,128)} %get-tuple-element.25.proj_hbm, f32[8,272]{1,0:T(8,128)} %reshape.30.param_hbm, f32[2,272]{1,0:T(2,128)} %reduce_sum.113.recv_hbm, ...), custom_call_target="tpu_custom_call" | custom-call | tf_op jit(solution)/shard_map/block_output/pallas_call | solution.py:70
  137.4 15.7 %all_to_all.63 = f32[16,2,1632]{2,1,0:T(2,128)S(1)} all-to-all(f32[16,2,1632]{2,1,0:T(2,128)} %get-tuple-element.28), channel_id=1, replica_groups=mesh['row'=16,'col'=16] {'row'}, dimensions={0} | all-to-all | bytes 417792 | tf_op jit(solution)/shard_map/all_to_all | solution.py:438
  153.2 10.6 %all_to_all.64 = f32[16,2,1632]{2,1,0:T(2,128)S(1)} all-to-all(f32[16,2,1632]{2,1,0:T(2,128)S(1)} %broadcast_in_dim.15), channel_id=1, replica_groups=mesh['row'=16,'col'=16] {'col'}, dimensions={0} | all-to-all | bytes 417792 | tf_op jit(solution)/shard_map/all_to_all | solution.py:441
  164.5 17.1 %depthwise.3 = (bf16[13,144,16,128]{3,2,1,0:T(8,128)(2,1)}, f32[16,2,1632]{2,1,0:T(2,128)}, f32[2,1632]{1,0:T(2,128)}) custom-call(bf16[2304,272]{1,0:T(8,128)(2,1)} %get-tuple-element.27.x_ref.x_hbm, bf16[2,272,1632]{2,1,0:T(8,128)(2,1)} %w_ref.3, f32[2,25,1632]{2,1,0:T(8,128)} %copy.43.dk_ref, f32[2,1632]{1,0:T(2,128)} %reduce_sum.115.recv_ref, ...), custom_call_target="tpu_custom_call" | custom-call | tf_op jit(solution)/shard_map/depthwise/pallas_call | solution.py:193
  181.6 15.2 %all_to_all.65 = f32[16,2,1632]{2,1,0:T(2,128)S(1)} all-to-all(f32[16,2,1632]{2,1,0:T(2,128)} %get-tuple-element.30), channel_id=1, replica_groups=mesh['row'=16,'col'=16] {'row'}, dimensions={0} | all-to-all | bytes 417792 | tf_op jit(solution)/shard_map/all_to_all | solution.py:438
  197.6 3.5 %all-to-all-start.9 = ((f32[16,2,1632]{2,1,0:T(2,128)}), f32[16,2,1632]{2,1,0:T(2,128)S(1)}, u32[]{:S(2)}, u32[]{:S(2)}) async-start(f32[16,2,1632]{2,1,0:T(2,128)} %broadcast_in_dim.16), calls=%async_computation.9 | async-start | bytes 425984 | tf_op jit(solution)/shard_map/all_to_all | solution.py:441
  201.7 6.9 %all-to-all-done.9 = f32[16,2,1632]{2,1,0:T(2,128)S(1)} async-done(((f32[16,2,1632]{2,1,0:T(2,128)}), f32[16,2,1632]{2,1,0:T(2,128)S(1)}, u32[]{:S(2)}, u32[]{:S(2)}) %all-to-all-start.9) | async-done | bytes 208928 | tf_op jit(solution)/shard_map/all_to_all | solution.py:441
  209.4 14.1 %lift_project.3 = (f32[3,768,272]{2,1,0:T(8,128)}, f32[16,2,272]{2,1,0:T(2,128)}, f32[2,1632]{1,0:T(2,128)}) custom-call(bf16[13,144,16,128]{3,2,1,0:T(8,128)(2,1)} %get-tuple-element.29.spread_hbm, f32[16,1664]{1,0:T(8,128)} %pad.4.param_ref.param_hbm, f32[2,1632,68]{2,1,0:T(8,128)} %copy.45.w1_hbm, f32[2,68]{1,0:T(2,128)} %b1_hbm.3, ...), custom_call_target="tpu_custom_call" | custom-call | tf_op jit(solution)/shard_map/lift_project/pallas_call | solution.py:70
  223.5 4.5 %all-to-all-start.10 = ((f32[16,2,272]{2,1,0:T(2,128)}), f32[16,2,272]{2,1,0:T(2,128)S(1)}, u32[]{:S(2)}, u32[]{:S(2)}) async-start(f32[16,2,272]{2,1,0:T(2,128)} %get-tuple-element.32), calls=%async_computation.10 | async-start | bytes 98304 | tf_op jit(solution)/shard_map/all_to_all | solution.py:438
  228.8 6.7 %all-to-all-done.10 = f32[16,2,272]{2,1,0:T(2,128)S(1)} async-done(((f32[16,2,272]{2,1,0:T(2,128)}), f32[16,2,272]{2,1,0:T(2,128)S(1)}, u32[]{:S(2)}, u32[]{:S(2)}) %all-to-all-start.10) | async-done | bytes 34848 | tf_op jit(solution)/shard_map/all_to_all | solution.py:438
  236.2 3.5 %all-to-all-start.11 = ((f32[16,2,272]{2,1,0:T(2,128)}), f32[16,2,272]{2,1,0:T(2,128)S(1)}, u32[]{:S(2)}, u32[]{:S(2)}) async-start(f32[16,2,272]{2,1,0:T(2,128)} %broadcast_in_dim.17), calls=%async_computation.11 | async-start | bytes 98304 | tf_op jit(solution)/shard_map/all_to_all | solution.py:441
  240.3 5.8 %all-to-all-done.11 = f32[16,2,272]{2,1,0:T(2,128)S(1)} async-done(((f32[16,2,272]{2,1,0:T(2,128)}), f32[16,2,272]{2,1,0:T(2,128)S(1)}, u32[]{:S(2)}, u32[]{:S(2)}) %all-to-all-start.11) | async-done | bytes 34848 | tf_op jit(solution)/shard_map/all_to_all | solution.py:441
  246.7 4.9 %block_output.3 = (bf16[2304,272]{1,0:T(8,128)(2,1)}, f32[2,272]{1,0:T(2,128)}, f32[2,272]{1,0:T(2,128)}) custom-call(bf16[2304,272]{1,0:T(8,128)(2,1)} %get-tuple-element.27.x_ref.x_hbm, f32[3,768,272]{2,1,0:T(8,128)} %get-tuple-element.31.proj_hbm, f32[8,272]{1,0:T(8,128)} %reshape.30.param_hbm, f32[2,272]{1,0:T(2,128)} %reduce_sum.119.recv_hbm, ...), custom_call_target="tpu_custom_call" | custom-call | tf_op jit(solution)/shard_map/block_output/pallas_call | solution.py:70
  (65 shorter events, 19.7 us)
Async XLA Ops:
  0.6 36.1 %copy-start.3 = (f32[2,2,1632]{2,1,0:T(2,128)S(1)}, f32[2,2,1632]{2,1,0:T(2,128)}, u32[]{:S(2)}) copy-start(f32[2,2,1632]{2,1,0:T(2,128)} %rest_1_.1) | copy-start | bytes 78340
  0.6 36.1 %copy-start.5 = (f32[2,2,1632]{2,1,0:T(2,128)S(1)}, f32[2,2,1632]{2,1,0:T(2,128)}, u32[]{:S(2)}) copy-start(f32[2,2,1632]{2,1,0:T(2,128)} %param.25) | copy-start | bytes 78340
  0.7 36.1 %copy-start.6 = (f32[2,2,1632]{2,1,0:T(2,128)S(1)}, f32[2,2,1632]{2,1,0:T(2,128)}, u32[]{:S(2)}) copy-start(f32[2,2,1632]{2,1,0:T(2,128)} %param.24) | copy-start | bytes 78340
  0.7 36.1 %copy-start.7 = (f32[2,2,1632]{2,1,0:T(2,128)S(1)}, f32[2,2,1632]{2,1,0:T(2,128)}, u32[]{:S(2)}) copy-start(f32[2,2,1632]{2,1,0:T(2,128)} %param.29) | copy-start | bytes 78340
  8.5 29.1 %copy-start.2 = (f32[2,25,1632]{2,0,1:T(2,128)S(1)}, f32[2,25,1632]{2,0,1:T(2,128)}, u32[]{:S(2)}) copy-start(f32[2,25,1632]{2,0,1:T(2,128)} %param.18) | copy-start | bytes 979204
  30.0 14.4 %all-to-all-start.1 = ((f32[16,2,1632]{2,1,0:T(2,128)}), f32[16,2,1632]{2,1,0:T(2,128)S(1)}, u32[]{:S(2)}, u32[]{:S(2)}) async-start(f32[16,2,1632]{2,1,0:T(2,128)} %broadcast_in_dim.12), calls=%async_computation.1 | async-start | bytes 425984 | tf_op jit(solution)/shard_map/all_to_all | solution.py:441
  45.1 36.7 %copy-start.1 = (f32[2,68,1632]{2,0,1:T(2,128)S(1)}, f32[2,68,1632]{2,0,1:T(2,128)}, u32[]{:S(2)}) copy-start(f32[2,68,1632]{2,0,1:T(2,128)} %param.21) | copy-start | bytes 2663428
  78.3 11.1 %all-to-all-start.3 = ((f32[16,2,1632]{2,1,0:T(2,128)}), f32[16,2,1632]{2,1,0:T(2,128)S(1)}, u32[]{:S(2)}, u32[]{:S(2)}) async-start(f32[16,2,1632]{2,1,0:T(2,128)} %broadcast_in_dim.13), calls=%async_computation.3 | async-start | bytes 425984 | tf_op jit(solution)/shard_map/all_to_all | solution.py:441
  81.8 3.6 %copy-start = (bf16[2,1632,272]{1,2,0:T(8,128)(2,1)S(1)}, bf16[2,1632,272]{1,2,0:T(8,128)(2,1)}, u32[]{:S(2)}) copy-start(bf16[2,1632,272]{1,2,0:T(8,128)(2,1)} %param.23) | copy-start | bytes 5326852
  90.1 31.0 %copy-start.4 = (f32[2,272]{1,0:T(2,128)S(1)}, f32[2,272]{1,0:T(2,128)}, u32[]{:S(2)}) copy-start(f32[2,272]{1,0:T(2,128)} %mean3_hbm.3) | copy-start | bytes 6532
  90.1 31.0 %copy-start.11 = (f32[2,272]{1,0:T(2,128)S(1)}, f32[2,272]{1,0:T(2,128)}, u32[]{:S(2)}) copy-start(f32[2,272]{1,0:T(2,128)} %param.27) | copy-start | bytes 6532
  90.1 31.0 %copy-start.12 = (f32[2,272]{1,0:T(2,128)S(1)}, f32[2,272]{1,0:T(2,128)}, u32[]{:S(2)}) copy-start(f32[2,272]{1,0:T(2,128)} %param.26) | copy-start | bytes 6532
  90.1 31.0 %copy-start.13 = (f32[2,272]{1,0:T(2,128)S(1)}, f32[2,272]{1,0:T(2,128)}, u32[]{:S(2)}) copy-start(f32[2,272]{1,0:T(2,128)} %param.31) | copy-start | bytes 6532
  116.9 10.7 %all-to-all-start.5 = ((f32[16,2,272]{2,1,0:T(2,128)}), f32[16,2,272]{2,1,0:T(2,128)S(1)}, u32[]{:S(2)}, u32[]{:S(2)}) async-start(f32[16,2,272]{2,1,0:T(2,128)} %broadcast_in_dim.14), calls=%async_computation.5 | async-start | bytes 98304 | tf_op jit(solution)/shard_map/all_to_all | solution.py:441
  164.5 36.6 %copy-start.8 = (f32[2,1632]{1,0:T(2,128)S(1)}, f32[2,1632]{1,0:T(2,128)}, u32[]{:S(2)}) copy-start(f32[2,1632]{1,0:T(2,128)} %get-tuple-element.35) | copy-start | bytes 39172
  164.5 36.6 %copy-start.9 = (f32[2,1632]{1,0:T(2,128)S(1)}, f32[2,1632]{1,0:T(2,128)}, u32[]{:S(2)}) copy-start(f32[2,1632]{1,0:T(2,128)} %get-tuple-element.36) | copy-start | bytes 39172
  164.5 36.6 %copy-start.14 = (f32[2,272]{1,0:T(2,128)S(1)}, f32[2,272]{1,0:T(2,128)}, u32[]{:S(2)}) copy-start(f32[2,272]{1,0:T(2,128)} %get-tuple-element.33) | copy-start | bytes 6532
  197.6 11.1 %all-to-all-start.9 = ((f32[16,2,1632]{2,1,0:T(2,128)}), f32[16,2,1632]{2,1,0:T(2,128)S(1)}, u32[]{:S(2)}, u32[]{:S(2)}) async-start(f32[16,2,1632]{2,1,0:T(2,128)} %broadcast_in_dim.16), calls=%async_computation.9 | async-start | bytes 425984 | tf_op jit(solution)/shard_map/all_to_all | solution.py:441
  209.3 18.6 %copy-start.10 = (f32[2,1632]{1,0:T(2,128)S(1)}, f32[2,1632]{1,0:T(2,128)}, u32[]{:S(2)}) copy-start(f32[2,1632]{1,0:T(2,128)} %get-tuple-element.37) | copy-start | bytes 39172
  223.5 12.0 %all-to-all-start.10 = ((f32[16,2,272]{2,1,0:T(2,128)}), f32[16,2,272]{2,1,0:T(2,128)S(1)}, u32[]{:S(2)}, u32[]{:S(2)}) async-start(f32[16,2,272]{2,1,0:T(2,128)} %get-tuple-element.32), calls=%async_computation.10 | async-start | bytes 98304 | tf_op jit(solution)/shard_map/all_to_all | solution.py:438
  236.2 10.0 %all-to-all-start.11 = ((f32[16,2,272]{2,1,0:T(2,128)}), f32[16,2,272]{2,1,0:T(2,128)S(1)}, u32[]{:S(2)}, u32[]{:S(2)}) async-start(f32[16,2,272]{2,1,0:T(2,128)} %broadcast_in_dim.17), calls=%async_computation.11 | async-start | bytes 98304 | tf_op jit(solution)/shard_map/all_to_all | solution.py:441
